TPU v7x, 256 devices: a whole 4x4x8 slice. The times are simulated.
256 devices in a mesh: tm: 8 (over y, x_lo), space: 32 (over z, x_hi, core).
Axes of the slice: x: 4 (x_hi: 2, x_lo: 2; x = x_hi * 2 + x_lo), y: 4, z: 8, core: 2. Of those that a mesh axis runs over, the one named last changes fastest.
Arguments:
- conserved_field: float32 [16, 10, 64, 4096], P('tm', None, None, 'space'), may hold values from -6 to 6
- face_neighbours: int32 [2, 4096], P(None, 'space'), may hold values from 0 to 4095, as said below
- counterpart_group: int32 [16], P('tm'), may hold values from 0 to 31
- counterpart_shift: int32 [16], P('tm'), may hold values from 0 to 127
- volume_operator: float32 [2, 64, 64], replicated, may hold values from -0.75 to 0.75
- flux_matrix: float32 [2, 10, 10], replicated, may hold values from -2 to 2
Outputs:
- new_state: float32 [16, 10, 64, 4096], P('tm', None, None, 'space')
- last_residual: float32 [16, 10, 64, 4096], P('tm', None, None, 'space')
Inputs may be any that keep to these rules, and one draw needn't show every extreme that they name: face_neighbours[0, e] = (e - d) mod 4096 and face_neighbours[1, e] = (e + d2) mod 4096 with 1 <= d, d2 <= 4; both distances 4 occur.
All inputs are finite; a program needn't handle non-finite values.
Results may differ from a plain program's by a relative error of at most 0.0001.
Values sent between devices are 32-bit elements; how exact they have to be, the bound alone decides.
A program may use at most 64 MiB of HBM per device.

v0:
```python
import jax
import jax.numpy as jnp
from jax import lax
from jax.sharding import PartitionSpec as P

SAMPLE_COUNT = 16
REACH = 4
ITERS = 2


lift_scale = 2.0
dissipation = 1.5
angular_speed = 0.5
damping_factor = 4.0
pseudo_step = 0.2


def from_behind(shard, axis, by):
    length = lax.axis_size(axis)
    return lax.ppermute(shard, axis, [(i, (i + by) % length) for i in range(length)])


def face_traces(field):
    inst_count = field.shape[0]
    var_count = field.shape[1]
    elem_count = field.shape[-1]
    cube_view = field.reshape(inst_count, var_count, 4, 4, 4, elem_count)
    lower_face = cube_view[:, :, 0].reshape(inst_count, var_count, 16, elem_count)
    upper_face = cube_view[:, :, 3].reshape(inst_count, var_count, 16, elem_count)
    slide_face = cube_view[:, :, :, :, 3].reshape(inst_count, var_count, 16, elem_count)
    return (lower_face, upper_face, slide_face)


def momentum_turning(boundary_samples, cycle_samples):
    blade_azimuth = 2.0 * jnp.pi * cycle_samples.astype(jnp.float32) / SAMPLE_COUNT
    cosine = jnp.cos(blade_azimuth)[:, None, None]
    sine = jnp.sin(blade_azimuth)[:, None, None]
    first_comp = boundary_samples[:, 1]
    second_comp = boundary_samples[:, 2]
    turned_one = cosine * first_comp - sine * second_comp
    turned_two = sine * first_comp + cosine * second_comp
    return jnp.concatenate(
        [
            boundary_samples[:, :1],
            turned_one[:, None],
            turned_two[:, None],
            boundary_samples[:, 3:],
        ],
        axis=1,
    )


def face_term(matrix, normal_sign, outside, inside):
    jump = outside - inside
    mixed = jnp.einsum("vw,twqe->tvqe", matrix, jump, precision=lax.Precision.HIGHEST)
    return 0.5 * lift_scale * (normal_sign * mixed - dissipation * jump)


def assemble(lower_term, upper_term, slide_term):
    inst_count = lower_term.shape[0]
    var_count = lower_term.shape[1]
    elem_count = lower_term.shape[-1]
    shaped = (inst_count, var_count, 4, 4, elem_count)
    corrections = jnp.zeros((inst_count, var_count, 4, 4, 4, elem_count), lower_term.dtype)
    corrections = corrections.at[:, :, 0].add(lower_term.reshape(shaped))
    corrections = corrections.at[:, :, 3].add(upper_term.reshape(shaped))
    corrections = corrections.at[:, :, :, :, 3].add(slide_term.reshape(shaped))
    return corrections.reshape(inst_count, var_count, 64, elem_count)


def spectral_operator():
    highest = lax.Precision.HIGHEST
    fourier_wavenumbers = jnp.arange(1, SAMPLE_COUNT // 2).astype(jnp.float32)
    cycle_samples = jnp.arange(SAMPLE_COUNT).astype(jnp.float32)
    rotation_angles = (
        2.0 * jnp.pi * fourier_wavenumbers[:, None] * cycle_samples[None, :] / SAMPLE_COUNT
    )
    gains = (
        2.0
        * angular_speed
        * fourier_wavenumbers
        * jnp.exp(-damping_factor * (fourier_wavenumbers / (SAMPLE_COUNT // 2)) ** 8)
        / SAMPLE_COUNT
    )
    cosine_table = jnp.cos(rotation_angles)
    sine_table = jnp.sin(rotation_angles)
    weighted_sin = gains[:, None] * sine_table
    weighted_cos = gains[:, None] * cosine_table
    return jnp.dot(cosine_table.T, weighted_sin, precision=highest) - jnp.dot(
        sine_table.T, weighted_cos, precision=highest
    )


def volume_matrix(volume_operator, flux_matrix):
    var_count = flux_matrix.shape[1]
    node_total = volume_operator.shape[1]
    joined = flux_matrix[:, :, None, :, None] * volume_operator[:, None, :, None, :]
    return jnp.sum(joined, axis=0).reshape(var_count * node_total, var_count * node_total)


def residual_of(
    field, face_neighbours, counterpart_group, counterpart_shift, volume_operator, flux_matrix
):
    sample_position = field.shape[0]
    var_count = field.shape[1]
    node_total = field.shape[2]
    elem_local = field.shape[-1]
    highest = lax.Precision.HIGHEST
    combined = volume_matrix(volume_operator, flux_matrix)
    flat_field = field.reshape(sample_position, var_count * node_total, elem_local)
    volume = jnp.einsum("ij,tje->tie", combined, flat_field, precision=highest).reshape(field.shape)
    lower_face, upper_face, slide_face = face_traces(field)
    prev_upper = from_behind(upper_face[..., elem_local - REACH :], "space", 1)
    next_lower = from_behind(lower_face[..., :REACH], "space", -1)
    element_total = elem_local * lax.axis_size("space")
    local_index = jnp.arange(elem_local, dtype=jnp.int32)
    global_index = lax.axis_index("space") * elem_local + local_index
    back_gap = (global_index - face_neighbours[0]) % element_total
    ahead_gap = (face_neighbours[1] - global_index) % element_total
    before_joined = jnp.concatenate([prev_upper, upper_face], axis=-1)
    after_joined = jnp.concatenate([lower_face, next_lower], axis=-1)
    lower_out = jnp.zeros_like(upper_face)
    upper_out = jnp.zeros_like(lower_face)
    for distance in range(1, REACH + 1):
        lower_out = jnp.where(
            back_gap == distance,
            before_joined[..., REACH - distance : REACH - distance + elem_local],
            lower_out,
        )
        upper_out = jnp.where(
            ahead_gap == distance, after_joined[..., distance : distance + elem_local], upper_out
        )
    window_start = (
        lax.axis_index("space") * elem_local + counterpart_group * elem_local + counterpart_shift
    ) % element_total
    carried = jnp.zeros_like(slide_face)
    segment = lax.all_gather(slide_face, "space", axis=3, tiled=True)
    span_rows = segment.shape[-1]
    filler = jnp.zeros(segment.shape[:-1] + (elem_local,), segment.dtype)
    padded = jnp.concatenate([filler, segment, filler], axis=-1)
    relative = window_start % element_total
    results = []
    for sample_slot in range(sample_position):
        picked_rows = carried[sample_slot]
        for offset in (relative[sample_slot], relative[sample_slot] - element_total):
            position = local_index + offset
            inside = (position >= 0) & (position < span_rows)
            begin = jnp.clip(offset + elem_local, 0, span_rows + elem_local)
            window = lax.dynamic_slice_in_dim(padded[sample_slot], begin, elem_local, 2)
            picked_rows = jnp.where(inside, window, picked_rows)
        results.append(picked_rows)
    paired_boundary = jnp.stack(results)
    cycle_samples = lax.axis_index("tm") * sample_position + jnp.arange(
        sample_position, dtype=jnp.int32
    )
    paired_boundary = momentum_turning(paired_boundary, cycle_samples)
    corrections = assemble(
        face_term(flux_matrix[0], -1.0, lower_out, lower_face),
        face_term(flux_matrix[0], 1.0, upper_out, upper_face),
        face_term(flux_matrix[1], 1.0, paired_boundary, slide_face),
    )
    operator = spectral_operator()
    gathered = lax.all_to_all(field, "tm", split_axis=2, concat_axis=0, tiled=True)
    flat = gathered.reshape(gathered.shape[0], -1)
    back_out = jnp.dot(operator, flat, precision=highest).reshape(gathered.shape)
    cyclic_signal = lax.all_to_all(back_out, "tm", split_axis=0, concat_axis=2, tiled=True)
    return volume + corrections + cyclic_signal


def per_device(
    conserved_field,
    face_neighbours,
    counterpart_group,
    counterpart_shift,
    volume_operator,
    flux_matrix,
):
    field = conserved_field
    residual = jnp.zeros_like(field)
    for sweep_index in range(ITERS):
        residual = residual_of(
            field,
            face_neighbours,
            counterpart_group,
            counterpart_shift,
            volume_operator,
            flux_matrix,
        )
        field = field - pseudo_step * residual
    return (field, residual)


def solution(mesh):
    return jax.shard_map(
        per_device,
        mesh=mesh,
        in_specs=(P("tm", None, None, "space"), P(None, "space"), P("tm"), P("tm"), P(), P()),
        out_specs=(P("tm", None, None, "space"), P("tm", None, None, "space")),
        check_vma=False,
    )
```

profile of v0, /device:TPU:1, one launch (start us, length us, event | category | flops | bytes accessed | tf_op | source)
XLA Modules:
  0.0 269.9 jit_solution(2099093047498293443)
XLA Ops:
  11.1 3.2 %collective-permute-start.1 = (f32[2,10,16,4]{3,1,2,0:T(8,128)}, f32[2,10,16,4]{3,1,2,0:T(8,128)}, u32[]{:S(2)}, u32[]{:S(2)}) collective-permute-start(f32[2,10,16,4]{3,1,2,0:T(8,128)} %bitcast.151), channel_id=1, source_target_pairs={{0,31},{1,0},{2,1},{3,2},{4,3},{5,4},{6,5},{7,6},{8,7},{9,8},{10,9... | collective-permute-start | bytes 15368 | tf_op jit(solution)/shard_map/ppermute | solution.py:20
  15.5 2.5 copy.136
  18.0 5.1 %all-to-all-start = ((f32[2,10,64,128]{3,1,0,2:T(8,128)}), f32[2,10,64,128]{3,1,0,2:T(8,128)}, u32[]{:S(2)}, u32[]{:S(2)}) async-start(f32[2,10,64,128]{3,1,0,2:T(8,128)} %copy.136), calls=%async_computation | async-start | bytes 2097152 | tf_op jit(solution)/shard_map/all_to_all | solution.py:163
  25.6 4.5 %copy.125 = f32[10,64,10,64]{3,2,1,0:T(8,128)} copy(f32[10,64,10,64]{3,1,2,0:T(8,128)S(1)} %multiply_reduce_fusion) | data formatting | bytes 3276800 | tf_op jit(solution)/shard_map/reduce_sum | solution.py:98
  30.1 3.9 %reshape.380 = f32[640,640,1]{1,0,2:T(8,128)S(1)} reshape(f32[10,64,10,64]{3,2,1,0:T(8,128)} %copy.125) | data formatting | bytes 3276800 | tf_op jit(solution)/shard_map/reshape | solution.py:98
  37.1 2.5 fusion.113
  42.8 2.2 fusion.3
  45.2 4.8 %fusion.7 = f32[2,10,16,128]{3,1,2,0:T(8,128)S(1)} fusion(f32[2,10,16,128]{3,1,2,0:T(8,128)} %bitcast.180, f32[2,10,16,4]{3,1,2,0:T(8,128)} %collective-permute-done.1, f32[2,10,16,128]{3,1,2,0:T(8,128)} %bitcast.6, pred[128]{0:T(512)(128)(4,1)} %get-tuple-element.102, pred[128]{0:T(512)(128)(4,1)} %get-tuple-element.101, pred[128]{0:T(512)(128)(4,1)S(1)} %copy-done.28, ...), kind=kOutput, calls=%fused_computation.19 | convolution fusion | flops 5734400 | bytes 1748992 | tf_op jit(solution)/shard_map/vw,twqe->tvqe/dot_general | solution.py:55
  50.0 2.4 copy.183
  52.4 2.0 reshape.373
  57.5 5.1 %all-to-all-start.1 = ((f32[16,10,8,128]{3,2,1,0:T(8,128)}), f32[16,10,8,128]{3,2,1,0:T(8,128)}, u32[]{:S(2)}, u32[]{:S(2)}) async-start(f32[16,10,8,128]{3,2,1,0:T(8,128)} %copy.139), calls=%async_computation.1 | async-start | bytes 1310720 | tf_op jit(solution)/shard_map/all_to_all | solution.py:166
  62.9 64.3 %all-gather.3.cloned.1.call-done = f32[2,10,16,4096]{3,1,2,0:T(8,128)} async-done(((f32[2,10,16,128]{3,1,2,0:T(8,128)}), f32[2,10,16,4096]{3,1,2,0:T(8,128)}) %all-gather.3.cloned.1.call-update) | async-done | bytes 5242896 | tf_op jit(solution)/shard_map/all_gather | solution.py:137
  127.3 4.0 %pad_maximum_fusion.1 = f32[2,10,16,4352]{3,1,2,0:T(8,128)S(1)} fusion(f32[2,10,16,128]{3,1,2,0:T(8,128)S(1)} %broadcast.255, f32[2,10,16,4096]{3,1,2,0:T(8,128)} %all-gather.3.cloned.1.call-done), kind=kLoop, calls=%fused_computation.1 | loop fusion | flops 2785280 | bytes 10977280 | tf_op jit(solution)/shard_map/concatenate | solution.py:140
  131.3 2.7 fusion.109
  142.2 3.3 %convolution_bitcast_fusion = f32[2,640,128]{1,2,0:T(8,128)S(1)} fusion(f32[2,640,128]{2,1,0:T(8,128)S(1)} %bitcast.155, f32[640,640,1]{1,0,2:T(8,128)S(1)} %reshape.380), kind=kOutput, calls=%fused_computation.5 | convolution fusion | flops 1258291200 | bytes 2949120 | tf_op jit(solution)/shard_map/ij,tje->tie/dot_general | solution.py:111
  148.7 5.4 %all-to-all-start.2 = ((f32[2,10,64,128]{3,0,1,2:T(2,128)}), f32[2,10,64,128]{3,0,1,2:T(2,128)S(1)}, u32[]{:S(2)}, u32[]{:S(2)}) async-start(f32[2,10,64,128]{3,0,1,2:T(2,128)} %copy.152), calls=%async_computation.2 | async-start | bytes 1310720 | tf_op jit(solution)/shard_map/all_to_all | solution.py:163
  154.1 3.3 %fusion.1 = f32[2,10,16,128]{3,1,2,0:T(8,128)S(1)} fusion(f32[2,10,16,128]{3,1,2,0:T(8,128)} %bitcast.47, f32[2,10,16,128]{3,1,2,0:T(8,128)S(1)} %bitcast.182, f32[2,10,16,4]{3,1,2,0:T(8,128)} %collective-permute-done.2, pred[128]{0:T(512)(128)(4,1)} %copy-done.31, pred[128]{0:T(512)(128)(4,1)} %copy-done.30, pred[128]{0:T(512)(128)(4,1)} %copy-done.29, ...), kind=kOutput, calls=%fused_computation.8 | convolution fusion | flops 5775360 | bytes 1748992 | tf_op jit(solution)/shard_map/vw,twqe->tvqe/dot_general | solution.py:55
  157.6 2.1 collective-permute-done.3
  159.6 4.0 %fusion.5 = f32[2,10,16,128]{3,1,2,0:T(8,128)S(1)} fusion(f32[2,10,16,128]{3,1,2,0:T(8,128)S(1)} %bitcast.183, f32[2,10,16,4]{3,1,2,0:T(8,128)} %collective-permute-done.3, f32[2,10,16,128]{3,1,2,0:T(8,128)} %bitcast.47, pred[128]{0:T(512)(128)(4,1)} %get-tuple-element.102, pred[128]{0:T(512)(128)(4,1)} %get-tuple-element.101, ...), kind=kOutput, calls=%fused_computation.15 | convolution fusion | flops 5734400 | bytes 1748992 | tf_op jit(solution)/shard_map/vw,twqe->tvqe/dot_general | solution.py:55
  171.2 4.2 %all-to-all-start.3 = ((f32[16,10,8,128]{3,2,1,0:T(8,128)}), f32[16,10,8,128]{3,2,1,0:T(8,128)}, u32[]{:S(2)}, u32[]{:S(2)}) async-start(f32[16,10,8,128]{3,2,1,0:T(8,128)} %copy.155), calls=%async_computation.3 | async-start | bytes 1310720 | tf_op jit(solution)/shard_map/all_to_all | solution.py:166
  175.4 74.9 %all-gather.5.cloned.1.call-done = f32[2,10,16,4096]{3,1,2,0:T(8,128)} async-done(((f32[2,10,16,128]{3,1,2,0:T(8,128)}), f32[2,10,16,4096]{3,1,2,0:T(8,128)}) %all-gather.5.cloned.1.call-update) | async-done | bytes 5242896 | tf_op jit(solution)/shard_map/all_gather | solution.py:137
  250.3 3.9 %pad_maximum_fusion = f32[2,10,16,4352]{3,1,2,0:T(8,128)S(1)} fusion(f32[2,10,16,128]{3,1,2,0:T(8,128)S(1)} %copy-done.3, f32[2,10,16,4096]{3,1,2,0:T(8,128)} %all-gather.5.cloned.1.call-done), kind=kLoop, calls=%fused_computation | loop fusion | flops 2785280 | bytes 10977280 | tf_op jit(solution)/shard_map/concatenate | solution.py:140
  254.3 2.7 fusion.108
  260.5 2.5 multiply_subtract_fusion
  (139 shorter events, 35.8 us)
Async XLA Ops:
  7.2 15.9 %copy-start.26 = (s32[2]{0:T(128)S(1)}, s32[2]{0:T(128)}, u32[]{:S(2)}) copy-start(s32[2]{0:T(128)} %param.21) | copy-start | bytes 28
  7.2 15.9 %copy-start.27 = (s32[2]{0:T(128)S(1)}, s32[2]{0:T(128)}, u32[]{:S(2)}) copy-start(s32[2]{0:T(128)} %param.20) | copy-start | bytes 28
  7.2 17.8 %copy-start.10 = (f32[2,10,10]{2,0,1:T(2,128)S(1)}, f32[2,10,10]{2,0,1:T(2,128)}, u32[]{:S(2)}) copy-start(f32[2,10,10]{2,0,1:T(2,128)} %param.23) | copy-start | bytes 2404
  7.2 17.8 %copy-start.7 = (f32[2,64,64]{2,1,0:T(8,128)S(1)}, f32[2,64,64]{2,1,0:T(8,128)}, u32[]{:S(2)}) copy-start(f32[2,64,64]{2,1,0:T(8,128)} %param.22) | copy-start | bytes 98308
  7.2 120.1 %all-gather.3.cloned.1.call-start = ((), (), s32[]{:S(2)}) async-start(), calls=%async_computation.4 | async-start | bytes 8650752 | tf_op jit(solution)/shard_map/all_gather | solution.py:137
  11.1 34.1 %collective-permute-start.1 = (f32[2,10,16,4]{3,1,2,0:T(8,128)}, f32[2,10,16,4]{3,1,2,0:T(8,128)}, u32[]{:S(2)}, u32[]{:S(2)}) collective-permute-start(f32[2,10,16,4]{3,1,2,0:T(8,128)} %bitcast.151), channel_id=1, source_target_pairs={{0,31},{1,0},{2,1},{3,2},{4,3},{5,4},{6,5},{7,6},{8,7},{9,8},{10,9... | collective-permute-start | bytes 15368 | tf_op jit(solution)/shard_map/ppermute | solution.py:20
  14.3 28.4 %copy-start.6 = (f32[2,10,1,4,4,128]{5,1,4,3,0,2:T(8,128)}, f32[2,10,1,4,4,128]{5,1,4,3,0,2:T(8,128)S(1)}, u32[]{:S(2)}) copy-start(f32[2,10,1,4,4,128]{5,1,4,3,0,2:T(8,128)S(1)} %copy.161) | copy-start | bytes 491524
  14.5 28.3 %collective-permute-start = (f32[2,10,16,4]{3,1,2,0:T(8,128)S(1)}, f32[2,10,16,4]{3,1,2,0:T(8,128)S(1)}, u32[]{:S(2)}, u32[]{:S(2)}) collective-permute-start(f32[2,10,16,4]{3,1,2,0:T(8,128)S(1)} %slice.407), channel_id=1, source_target_pairs={{0,1},{1,2},{2,3},{3,4},{4,5},{5,6},{6,7},{7,8},{8,9},{9,10},{10,1... | collective-permute-start | bytes 15368 | tf_op jit(solution)/shard_map/ppermute | solution.py:20
  18.0 32.0 %all-to-all-start = ((f32[2,10,64,128]{3,1,0,2:T(8,128)}), f32[2,10,64,128]{3,1,0,2:T(8,128)}, u32[]{:S(2)}, u32[]{:S(2)}) async-start(f32[2,10,64,128]{3,1,0,2:T(8,128)} %copy.136), calls=%async_computation | async-start | bytes 2097152 | tf_op jit(solution)/shard_map/all_to_all | solution.py:163
  34.6 99.4 %copy-start.19 = (pred[128]{0:T(512)(128)(4,1)}, pred[128]{0:T(512)(128)(4,1)S(1)}, u32[]{:S(2)}) copy-start(pred[128]{0:T(512)(128)(4,1)S(1)} %get-tuple-element.110) | copy-start | bytes 388
  34.6 99.4 %copy-start.21 = (pred[128]{0:T(512)(128)(4,1)}, pred[128]{0:T(512)(128)(4,1)S(1)}, u32[]{:S(2)}) copy-start(pred[128]{0:T(512)(128)(4,1)S(1)} %get-tuple-element.111) | copy-start | bytes 388
  35.2 99.9 %copy-start.15 = (pred[128]{0:T(512)(128)(4,1)}, pred[128]{0:T(512)(128)(4,1)S(1)}, u32[]{:S(2)}) copy-start(pred[128]{0:T(512)(128)(4,1)S(1)} %get-tuple-element.108) | copy-start | bytes 388
  35.3 99.9 %copy-start.17 = (pred[128]{0:T(512)(128)(4,1)}, pred[128]{0:T(512)(128)(4,1)S(1)}, u32[]{:S(2)}) copy-start(pred[128]{0:T(512)(128)(4,1)S(1)} %get-tuple-element.109) | copy-start | bytes 388
  35.9 19.7 %copy-start.8 = (f32[16,16,1,1]{1,0,3,2:T(8,128)}, f32[16,16,1,1]{1,0,3,2:T(8,128)S(1)}, u32[]{:S(2)}) copy-start(f32[16,16,1,1]{1,0,3,2:T(8,128)S(1)} %fusion.8) | copy-start | bytes 3076
  36.5 8.5 %copy-start.25 = (pred[128]{0:T(512)(128)(4,1)}, pred[128]{0:T(512)(128)(4,1)S(1)}, u32[]{:S(2)}) copy-start(pred[128]{0:T(512)(128)(4,1)S(1)} %get-tuple-element.96) | copy-start | bytes 388
  37.0 8.1 %copy-start.24 = (pred[128]{0:T(512)(128)(4,1)S(1)}, pred[128]{0:T(512)(128)(4,1)}, u32[]{:S(2)}) copy-start(pred[128]{0:T(512)(128)(4,1)} %get-tuple-element.82) | copy-start | bytes 388
  57.5 79.8 %all-to-all-start.1 = ((f32[16,10,8,128]{3,2,1,0:T(8,128)}), f32[16,10,8,128]{3,2,1,0:T(8,128)}, u32[]{:S(2)}, u32[]{:S(2)}) async-start(f32[16,10,8,128]{3,2,1,0:T(8,128)} %copy.139), calls=%async_computation.1 | async-start | bytes 1310720 | tf_op jit(solution)/shard_map/all_to_all | solution.py:166
  62.7 187.6 %all-gather.5.cloned.1.call-start = ((), (), s32[]{:S(2)}) async-start(), calls=%async_computation.5 | async-start | bytes 8650752 | tf_op jit(solution)/shard_map/all_gather | solution.py:137
  140.9 13.2 %collective-permute-start.2 = (f32[2,10,16,4]{3,1,2,0:T(8,128)}, f32[2,10,16,4]{3,1,2,0:T(8,128)}, u32[]{:S(2)}, u32[]{:S(2)}) collective-permute-start(f32[2,10,16,4]{3,1,2,0:T(8,128)} %slice.429), channel_id=1, source_target_pairs={{0,1},{1,2},{2,3},{3,4},{4,5},{5,6},{6,7},{7,8},{8,9},{9,10},{10,1... | collective-permute-start | bytes 15368 | tf_op jit(solution)/shard_map/ppermute | solution.py:20
  148.7 10.9 %collective-permute-start.3 = (f32[2,10,16,4]{3,1,2,0:T(8,128)}, f32[2,10,16,4]{3,1,2,0:T(8,128)}, u32[]{:S(2)}, u32[]{:S(2)}) collective-permute-start(f32[2,10,16,4]{3,1,2,0:T(8,128)} %bitcast.152), channel_id=1, source_target_pairs={{0,31},{1,0},{2,1},{3,2},{4,3},{5,4},{6,5},{7,6},{8,7},{9,8},{10,9... | collective-permute-start | bytes 15368 | tf_op jit(solution)/shard_map/ppermute | solution.py:20
  148.7 16.5 %all-to-all-start.2 = ((f32[2,10,64,128]{3,0,1,2:T(2,128)}), f32[2,10,64,128]{3,0,1,2:T(2,128)S(1)}, u32[]{:S(2)}, u32[]{:S(2)}) async-start(f32[2,10,64,128]{3,0,1,2:T(2,128)} %copy.152), calls=%async_computation.2 | async-start | bytes 1310720 | tf_op jit(solution)/shard_map/all_to_all | solution.py:163
  157.4 11.9 %copy-start.9 = (f32[16,16,1,1]{1,0,3,2:T(8,128)S(1)}, f32[16,16,1,1]{1,0,3,2:T(8,128)}, u32[]{:S(2)}) copy-start(f32[16,16,1,1]{1,0,3,2:T(8,128)} %copy-done.8) | copy-start | bytes 3076
  157.6 92.7 %copy-start.3 = (f32[2,10,16,128]{3,1,2,0:T(8,128)S(1)}, f32[2,10,16,128]{3,1,2,0:T(8,128)}, u32[]{:S(2)}) copy-start(f32[2,10,16,128]{3,1,2,0:T(8,128)} %copy-done.2) | copy-start | bytes 491524
  171.2 89.3 %all-to-all-start.3 = ((f32[16,10,8,128]{3,2,1,0:T(8,128)}), f32[16,10,8,128]{3,2,1,0:T(8,128)}, u32[]{:S(2)}, u32[]{:S(2)}) async-start(f32[16,10,8,128]{3,2,1,0:T(8,128)} %copy.155), calls=%async_computation.3 | async-start | bytes 1310720 | tf_op jit(solution)/shard_map/all_to_all | solution.py:166
  (18 other events, 91.1 us)
Sparse Core Ops, SparseCore 0:
  10.6 116.6 all-gather.2
  140.1 110.1 all-gather.4
where the time goes:
time: 271 us; the launch traced here: 270 us
  waiting for transfers between devices  143 us (53%)
  local copies, waits for them, and re-layouts  40.4 us (15%)
  starting transfers between devices  25.6 us (9%)
  matrix products  23.2 us (9%)
  other arithmetic  19.2 us (7%)
  between operations  18.6 us (7%)
    all_gather x2, waiting for transfers between devices, residual_of(): segment = lax.all_gather(slide_face, 'space', axis=3, tiled=True)  139 us
    dot_general x6, matrix products, face_term(): jnp.einsum('vw,twqe->tvqe', matrix, jump, precision=lax.Precision.HIGHEST)  15.2 us
    all_to_all x2, starting transfers between devices, residual_of(): lax.all_to_all(field, 'tm', split_axis=2, concat_axis=0, tiled=True)  10.4 us
    all_to_all x2, starting transfers between devices, residual_of(): lax.all_to_all(back_out, 'tm', split_axis=0, concat_axis=2, tiled=True)  9.33 us
    unnamed x74, local copies, waits for them, and re-layouts  8.22 us
    concatenate x2, other arithmetic, residual_of(): padded = jnp.concatenate([filler, segment, filler], axis=-1)  7.94 us
    dot_general x2, matrix products, residual_of(): jnp.einsum('ij,tje->tie', combined, flat_field, precision=highest)  5.82 us
    ppermute x4, starting transfers between devices, from_behind(): lax.ppermute(shard, axis, [(i, (i + by) % length) for i in range(length)])  5.54 us
  transfers between devices with their start and end apart: 10, of which 4 were waited for; matrix products, arithmetic and copies ran while one was open for 28% of the time, Pallas kernels for 0%

commit v1 on v0

v1 whole, which is shorter than its diff:
```python
import math

import jax
import jax.numpy as jnp
from jax import lax
from jax.experimental import pallas as pl
from jax.experimental.pallas import tpu as pltpu
from jax.sharding import PartitionSpec as P

SAMPLE_COUNT = 16
REACH = 4
ITERS = 2
VARS = 10
NODES = 64
LANES = 128

lift_scale = 2.0
dissipation = 1.5
angular_speed = 0.5
damping_factor = 4.0
pseudo_step = 0.2

MESH = pl.DeviceIdType.MESH
TM = 8
SP = 32
Z = 8
Q = 4


def spectral_weights():
    half = SAMPLE_COUNT // 2
    weights = []
    for m in range(1, half):
        total = 0.0
        for k in range(1, half):
            gain = 2.0 * angular_speed * k * math.exp(-damping_factor * (k / half) ** 8) / SAMPLE_COUNT
            total += gain * math.sin(2.0 * math.pi * k * m / SAMPLE_COUNT)
        weights.append(total)
    return weights


def pick(index, values):
    out = jnp.float32(values[0])
    for k in range(1, len(values)):
        out = jnp.where(index == k, jnp.float32(values[k]), out)
    return out


def kernel(
    u_ref, fn_ref, group_ref, shift_ref, vol_ref, flux_ref,
    new_ref, res_ref,
    ub, a_hi, a_lo, gat, der, tem, ring_00, ring_01, ring_10, ring_11, cols_00, cols_01, cols_10, cols_11,
    packs, packed, side, lo_b, up_b, sl_b, in_sem, fs, fr, bs, br, zs, zr, cs, cr, ps, pr,
):
    ring = ((ring_00, ring_01), (ring_10, ring_11))
    cols = ((cols_00, cols_01), (cols_10, cols_11))
    tm = lax.axis_index("tm")
    sp = lax.axis_index("space")
    z = sp // Q
    q = sp % Q

    def space_of(zz, qq):
        return zz * Q + qq

    z_up = space_of((z + 1) % Z, q)
    z_dn = space_of((z + Z - 1) % Z, q)
    mate = space_of(z, q + 1 - 2 * (q % 2))
    cross = space_of(z, (q + 2) % Q)
    after = (sp + 1) % SP
    before = (sp + SP - 1) % SP

    load = pltpu.make_async_copy(u_ref, ub.at[0], in_sem)
    load.start()

    barrier = pltpu.get_barrier_semaphore()
    for k in range(1, TM):
        pl.semaphore_signal(barrier, inc=1, device_id={"tm": (tm + k) % TM}, device_id_type=MESH)
    for other in (z_up, z_dn, mate, cross, after, before):
        pl.semaphore_signal(barrier, inc=1, device_id={"space": other}, device_id_type=MESH)
    load.wait()
    pl.semaphore_wait(barrier, TM - 1 + 6)

    lane16 = lax.broadcasted_iota(jnp.int32, (16, LANES), 1)
    gidx = sp * LANES + lane16
    back_gap = jnp.bitwise_and(gidx - fn_ref[0:1, :], SP * LANES - 1)
    ahead_gap = jnp.bitwise_and(fn_ref[1:2, :] - gidx, SP * LANES - 1)

    weights = spectral_weights()
    cosines = [math.cos(2.0 * math.pi * k / SAMPLE_COUNT) for k in range(SAMPLE_COUNT)]
    sines = [math.sin(2.0 * math.pi * k / SAMPLE_COUNT) for k in range(SAMPLE_COUNT)]

    def rows_of(index):
        return pl.ds(pl.multiple_of(index * 8, 8), 8)

    def forward_copy(it, k):
        peer = (tm + k) % TM
        return pltpu.make_async_remote_copy(
            src_ref=ub.at[it, :, :, rows_of(peer), :], dst_ref=gat.at[it, tm],
            send_sem=fs.at[it, k], recv_sem=fr.at[it, k], device_id={"tm": peer}, device_id_type=MESH)

    def forward_arrival(it, k):
        peer = (tm + TM - k) % TM
        return pltpu.make_async_remote_copy(
            src_ref=ub.at[it, :, :, rows_of(peer), :], dst_ref=gat.at[it, peer],
            send_sem=fs.at[it, k], recv_sem=fr.at[it, k], device_id={"tm": peer}, device_id_type=MESH)

    def back_copy(it, k):
        peer = (tm + k) % TM
        return pltpu.make_async_remote_copy(
            src_ref=der.at[it, pl.ds(2 * peer, 2)], dst_ref=tem.at[it, :, :, rows_of(tm), :],
            send_sem=bs.at[it, k], recv_sem=br.at[it, k], device_id={"tm": peer}, device_id_type=MESH)

    def back_arrival(it, k):
        peer = (tm + TM - k) % TM
        return pltpu.make_async_remote_copy(
            src_ref=der.at[it, pl.ds(2 * peer, 2)], dst_ref=tem.at[it, :, :, rows_of(peer), :],
            send_sem=bs.at[it, k], recv_sem=br.at[it, k], device_id={"tm": peer}, device_id_type=MESH)

    def ring_copy(it, step, way, t):
        if way == 0:
            origin, target = (z + Z - (step - 1)) % Z, z_up
        else:
            origin, target = (z + step - 1) % Z, z_dn
        block = ring[it][t].at[origin]
        slot = ((step - 1) * 2 + way) * 2 + t
        return pltpu.make_async_remote_copy(
            src_ref=block, dst_ref=block, send_sem=zs.at[it, slot], recv_sem=zr.at[it, slot],
            device_id={"space": target}, device_id_type=MESH)

    def ring_arrival(it, step, way, t):
        if way == 0:
            origin, target = (z + Z - step) % Z, z_up
        else:
            origin, target = (z + step) % Z, z_dn
        block = ring[it][t].at[origin]
        slot = ((step - 1) * 2 + way) * 2 + t
        return pltpu.make_async_remote_copy(
            src_ref=block, dst_ref=block, send_sem=zs.at[it, slot], recv_sem=zr.at[it, slot],
            device_id={"space": target}, device_id_type=MESH)

    def column_copy(it, kind, t):
        origin, target = ((q, mate), (q, cross), ((q + 2) % Q, mate))[kind]
        block = cols[it][t].at[origin]
        slot = kind * 2 + t
        return pltpu.make_async_remote_copy(
            src_ref=block, dst_ref=block, send_sem=cs.at[it, slot], recv_sem=cr.at[it, slot],
            device_id={"space": target}, device_id_type=MESH)

    def column_arrival(it, kind, t):
        mate_q = q + 1 - 2 * (q % 2)
        origin, target = ((mate_q, mate), ((q + 2) % Q, cross), ((mate_q + 2) % Q, mate))[kind]
        block = cols[it][t].at[origin]
        slot = kind * 2 + t
        return pltpu.make_async_remote_copy(
            src_ref=block, dst_ref=block, send_sem=cs.at[it, slot], recv_sem=cr.at[it, slot],
            device_id={"space": target}, device_id_type=MESH)

    def pack_copy(it, way):
        target = (after, before)[way]
        return pltpu.make_async_remote_copy(
            src_ref=packs.at[it, way], dst_ref=packed.at[it, way], send_sem=ps.at[it, way], recv_sem=pr.at[it, way],
            device_id={"space": target}, device_id_type=MESH)

    def ring_steps(step):
        return ((0, 0), (1, 0), (0, 1), (1, 1)) if step < 4 else ((0, 0), (1, 1))

    def build_matrix():
        row = lax.broadcasted_iota(jnp.int32, (NODES, LANES), 0)
        lane = lax.broadcasted_iota(jnp.int32, (NODES, LANES), 1)
        first = lane < NODES
        on = row == jnp.bitwise_and(lane, NODES - 1)
        one, zero = jnp.float32(1.0), jnp.float32(0.0)
        lower = jnp.where(on & (row < 16), one, zero)
        upper = jnp.where(on & (row >= 48), one, zero)
        slide = jnp.where(on & (jnp.bitwise_and(row, 3) == 3), one, zero)
        scale = jnp.float32(0.5 * lift_scale)
        side[0] = vol_ref[0] + scale * (lower - upper)
        side[1] = vol_ref[1] - scale * slide
        side[2] = (scale * jnp.float32(dissipation)) * (lower + upper + slide)

        def row_block(v, carry):
            for j in range(VARS // 2):
                tile = jnp.zeros((NODES, LANES), jnp.float32)
                for d in range(2):
                    factor = jnp.where(first, flux_ref[d, v, 2 * j], flux_ref[d, v, 2 * j + 1])
                    tile = tile + factor * side[d]
                own = jnp.where(first, jnp.where(v == 2 * j, one, zero), jnp.where(v == 2 * j + 1, one, zero))
                tile = tile + own * side[2]
                high = tile.astype(jnp.bfloat16)
                where = (pl.ds(pl.multiple_of(v * NODES, NODES), NODES), pl.ds(j * LANES, LANES))
                a_hi[where] = high
                a_lo[where] = (tile - high.astype(jnp.float32)).astype(jnp.bfloat16)
            return carry

        lax.fori_loop(0, VARS, row_block, 0)

    def volume_part(it):
        u = jnp.concatenate(
            [ub[it, 0].reshape(VARS * NODES, LANES), ub[it, 1].reshape(VARS * NODES, LANES)], axis=1)
        high = u.astype(jnp.bfloat16)
        low = (u - high.astype(jnp.float32)).astype(jnp.bfloat16)
        for part in range(2):
            rows = pl.ds(part * 320, 320)
            out = jnp.dot(a_hi[rows, :], high, preferred_element_type=jnp.float32)
            out = out + jnp.dot(a_hi[rows, :], low, preferred_element_type=jnp.float32)
            out = out + jnp.dot(a_lo[rows, :], high, preferred_element_type=jnp.float32)
            for t in range(2):
                res_ref[t, pl.ds(part * 5, 5)] = out[:, t * LANES:(t + 1) * LANES].reshape(5, NODES, LANES)

    def iteration(it):
        for t in range(2):
            ring[it][t][z] = ub[it, t, :, pl.ds(3, 16, stride=4), :]
        for way, t in ring_steps(1):
            ring_copy(it, 1, way, t).start()
        for k in range(1, TM):
            forward_copy(it, k).start()
        up_pack = jnp.zeros((16, LANES), jnp.float32)
        lo_pack = jnp.zeros((16, LANES), jnp.float32)
        for i in range(2 * VARS):
            mine = (lane16 >= REACH * i) & (lane16 < REACH * (i + 1))
            u_face = ub[it, i // VARS, i % VARS, pl.ds(48, 16), :]
            l_face = ub[it, i // VARS, i % VARS, pl.ds(0, 16), :]
            up_pack = jnp.where(mine, pltpu.roll(u_face, (REACH * i + REACH) % LANES, 1), up_pack)
            lo_pack = jnp.where(mine, pltpu.roll(l_face, REACH * i, 1) if i else l_face, lo_pack)
        packs[it, 0] = up_pack
        packs[it, 1] = lo_pack
        for way in range(2):
            pack_copy(it, way).start()
        gat[it, tm] = ub[it, :, :, rows_of(tm), :]

        if it == 0:
            build_matrix()

        volume_part(it)

        for way, t in ring_steps(1):
            ring_arrival(it, 1, way, t).wait_recv()
            if (way, t) in ring_steps(2):
                ring_copy(it, 2, way, t).start()

        for way in range(2):
            pack_copy(it, way).wait_recv()
        from_before = packed[it, 0]
        from_after = packed[it, 1]
        behind = lane16 - back_gap
        ahead = lane16 + ahead_gap
        for i in range(2 * VARS):
            u_face = ub[it, i // VARS, i % VARS, pl.ds(48, 16), :]
            l_face = ub[it, i // VARS, i % VARS, pl.ds(0, 16), :]
            own = jnp.take_along_axis(u_face, jnp.bitwise_and(behind, LANES - 1), axis=1)
            far = jnp.take_along_axis(from_before, jnp.bitwise_and(behind + REACH * (i + 1), LANES - 1), axis=1)
            lo_b[i // VARS, i % VARS] = jnp.where(behind < 0, far, own)
            own = jnp.take_along_axis(l_face, jnp.bitwise_and(ahead, LANES - 1), axis=1)
            far = jnp.take_along_axis(from_after, jnp.bitwise_and(ahead + REACH * i, LANES - 1), axis=1)
            up_b[i // VARS, i % VARS] = jnp.where(ahead >= LANES, far, own)

        scale = jnp.float32(0.5 * lift_scale)
        loss = jnp.float32(0.5 * lift_scale * dissipation)

        def first_faces(v, c):
            low = -loss * lo_b[:, v]
            upp = -loss * up_b[:, v]
            for w in range(VARS):
                f = scale * flux_ref[0, v, w]
                low = low - f * lo_b[:, w]
                upp = upp + f * up_b[:, w]
            res_ref[:, v, pl.ds(0, 16), :] += low
            res_ref[:, v, pl.ds(48, 16), :] += upp
            return c

        lax.fori_loop(0, VARS, first_faces, 0)

        for way, t in ring_steps(2):
            ring_arrival(it, 2, way, t).wait_recv()
            if (way, t) in ring_steps(3):
                ring_copy(it, 3, way, t).start()

        for k in range(1, TM):
            forward_arrival(it, k).wait_recv()

        def derive(v, c):
            x = [gat[it, t // 2, t % 2, v] for t in range(SAMPLE_COUNT)]
            diff = {}
            for t in range(SAMPLE_COUNT // 2):
                for m in range(1, SAMPLE_COUNT // 2):
                    diff[t, m] = x[(t + m) % SAMPLE_COUNT] - x[(t - m) % SAMPLE_COUNT]
            for t in range(SAMPLE_COUNT // 2):
                near = jnp.float32(weights[0]) * diff[t, 1]
                opposite = jnp.float32(-weights[SAMPLE_COUNT // 2 - 2]) * diff[t, 1]
                for m in range(2, SAMPLE_COUNT // 2):
                    near = near + jnp.float32(weights[m - 1]) * diff[t, m]
                    opposite = opposite - jnp.float32(weights[SAMPLE_COUNT // 2 - m - 1]) * diff[t, m]
                der[it, t, v] = near
                der[it, t + SAMPLE_COUNT // 2, v] = opposite
            return c

        lax.fori_loop(0, VARS, derive, 0)
        for k in range(1, TM):
            back_copy(it, k).start()
        tem[it, :, :, rows_of(tm), :] = der[it, pl.ds(2 * tm, 2)]

        for way, t in ring_steps(3):
            ring_arrival(it, 3, way, t).wait_recv()
            if (way, t) in ring_steps(4):
                ring_copy(it, 4, way, t).start()
        for way, t in ring_steps(4):
            ring_arrival(it, 4, way, t).wait_recv()

        lane_b = lax.broadcasted_iota(jnp.int32, (VARS, 16, LANES), 2)
        for t in range(2):
            group, shift = group_ref[t], shift_ref[t]
            first_dst = jnp.bitwise_and(q - group, Q - 1)
            second_dst = jnp.bitwise_and(q - group - 1, Q - 1)
            first = jnp.bitwise_and(z + lax.shift_right_arithmetic(first_dst + group - q, 2), Z - 1)
            second = jnp.bitwise_and(z + lax.shift_right_arithmetic(second_dst + group + 1 - q, 2), Z - 1)
            cols[it][t][q] = jnp.where(lane_b >= shift, ring[it][t][first], ring[it][t][second])
            column_copy(it, 1, t).start()
            column_copy(it, 0, t).start()
        for t in range(2):
            column_arrival(it, 1, t).wait_recv()
            column_copy(it, 2, t).start()
        for t in range(2):
            group, shift = group_ref[t], shift_ref[t]
            column_arrival(it, 0, t).wait_recv()
            column_arrival(it, 2, t).wait_recv()
            first = cols[it][t][jnp.bitwise_and(q + group, Q - 1)]
            second = cols[it][t][jnp.bitwise_and(q + group + 1, Q - 1)]
            both = jnp.where(lane_b >= shift, first, second)
            both = pltpu.roll(both.reshape(VARS * 16, LANES), jnp.bitwise_and(LANES - shift, LANES - 1), 1)
            sl_b[t] = both.reshape(VARS, 16, LANES)
            cosine, sine = pick(2 * tm + t, cosines), pick(2 * tm + t, sines)
            one, two = sl_b[t, 1], sl_b[t, 2]
            sl_b[t, 1] = cosine * one - sine * two
            sl_b[t, 2] = sine * one + cosine * two

        for k in range(1, TM):
            back_arrival(it, k).wait_recv()

        def finish(v, c):
            for t in range(2):
                term = -loss * sl_b[t, v]
                for w in range(VARS):
                    term = term + (scale * flux_ref[1, v, w]) * sl_b[t, w]
                res_ref[t, v, pl.ds(3, 16, stride=4), :] += term
                total = res_ref[t, v] + tem[it, t, v]
                res_ref[t, v] = total
                following = ub[it, t, v] - jnp.float32(pseudo_step) * total
                ub[it + 1, t, v] = following
                new_ref[t, v] = following
            return c

        lax.fori_loop(0, VARS, finish, 0)

        for k in range(1, TM):
            forward_copy(it, k).wait_send()
            back_copy(it, k).wait_send()
        for step in range(1, 5):
            for way, t in ring_steps(step):
                ring_copy(it, step, way, t).wait_send()
        for kind in range(3):
            for t in range(2):
                column_copy(it, kind, t).wait_send()
        for way in range(2):
            pack_copy(it, way).wait_send()

    for it in range(ITERS):
        iteration(it)


def per_device(conserved_field, face_neighbours, counterpart_group, counterpart_shift, volume_operator, flux_matrix):
    wide = jnp.concatenate([volume_operator, volume_operator], axis=2)
    state = jax.ShapeDtypeStruct(conserved_field.shape, jnp.float32)
    vmem = pl.BlockSpec(memory_space=pltpu.VMEM)
    smem = pl.BlockSpec(memory_space=pltpu.SMEM)
    f32, bf16 = jnp.float32, jnp.bfloat16
    dma = pltpu.SemaphoreType.DMA
    return pl.pallas_call(
        kernel,
        out_shape=(state, state),
        in_specs=[pl.BlockSpec(memory_space=pl.ANY), vmem, smem, smem, vmem, smem],
        out_specs=(vmem, vmem),
        scratch_shapes=[
            pltpu.VMEM((ITERS + 1, 2, VARS, NODES, LANES), f32),
            pltpu.VMEM((VARS * NODES, VARS * NODES), bf16),
            pltpu.VMEM((VARS * NODES, VARS * NODES), bf16),
            pltpu.VMEM((ITERS, TM, 2, VARS, 8, LANES), f32),
            pltpu.VMEM((ITERS, SAMPLE_COUNT, VARS, 8, LANES), f32),
            pltpu.VMEM((ITERS, 2, VARS, NODES, LANES), f32),
            *[pltpu.VMEM((Z, VARS, 16, LANES), f32)] * 4,
            *[pltpu.VMEM((Q, VARS, 16, LANES), f32)] * 4,
            pltpu.VMEM((ITERS, 2, 16, LANES), f32),
            pltpu.VMEM((ITERS, 2, 16, LANES), f32),
            pltpu.VMEM((3, NODES, LANES), f32),
            pltpu.VMEM((2, VARS, 16, LANES), f32),
            pltpu.VMEM((2, VARS, 16, LANES), f32),
            pltpu.VMEM((2, VARS, 16, LANES), f32),
            dma,
            dma((ITERS, TM)), dma((ITERS, TM)),
            dma((ITERS, TM)), dma((ITERS, TM)),
            dma((ITERS, 16)), dma((ITERS, 16)),
            dma((ITERS, 6)), dma((ITERS, 6)),
            dma((ITERS, 2)), dma((ITERS, 2)),
        ],
        compiler_params=pltpu.CompilerParams(
            collective_id=0, has_side_effects=True, vmem_limit_bytes=48 * 1024 * 1024),
        name="iterations",
    )(conserved_field, face_neighbours, counterpart_group, counterpart_shift, wide, flux_matrix)


def solution(mesh):
    return jax.shard_map(
        per_device,
        mesh=mesh,
        in_specs=(P("tm", None, None, "space"), P(None, "space"), P("tm"), P("tm"), P(), P()),
        out_specs=(P("tm", None, None, "space"), P("tm", None, None, "space")),
        check_vma=False,
    )
```

time: 271 us -> 69.4 us (0.26)
  waiting for transfers between devices: 143 us -> 0 us
  Pallas kernels: 0 us -> 64.1 us
  local copies, waits for them, and re-layouts: 40.4 us -> 3.47 us
  starting transfers between devices: 25.6 us -> 0 us
  matrix products: 23.2 us -> 0 us
  other arithmetic: 19.2 us -> 1 us
  between operations: 18.6 us -> 0.68 us
    all_gather x2 -> x0, waiting for transfers between devices: 139 us -> none  [residual_of(): segment = lax.all_gather(slide_face, 'space', axis=3, tiled=True)]
    pallas_call x0 -> x1, Pallas kernels: none -> 64.1 us  [per_device(): pl.pallas_call(kernel, out_shape=(state, state), in_specs=[pl.BlockSpec(m...]
    dot_general x12 -> x0, matrix products: 23.2 us -> none  [the longest x6 15.2 us: face_term(): jnp.einsum('vw,twqe->tvqe', matrix, jump, precision=lax.Precision.HIGHEST)]
    all_to_all x4 -> x0, starting transfers between devices: 19.7 us -> none  [the longest x2 10.4 us: residual_of(): lax.all_to_all(field, 'tm', split_axis=2, concat_axis=0, tiled=True)]
    slice x9 -> x0, local copies, waits for them, and re-layouts: 9.39 us -> none  [the longest x2 5.33 us: residual_of(): window = lax.dynamic_slice_in_dim(padded[sample_slot], begin, elem_local, 2)]
    reshape x3 -> x0, local copies, waits for them, and re-layouts: 7.91 us -> none  [the longest x2 4.06 us: residual_of(): flat = gathered.reshape(gathered.shape[0], -1)]
    concatenate x2 -> x1, other arithmetic: 7.94 us -> 1 us  [per_device(): wide = jnp.concatenate([volume_operator, volume_operator], axis=2)]
    ppermute x4 -> x0, starting transfers between devices: 5.54 us -> none  [from_behind(): lax.ppermute(shard, axis, [(i, (i + by) % length) for i in range(length)])]
  transfers between devices with their start and end apart: 10 -> 0, of which waited for: 4 -> 0; matrix products, arithmetic and copies ran while one was open for 28% -> 0% of each run, Pallas kernels for 0% -> 0%
where the time goes in v1:
time: 69.4 us; the launch traced here: 69.2 us
  Pallas kernels  64.1 us (92%)
  local copies, waits for them, and re-layouts  3.47 us (5%)
  other arithmetic  1 us (1%)
    pallas_call x1, Pallas kernels, per_device(): pl.pallas_call(kernel, out_shape=(state, state), in_specs=[pl.BlockSpec(m...  64.1 us
    unnamed x11, local copies, waits for them, and re-layouts  3.47 us

profile of v1, /device:TPU:1, one launch (start us, length us, event | category | flops | bytes accessed | tf_op | source)
XLA Modules:
  0.0 69.2 jit_solution(4358425912765253576)
XLA Ops:
  0.6 0.7 %copy.8.flux_ref = f32[2,10,10]{2,1,0:T(8,128)S(1)} copy(f32[2,10,10]{2,0,1:T(2,128)} %param.11) | data formatting | bytes 1600 | tf_op args[5]
  1.3 0.0 copy-start.1
  1.3 0.0 copy-start.2
  1.3 0.0 copy-start.3
  1.3 1.0 %pad_maximum_fusion.vol_ref = f32[2,64,128]{2,1,0:T(8,128)S(1)} fusion(f32[2,64,64]{2,1,0:T(8,128)} %param.10), kind=kLoop, calls=%fused_computation | loop fusion | flops 16384 | bytes 98304 | tf_op jit(solution)/shard_map/concatenate | solution.py:371
  2.3 0.0 copy-done.1
  2.4 0.0 copy-done.2
  2.4 0.0 copy-done.3
  2.4 0.0 copy-start
  2.4 1.1 %copy-done = f32[2,10,64,128]{3,2,1,0:T(8,128)S(1)} copy-done((f32[2,10,64,128]{3,2,1,0:T(8,128)S(1)}, f32[2,10,64,128]{3,2,1,0:T(8,128)}, u32[]{:S(2)}) %copy-start) | copy-done | bytes 655384
  3.5 64.1 %iterations.1 = (f32[2,10,64,128]{3,2,1,0:T(8,128)S(1)}, f32[2,10,64,128]{3,2,1,0:T(8,128)S(1)}) custom-call(f32[2,10,64,128]{3,2,1,0:T(8,128)S(1)} %copy-done, s32[2,128]{1,0:T(2,128)S(1)} %copy-done.1, s32[2]{0:T(128)S(1)} %copy-done.2, s32[2]{0:T(128)S(1)} %copy-done.3, f32[2,64,128]{2,1,0:T(8,128)S(1)} %pad_maximum_fusion.vol_ref, ...), custom_call_target="tpu_custom_call" | custom-call | tf_op jit(solution)/shard_map/iterations/pallas_call | solution.py:377
  67.5 0.8 %copy.11 = f32[2,10,64,128]{3,2,1,0:T(8,128)} copy(f32[2,10,64,128]{3,2,1,0:T(8,128)S(1)} %get-tuple-element.4) | data formatting | bytes 1310720
  68.4 0.8 %copy.12 = f32[2,10,64,128]{3,2,1,0:T(8,128)} copy(f32[2,10,64,128]{3,2,1,0:T(8,128)S(1)} %get-tuple-element.5) | data formatting | bytes 1310720
Async XLA Ops:
  1.3 1.0 %copy-start.1 = (s32[2,128]{1,0:T(2,128)S(1)}, s32[2,128]{1,0:T(2,128)}, u32[]{:S(2)}) copy-start(s32[2,128]{1,0:T(2,128)} %fn_ref.1) | copy-start | bytes 3076
  1.3 1.0 %copy-start.2 = (s32[2]{0:T(128)S(1)}, s32[2]{0:T(128)}, u32[]{:S(2)}) copy-start(s32[2]{0:T(128)} %group_ref.1) | copy-start | bytes 28
  1.3 1.0 %copy-start.3 = (s32[2]{0:T(128)S(1)}, s32[2]{0:T(128)}, u32[]{:S(2)}) copy-start(s32[2]{0:T(128)} %shift_ref.1) | copy-start | bytes 28
  2.4 1.1 %copy-start = (f32[2,10,64,128]{3,2,1,0:T(8,128)S(1)}, f32[2,10,64,128]{3,2,1,0:T(8,128)}, u32[]{:S(2)}) copy-start(f32[2,10,64,128]{3,2,1,0:T(8,128)} %u_ref.1) | copy-start | bytes 1966084

commit v2 on v1

--- a/solution.py
+++ b/solution.py
@@ -13,6 +13,8 @@
 VARS = 10
 NODES = 64
 LANES = 128
+PARTS = 2
+PIECE = VARS // PARTS
 
 lift_scale = 2.0
 dissipation = 1.5
@@ -49,11 +51,11 @@
 def kernel(
     u_ref, fn_ref, group_ref, shift_ref, vol_ref, flux_ref,
     new_ref, res_ref,
-    ub, a_hi, a_lo, gat, der, tem, ring_00, ring_01, ring_10, ring_11, cols_00, cols_01, cols_10, cols_11,
-    packs, packed, side, lo_b, up_b, sl_b, in_sem, fs, fr, bs, br, zs, zr, cs, cr, ps, pr,
+    ub, a_hi, a_lo, gat, der, tem, ring_00, ring_01, ring_10, ring_11, cols_00, cols_01, cols_10, cols_11, cols_20, cols_21,
+    packs, packed, side, lo_b, up_b, sl_b, tw_b, in_sem, fs, fr, bs, br, zs, zr, cs, cr, ps, pr,
 ):
     ring = ((ring_00, ring_01), (ring_10, ring_11))
-    cols = ((cols_00, cols_01), (cols_10, cols_11))
+    cols = ((cols_00, cols_01), (cols_10, cols_11), (cols_20, cols_21))
     tm = lax.axis_index("tm")
     sp = lax.axis_index("space")
     z = sp // Q
@@ -77,8 +79,9 @@
         pl.semaphore_signal(barrier, inc=1, device_id={"tm": (tm + k) % TM}, device_id_type=MESH)
     for other in (z_up, z_dn, mate, cross, after, before):
         pl.semaphore_signal(barrier, inc=1, device_id={"space": other}, device_id_type=MESH)
-    load.wait()
-    pl.semaphore_wait(barrier, TM - 1 + 6)
+    with jax.named_scope("entry"):
+        load.wait()
+        pl.semaphore_wait(barrier, TM - 1 + 6)
 
     lane16 = lax.broadcasted_iota(jnp.int32, (16, LANES), 1)
     gidx = sp * LANES + lane16
@@ -116,43 +119,46 @@
             src_ref=der.at[it, pl.ds(2 * peer, 2)], dst_ref=tem.at[it, :, :, rows_of(peer), :],
             send_sem=bs.at[it, k], recv_sem=br.at[it, k], device_id={"tm": peer}, device_id_type=MESH)
 
-    def ring_copy(it, step, way, t):
+    def ring_slot(step, way, t, part):
+        return (((step - 1) * 2 + way) * 2 + t) * PARTS + part
+
+    def ring_copy(it, step, way, t, part):
         if way == 0:
             origin, target = (z + Z - (step - 1)) % Z, z_up
         else:
             origin, target = (z + step - 1) % Z, z_dn
-        block = ring[it][t].at[origin]
-        slot = ((step - 1) * 2 + way) * 2 + t
+        block = ring[it][t].at[origin, pl.ds(part * PIECE, PIECE)]
+        slot = ring_slot(step, way, t, part)
         return pltpu.make_async_remote_copy(
             src_ref=block, dst_ref=block, send_sem=zs.at[it, slot], recv_sem=zr.at[it, slot],
             device_id={"space": target}, device_id_type=MESH)
 
-    def ring_arrival(it, step, way, t):
+    def ring_arrival(it, step, way, t, part):
         if way == 0:
             origin, target = (z + Z - step) % Z, z_up
         else:
             origin, target = (z + step) % Z, z_dn
-        block = ring[it][t].at[origin]
-        slot = ((step - 1) * 2 + way) * 2 + t
+        block = ring[it][t].at[origin, pl.ds(part * PIECE, PIECE)]
+        slot = ring_slot(step, way, t, part)
         return pltpu.make_async_remote_copy(
             src_ref=block, dst_ref=block, send_sem=zs.at[it, slot], recv_sem=zr.at[it, slot],
             device_id={"space": target}, device_id_type=MESH)
 
-    def column_copy(it, kind, t):
-        origin, target = ((q, mate), (q, cross), ((q + 2) % Q, mate))[kind]
-        block = cols[it][t].at[origin]
-        slot = kind * 2 + t
-        return pltpu.make_async_remote_copy(
-            src_ref=block, dst_ref=block, send_sem=cs.at[it, slot], recv_sem=cr.at[it, slot],
+    def column_copy(kind, hop, t):
+        origin, target = ((q, mate), (q, cross), ((q + 2) % Q, mate))[hop]
+        block = cols[kind][t].at[origin]
+        slot = hop * 2 + t
+        return pltpu.make_async_remote_copy(
+            src_ref=block, dst_ref=block, send_sem=cs.at[kind, slot], recv_sem=cr.at[kind, slot],
             device_id={"space": target}, device_id_type=MESH)
 
-    def column_arrival(it, kind, t):
+    def column_arrival(kind, hop, t):
         mate_q = q + 1 - 2 * (q % 2)
-        origin, target = ((mate_q, mate), ((q + 2) % Q, cross), ((mate_q + 2) % Q, mate))[kind]
-        block = cols[it][t].at[origin]
-        slot = kind * 2 + t
-        return pltpu.make_async_remote_copy(
-            src_ref=block, dst_ref=block, send_sem=cs.at[it, slot], recv_sem=cr.at[it, slot],
+        origin, target = ((mate_q, mate), ((q + 2) % Q, cross), ((mate_q + 2) % Q, mate))[hop]
+        block = cols[kind][t].at[origin]
+        slot = hop * 2 + t
+        return pltpu.make_async_remote_copy(
+            src_ref=block, dst_ref=block, send_sem=cs.at[kind, slot], recv_sem=cr.at[kind, slot],
             device_id={"space": target}, device_id_type=MESH)
 
     def pack_copy(it, way):
@@ -160,9 +166,6 @@
         return pltpu.make_async_remote_copy(
             src_ref=packs.at[it, way], dst_ref=packed.at[it, way], send_sem=ps.at[it, way], recv_sem=pr.at[it, way],
             device_id={"space": target}, device_id_type=MESH)
-
-    def ring_steps(step):
-        return ((0, 0), (1, 0), (0, 1), (1, 1)) if step < 4 else ((0, 0), (1, 1))
 
     def build_matrix():
         row = lax.broadcasted_iota(jnp.int32, (NODES, LANES), 0)
@@ -174,15 +177,15 @@
         upper = jnp.where(on & (row >= 48), one, zero)
         slide = jnp.where(on & (jnp.bitwise_and(row, 3) == 3), one, zero)
         scale = jnp.float32(0.5 * lift_scale)
-        side[0] = vol_ref[0] + scale * (lower - upper)
-        side[1] = vol_ref[1] - scale * slide
+        side[0] = jnp.concatenate([vol_ref[0], vol_ref[0]], axis=1) + scale * (lower - upper)
+        side[1] = jnp.concatenate([vol_ref[1], vol_ref[1]], axis=1) - scale * slide
         side[2] = (scale * jnp.float32(dissipation)) * (lower + upper + slide)
 
         def row_block(v, carry):
             for j in range(VARS // 2):
                 tile = jnp.zeros((NODES, LANES), jnp.float32)
                 for d in range(2):
-                    factor = jnp.where(first, flux_ref[d, v, 2 * j], flux_ref[d, v, 2 * j + 1])
+                    factor = jnp.where(first, flux_ref[v, d, 2 * j], flux_ref[v, d, 2 * j + 1])
                     tile = tile + factor * side[d]
                 own = jnp.where(first, jnp.where(v == 2 * j, one, zero), jnp.where(v == 2 * j + 1, one, zero))
                 tile = tile + own * side[2]
@@ -207,13 +210,22 @@
             for t in range(2):
                 res_ref[t, pl.ds(part * 5, 5)] = out[:, t * LANES:(t + 1) * LANES].reshape(5, NODES, LANES)
 
-    def iteration(it):
-        for t in range(2):
-            ring[it][t][z] = ub[it, t, :, pl.ds(3, 16, stride=4), :]
-        for way, t in ring_steps(1):
-            ring_copy(it, 1, way, t).start()
-        for k in range(1, TM):
-            forward_copy(it, k).start()
+    def ring_chunks(step, t):
+        ways = (0, 1) if step < 4 else (t,)
+        return [(way, part) for part in range(PARTS) for way in ways]
+
+    def ring_start(it, t):
+        for way, part in ring_chunks(1, t):
+            ring_copy(it, 1, way, t, part).start()
+
+    def ring_relay(it, step, t):
+        onward = ring_chunks(step + 1, t) if step < 4 else []
+        for way, part in ring_chunks(step, t):
+            ring_arrival(it, step, way, t, part).wait_recv()
+            if (way, part) in onward:
+                ring_copy(it, step + 1, way, t, part).start()
+
+    def pack_traces(it):
         up_pack = jnp.zeros((16, LANES), jnp.float32)
         lo_pack = jnp.zeros((16, LANES), jnp.float32)
         for i in range(2 * VARS):
@@ -226,18 +238,11 @@
         packs[it, 1] = lo_pack
         for way in range(2):
             pack_copy(it, way).start()
-        gat[it, tm] = ub[it, :, :, rows_of(tm), :]
-
-        if it == 0:
-            build_matrix()
-
-        volume_part(it)
-
-        for way, t in ring_steps(1):
-            ring_arrival(it, 1, way, t).wait_recv()
-            if (way, t) in ring_steps(2):
-                ring_copy(it, 2, way, t).start()
-
+
+    scale = jnp.float32(0.5 * lift_scale)
+    loss = jnp.float32(0.5 * lift_scale * dissipation)
+
+    def first_direction(it):
         for way in range(2):
             pack_copy(it, way).wait_recv()
         from_before = packed[it, 0]
@@ -254,14 +259,11 @@
             far = jnp.take_along_axis(from_after, jnp.bitwise_and(ahead + REACH * i, LANES - 1), axis=1)
             up_b[i // VARS, i % VARS] = jnp.where(ahead >= LANES, far, own)
 
-        scale = jnp.float32(0.5 * lift_scale)
-        loss = jnp.float32(0.5 * lift_scale * dissipation)
-
         def first_faces(v, c):
             low = -loss * lo_b[:, v]
             upp = -loss * up_b[:, v]
             for w in range(VARS):
-                f = scale * flux_ref[0, v, w]
+                f = scale * flux_ref[v, 0, w]
                 low = low - f * lo_b[:, w]
                 upp = upp + f * up_b[:, w]
             res_ref[:, v, pl.ds(0, 16), :] += low
@@ -270,11 +272,7 @@
 
         lax.fori_loop(0, VARS, first_faces, 0)
 
-        for way, t in ring_steps(2):
-            ring_arrival(it, 2, way, t).wait_recv()
-            if (way, t) in ring_steps(3):
-                ring_copy(it, 3, way, t).start()
-
+    def time_derivative(it):
         for k in range(1, TM):
             forward_arrival(it, k).wait_recv()
 
@@ -299,76 +297,195 @@
             back_copy(it, k).start()
         tem[it, :, :, rows_of(tm), :] = der[it, pl.ds(2 * tm, 2)]
 
-        for way, t in ring_steps(3):
-            ring_arrival(it, 3, way, t).wait_recv()
-            if (way, t) in ring_steps(4):
-                ring_copy(it, 4, way, t).start()
-        for way, t in ring_steps(4):
-            ring_arrival(it, 4, way, t).wait_recv()
-
-        lane_b = lax.broadcasted_iota(jnp.int32, (VARS, 16, LANES), 2)
-        for t in range(2):
-            group, shift = group_ref[t], shift_ref[t]
-            first_dst = jnp.bitwise_and(q - group, Q - 1)
-            second_dst = jnp.bitwise_and(q - group - 1, Q - 1)
-            first = jnp.bitwise_and(z + lax.shift_right_arithmetic(first_dst + group - q, 2), Z - 1)
-            second = jnp.bitwise_and(z + lax.shift_right_arithmetic(second_dst + group + 1 - q, 2), Z - 1)
-            cols[it][t][q] = jnp.where(lane_b >= shift, ring[it][t][first], ring[it][t][second])
-            column_copy(it, 1, t).start()
-            column_copy(it, 0, t).start()
-        for t in range(2):
-            column_arrival(it, 1, t).wait_recv()
-            column_copy(it, 2, t).start()
-        for t in range(2):
-            group, shift = group_ref[t], shift_ref[t]
-            column_arrival(it, 0, t).wait_recv()
-            column_arrival(it, 2, t).wait_recv()
-            first = cols[it][t][jnp.bitwise_and(q + group, Q - 1)]
-            second = cols[it][t][jnp.bitwise_and(q + group + 1, Q - 1)]
-            both = jnp.where(lane_b >= shift, first, second)
-            both = pltpu.roll(both.reshape(VARS * 16, LANES), jnp.bitwise_and(LANES - shift, LANES - 1), 1)
-            sl_b[t] = both.reshape(VARS, 16, LANES)
-            cosine, sine = pick(2 * tm + t, cosines), pick(2 * tm + t, sines)
-            one, two = sl_b[t, 1], sl_b[t, 2]
-            sl_b[t, 1] = cosine * one - sine * two
-            sl_b[t, 2] = sine * one + cosine * two
-
+    def offset_of(kind, t):
+        group, shift = group_ref[t], shift_ref[t]
+        if kind == 1:
+            group = jnp.bitwise_and(2 * group + lax.shift_right_arithmetic(shift, 6), SP - 1)
+            shift = jnp.bitwise_and(2 * shift, LANES - 1)
+        return group, shift
+
+    lane_b = lax.broadcasted_iota(jnp.int32, (VARS, 16, LANES), 2)
+
+    def column_start(kind, t):
+        it = kind // 2
+        group, shift = offset_of(kind, t)
+        first_dst = jnp.bitwise_and(q - group, Q - 1)
+        second_dst = jnp.bitwise_and(q - group - 1, Q - 1)
+        first = jnp.bitwise_and(z + lax.shift_right_arithmetic(first_dst + group - q, 2), Z - 1)
+        second = jnp.bitwise_and(z + lax.shift_right_arithmetic(second_dst + group + 1 - q, 2), Z - 1)
+        cols[kind][t][q] = jnp.where(lane_b >= shift, ring[it][t][first], ring[it][t][second])
+        column_copy(kind, 1, t).start()
+        column_copy(kind, 0, t).start()
+
+    def column_relay(kind, t):
+        column_arrival(kind, 1, t).wait_recv()
+        column_copy(kind, 2, t).start()
+
+    def column_finish(kind, t):
+        column_arrival(kind, 0, t).wait_recv()
+        column_arrival(kind, 2, t).wait_recv()
+        group, shift = offset_of(kind, t)
+        first = cols[kind][t][jnp.bitwise_and(q + group, Q - 1)]
+        second = cols[kind][t][jnp.bitwise_and(q + group + 1, Q - 1)]
+        both = jnp.where(lane_b >= shift, first, second)
+        both = pltpu.roll(both.reshape(VARS * 16, LANES), jnp.bitwise_and(LANES - shift, LANES - 1), 1)
+        return both.reshape(VARS, 16, LANES)
+
+    def turn(t):
+        cosine, sine = pick(2 * tm + t, cosines), pick(2 * tm + t, sines)
+        one, two = sl_b[t, 1], sl_b[t, 2]
+        sl_b[t, 1] = cosine * one - sine * two
+        sl_b[t, 2] = sine * one + cosine * two
+
+    def slide_term(t, v):
+        term = -loss * sl_b[t, v]
+        for w in range(VARS):
+            term = term + (scale * flux_ref[v, 1, w]) * sl_b[t, w]
+        return term
+
+    step_size = jnp.float32(pseudo_step)
+    scope = jax.named_scope
+
+    with scope("start0"):
+        for t in range(2):
+            ring[0][t][z] = ub[0, t, :, pl.ds(3, 16, stride=4), :]
+            ring_start(0, t)
         for k in range(1, TM):
-            back_arrival(it, k).wait_recv()
-
-        def finish(v, c):
+            forward_copy(0, k).start()
+        pack_traces(0)
+        gat[0, tm] = ub[0, :, :, rows_of(tm), :]
+    with scope("matrix"):
+        build_matrix()
+    with scope("volume0"):
+        volume_part(0)
+    with scope("ring0_1"):
+        ring_relay(0, 1, 0)
+        ring_relay(0, 1, 1)
+    with scope("ring0_2a"):
+        ring_relay(0, 2, 0)
+    with scope("derive0"):
+        time_derivative(0)
+    with scope("ring0_2b"):
+        ring_relay(0, 2, 1)
+    with scope("first0"):
+        first_direction(0)
+    with scope("ring0_3"):
+        ring_relay(0, 3, 0)
+        ring_relay(0, 3, 1)
+    with scope("ring0_4"):
+        for t in range(2):
+            ring_relay(0, 4, t)
+            column_start(0, t)
+    with scope("back0"):
+        for k in range(1, TM):
+            back_arrival(0, k).wait_recv()
+
+    def partial_state(v, c):
+        for t in range(2):
+            ub[1, t, v] = ub[0, t, v] - step_size * (res_ref[t, v] + tem[0, t, v])
+        return c
+
+    with scope("w"):
+        lax.fori_loop(0, VARS, partial_state, 0)
+        for t in range(2):
+            ring[1][t][z] = ub[1, t, :, pl.ds(3, 16, stride=4), :]
+            ring_start(1, t)
+    with scope("cols1_start"):
+        for t in range(2):
+            column_start(1, t)
+    with scope("ring1_1a"):
+        ring_relay(1, 1, 0)
+    with scope("cols0_relay"):
+        for t in range(2):
+            column_relay(0, t)
+    with scope("ring1_1b"):
+        ring_relay(1, 1, 1)
+    with scope("cols0_finish"):
+        for t in range(2):
+            sl_b[t] = column_finish(0, t)
+            turn(t)
+
+    def next_state(v, c):
+        for t in range(2):
+            ub[1, t, v, pl.ds(3, 16, stride=4), :] += -step_size * slide_term(t, v)
+        return c
+
+    with scope("u1"):
+        lax.fori_loop(0, VARS, next_state, 0)
+        for k in range(1, TM):
+            forward_copy(1, k).start()
+        pack_traces(1)
+        gat[1, tm] = ub[1, :, :, rows_of(tm), :]
+    with scope("volume1"):
+        volume_part(1)
+    with scope("ring1_2"):
+        ring_relay(1, 2, 0)
+    with scope("cols1_relay"):
+        for t in range(2):
+            column_relay(1, t)
+    with scope("ring1_2b"):
+        ring_relay(1, 2, 1)
+    with scope("cols1_finish"):
+        for t in range(2):
+            sl_b[t] = column_finish(1, t)
+            turn(t)
+
+        def twice(v, c):
             for t in range(2):
-                term = -loss * sl_b[t, v]
-                for w in range(VARS):
-                    term = term + (scale * flux_ref[1, v, w]) * sl_b[t, w]
-                res_ref[t, v, pl.ds(3, 16, stride=4), :] += term
-                total = res_ref[t, v] + tem[it, t, v]
-                res_ref[t, v] = total
-                following = ub[it, t, v] - jnp.float32(pseudo_step) * total
-                ub[it + 1, t, v] = following
-                new_ref[t, v] = following
+                tw_b[t, v] = step_size * slide_term(t, v)
             return c
 
+        lax.fori_loop(0, VARS, twice, 0)
+    with scope("first1"):
+        first_direction(1)
+    with scope("ring1_3"):
+        ring_relay(1, 3, 0)
+        ring_relay(1, 3, 1)
+    with scope("derive1"):
+        time_derivative(1)
+    with scope("ring1_4"):
+        for t in range(2):
+            ring_relay(1, 4, t)
+            column_start(2, t)
+    with scope("cols2_relay"):
+        for t in range(2):
+            column_relay(2, t)
+    with scope("cols2_finish"):
+        for t in range(2):
+            sl_b[t] = column_finish(2, t) - tw_b[t]
+            turn(t)
+    with scope("back1"):
+        for k in range(1, TM):
+            back_arrival(1, k).wait_recv()
+
+    def finish(v, c):
+        for t in range(2):
+            res_ref[t, v, pl.ds(3, 16, stride=4), :] += slide_term(t, v)
+            total = res_ref[t, v] + tem[1, t, v]
+            res_ref[t, v] = total
+            new_ref[t, v] = ub[1, t, v] - step_size * total
+        return c
+
+    with scope("finish"):
         lax.fori_loop(0, VARS, finish, 0)
-
-        for k in range(1, TM):
-            forward_copy(it, k).wait_send()
-            back_copy(it, k).wait_send()
-        for step in range(1, 5):
-            for way, t in ring_steps(step):
-                ring_copy(it, step, way, t).wait_send()
+    with scope("sends"):
+        for it in range(ITERS):
+            for k in range(1, TM):
+                forward_copy(it, k).wait_send()
+                back_copy(it, k).wait_send()
+            for step in range(1, 5):
+                for t in range(2):
+                    for way, part in ring_chunks(step, t):
+                        ring_copy(it, step, way, t, part).wait_send()
+            for way in range(2):
+                pack_copy(it, way).wait_send()
         for kind in range(3):
-            for t in range(2):
-                column_copy(it, kind, t).wait_send()
-        for way in range(2):
-            pack_copy(it, way).wait_send()
-
-    for it in range(ITERS):
-        iteration(it)
+            for hop in range(3):
+                for t in range(2):
+                    column_copy(kind, hop, t).wait_send()
 
 
 def per_device(conserved_field, face_neighbours, counterpart_group, counterpart_shift, volume_operator, flux_matrix):
-    wide = jnp.concatenate([volume_operator, volume_operator], axis=2)
     state = jax.ShapeDtypeStruct(conserved_field.shape, jnp.float32)
     vmem = pl.BlockSpec(memory_space=pltpu.VMEM)
     smem = pl.BlockSpec(memory_space=pltpu.SMEM)
@@ -380,31 +497,33 @@
         in_specs=[pl.BlockSpec(memory_space=pl.ANY), vmem, smem, smem, vmem, smem],
         out_specs=(vmem, vmem),
         scratch_shapes=[
-            pltpu.VMEM((ITERS + 1, 2, VARS, NODES, LANES), f32),
+            pltpu.VMEM((ITERS, 2, VARS, NODES, LANES), f32),
             pltpu.VMEM((VARS * NODES, VARS * NODES), bf16),
             pltpu.VMEM((VARS * NODES, VARS * NODES), bf16),
             pltpu.VMEM((ITERS, TM, 2, VARS, 8, LANES), f32),
             pltpu.VMEM((ITERS, SAMPLE_COUNT, VARS, 8, LANES), f32),
             pltpu.VMEM((ITERS, 2, VARS, NODES, LANES), f32),
             *[pltpu.VMEM((Z, VARS, 16, LANES), f32)] * 4,
-            *[pltpu.VMEM((Q, VARS, 16, LANES), f32)] * 4,
+            *[pltpu.VMEM((Q, VARS, 16, LANES), f32)] * 6,
             pltpu.VMEM((ITERS, 2, 16, LANES), f32),
             pltpu.VMEM((ITERS, 2, 16, LANES), f32),
             pltpu.VMEM((3, NODES, LANES), f32),
             pltpu.VMEM((2, VARS, 16, LANES), f32),
             pltpu.VMEM((2, VARS, 16, LANES), f32),
             pltpu.VMEM((2, VARS, 16, LANES), f32),
+            pltpu.VMEM((2, VARS, 16, LANES), f32),
             dma,
             dma((ITERS, TM)), dma((ITERS, TM)),
             dma((ITERS, TM)), dma((ITERS, TM)),
-            dma((ITERS, 16)), dma((ITERS, 16)),
-            dma((ITERS, 6)), dma((ITERS, 6)),
+            dma((ITERS, 16 * PARTS)), dma((ITERS, 16 * PARTS)),
+            dma((3, 6)), dma((3, 6)),
             dma((ITERS, 2)), dma((ITERS, 2)),
         ],
         compiler_params=pltpu.CompilerParams(
             collective_id=0, has_side_effects=True, vmem_limit_bytes=48 * 1024 * 1024),
         name="iterations",
-    )(conserved_field, face_neighbours, counterpart_group, counterpart_shift, wide, flux_matrix)
+    )(conserved_field, face_neighbours, counterpart_group, counterpart_shift, volume_operator,
+      jnp.transpose(flux_matrix, (1, 0, 2)))
 
 
 def solution(mesh):

time: 69.4 us -> 71.1 us (1.024)
  local copies, waits for them, and re-layouts: 3.47 us -> 5.64 us
  other arithmetic: 1 us -> 0 us
    unnamed x11 -> x14, local copies, waits for them, and re-layouts: 3.47 us -> 5.64 us
    concatenate x1 -> x0, other arithmetic: 1 us -> none  [per_device(): wide = jnp.concatenate([volume_operator, volume_operator], axis=2)]
where the time goes in v2:
time: 71.1 us; the launch traced here: 70.8 us
  Pallas kernels  64.5 us (91%)
  local copies, waits for them, and re-layouts  5.64 us (8%)
    pallas_call x1, Pallas kernels, per_device(): pl.pallas_call(kernel, out_shape=(state, state), in_specs=[pl.BlockSpec(m...  64.5 us
    unnamed x14, local copies, waits for them, and re-layouts  5.64 us

profile of v2, /device:TPU:1, one launch (start us, length us, event | category | flops | bytes accessed | tf_op | source)
XLA Modules:
  0.0 70.8 jit_solution(16316893234665760371)
XLA Ops:
  0.6 0.0 copy-start.4
  0.6 0.0 copy-start.3
  0.7 0.6 copy-done.4
  1.3 0.0 copy-done.3
  1.3 0.0 copy-start
  1.3 1.1 %copy-done = f32[2,10,64,128]{3,2,1,0:T(8,128)S(1)} copy-done((f32[2,10,64,128]{3,2,1,0:T(8,128)S(1)}, f32[2,10,64,128]{3,2,1,0:T(8,128)}, u32[]{:S(2)}) %copy-start) | copy-done | bytes 655384
  2.4 0.0 copy-start.1
  2.4 0.8 %copy-done.1 = f32[2,64,64]{2,1,0:T(8,128)S(1)} copy-done((f32[2,64,64]{2,1,0:T(8,128)S(1)}, f32[2,64,64]{2,1,0:T(8,128)}, u32[]{:S(2)}) %copy-start.1) | copy-done | bytes 32792
  3.3 0.0 copy-start.2
  3.3 0.7 copy-done.2
  4.0 0.0 copy-start.5
  4.0 0.7 copy-done.5
  4.6 64.5 %iterations.1 = (f32[2,10,64,128]{3,2,1,0:T(8,128)S(1)}, f32[2,10,64,128]{3,2,1,0:T(8,128)S(1)}) custom-call(f32[2,10,64,128]{3,2,1,0:T(8,128)S(1)} %copy-done, s32[2,128]{1,0:T(2,128)S(1)} %copy-done.3, s32[2]{0:T(128)S(1)} %copy-done.4, s32[2]{0:T(128)S(1)} %copy-done.5, f32[2,64,64]{2,1,0:T(8,128)S(1)} %copy-done.1, f32[10,2,10]{2,1,0:T(2,128)S(1)} %bitcast.1), custom_call_target="tpu_custom_call" | custom-call | tf_op jit(solution)/shard_map/iterations/pallas_call | solution.py:494
  69.1 0.8 %copy.10 = f32[2,10,64,128]{3,2,1,0:T(8,128)} copy(f32[2,10,64,128]{3,2,1,0:T(8,128)S(1)} %get-tuple-element.4) | data formatting | bytes 1310720
  70.0 0.8 %copy.11 = f32[2,10,64,128]{3,2,1,0:T(8,128)} copy(f32[2,10,64,128]{3,2,1,0:T(8,128)S(1)} %get-tuple-element.5) | data formatting | bytes 1310720
Async XLA Ops:
  0.6 0.7 copy-start.4
  0.6 0.7 copy-start.3
  1.3 1.1 %copy-start = (f32[2,10,64,128]{3,2,1,0:T(8,128)S(1)}, f32[2,10,64,128]{3,2,1,0:T(8,128)}, u32[]{:S(2)}) copy-start(f32[2,10,64,128]{3,2,1,0:T(8,128)} %u_ref.1) | copy-start | bytes 1966084
  2.4 0.8 %copy-start.1 = (f32[2,64,64]{2,1,0:T(8,128)S(1)}, f32[2,64,64]{2,1,0:T(8,128)}, u32[]{:S(2)}) copy-start(f32[2,64,64]{2,1,0:T(8,128)} %vol_ref.1) | copy-start | bytes 98308
  3.3 0.7 copy-start.2
  4.0 0.7 copy-start.5

commit v3 on v2

--- a/solution.py
+++ b/solution.py
@@ -13,7 +13,7 @@
 VARS = 10
 NODES = 64
 LANES = 128
-PARTS = 2
+PARTS = 5
 PIECE = VARS // PARTS
 
 lift_scale = 2.0
@@ -23,6 +23,7 @@
 pseudo_step = 0.2
 
 MESH = pl.DeviceIdType.MESH
+MOVES = ((2, 1), (1, 1), (3, 1), (0, 1), (2, 0), (1, 0), (3, 0))
 TM = 8
 SP = 32
 Z = 8
@@ -51,7 +52,7 @@
 def kernel(
     u_ref, fn_ref, group_ref, shift_ref, vol_ref, flux_ref,
     new_ref, res_ref,
-    ub, a_hi, a_lo, gat, der, tem, ring_00, ring_01, ring_10, ring_11, cols_00, cols_01, cols_10, cols_11, cols_20, cols_21,
+    ub, a_hi, a_lo, gat, der, der2, tem, tem2, sig, sig_gat, sig_der, sig_tem, ring_00, ring_01, ring_10, ring_11, cols_00, cols_01, cols_10, cols_11, cols_20, cols_21,
     packs, packed, side, lo_b, up_b, sl_b, tw_b, in_sem, fs, fr, bs, br, zs, zr, cs, cr, ps, pr,
 ):
     ring = ((ring_00, ring_01), (ring_10, ring_11))
@@ -95,29 +96,48 @@
     def rows_of(index):
         return pl.ds(pl.multiple_of(index * 8, 8), 8)
 
-    def forward_copy(it, k):
-        peer = (tm + k) % TM
-        return pltpu.make_async_remote_copy(
-            src_ref=ub.at[it, :, :, rows_of(peer), :], dst_ref=gat.at[it, tm],
-            send_sem=fs.at[it, k], recv_sem=fr.at[it, k], device_id={"tm": peer}, device_id_type=MESH)
-
-    def forward_arrival(it, k):
-        peer = (tm + TM - k) % TM
-        return pltpu.make_async_remote_copy(
-            src_ref=ub.at[it, :, :, rows_of(peer), :], dst_ref=gat.at[it, peer],
-            send_sem=fs.at[it, k], recv_sem=fr.at[it, k], device_id={"tm": peer}, device_id_type=MESH)
-
-    def back_copy(it, k):
-        peer = (tm + k) % TM
-        return pltpu.make_async_remote_copy(
-            src_ref=der.at[it, pl.ds(2 * peer, 2)], dst_ref=tem.at[it, :, :, rows_of(tm), :],
-            send_sem=bs.at[it, k], recv_sem=br.at[it, k], device_id={"tm": peer}, device_id_type=MESH)
-
-    def back_arrival(it, k):
-        peer = (tm + TM - k) % TM
-        return pltpu.make_async_remote_copy(
-            src_ref=der.at[it, pl.ds(2 * peer, 2)], dst_ref=tem.at[it, :, :, rows_of(peer), :],
-            send_sem=bs.at[it, k], recv_sem=br.at[it, k], device_id={"tm": peer}, device_id_type=MESH)
+    def peer_at(k, sign):
+        dy, dx = MOVES[k]
+        return ((tm // 2 + sign * dy + 4) % 4) * 2 + (tm % 2 + dx) % 2
+
+    def three(index):
+        return pl.ds(3 * index, 3)
+
+    def forward_copy(kind, k):
+        peer = peer_at(k, 1)
+        source = ub.at[0, :, :, rows_of(peer), :] if kind == 0 else sig.at[:, three(peer)]
+        target = gat.at[tm] if kind == 0 else sig_gat.at[tm]
+        return pltpu.make_async_remote_copy(
+            src_ref=source, dst_ref=target, send_sem=fs.at[kind, k], recv_sem=fr.at[kind, k],
+            device_id={"tm": peer}, device_id_type=MESH)
+
+    def forward_arrival(kind, k):
+        peer = peer_at(k, -1)
+        source = ub.at[0, :, :, rows_of(peer), :] if kind == 0 else sig.at[:, three(peer)]
+        target = gat.at[peer] if kind == 0 else sig_gat.at[peer]
+        return pltpu.make_async_remote_copy(
+            src_ref=source, dst_ref=target, send_sem=fs.at[kind, k], recv_sem=fr.at[kind, k],
+            device_id={"tm": peer}, device_id_type=MESH)
+
+    def back_refs(kind, peer, place):
+        source = (der, sig_der, der2)[kind].at[pl.ds(2 * peer, 2)]
+        if kind == 1:
+            return source, sig_tem.at[:, three(place)]
+        return source, (tem, None, tem2)[kind].at[:, :, rows_of(place), :]
+
+    def back_copy(kind, k):
+        peer = peer_at(k, 1)
+        source, target = back_refs(kind, peer, tm)
+        return pltpu.make_async_remote_copy(
+            src_ref=source, dst_ref=target, send_sem=bs.at[kind, k], recv_sem=br.at[kind, k],
+            device_id={"tm": peer}, device_id_type=MESH)
+
+    def back_arrival(kind, k):
+        peer = peer_at(k, -1)
+        source, target = back_refs(kind, peer, peer)
+        return pltpu.make_async_remote_copy(
+            src_ref=source, dst_ref=target, send_sem=bs.at[kind, k], recv_sem=br.at[kind, k],
+            device_id={"tm": peer}, device_id_type=MESH)
 
     def ring_slot(step, way, t, part):
         return (((step - 1) * 2 + way) * 2 + t) * PARTS + part
@@ -234,19 +254,19 @@
             l_face = ub[it, i // VARS, i % VARS, pl.ds(0, 16), :]
             up_pack = jnp.where(mine, pltpu.roll(u_face, (REACH * i + REACH) % LANES, 1), up_pack)
             lo_pack = jnp.where(mine, pltpu.roll(l_face, REACH * i, 1) if i else l_face, lo_pack)
-        packs[it, 0] = up_pack
-        packs[it, 1] = lo_pack
+        packs[it // 2, 0] = up_pack
+        packs[it // 2, 1] = lo_pack
         for way in range(2):
-            pack_copy(it, way).start()
+            pack_copy(it // 2, way).start()
 
     scale = jnp.float32(0.5 * lift_scale)
     loss = jnp.float32(0.5 * lift_scale * dissipation)
 
     def first_direction(it):
         for way in range(2):
-            pack_copy(it, way).wait_recv()
-        from_before = packed[it, 0]
-        from_after = packed[it, 1]
+            pack_copy(it // 2, way).wait_recv()
+        from_before = packed[it // 2, 0]
+        from_after = packed[it // 2, 1]
         behind = lane16 - back_gap
         ahead = lane16 + ahead_gap
         for i in range(2 * VARS):
@@ -272,30 +292,34 @@
 
         lax.fori_loop(0, VARS, first_faces, 0)
 
-    def time_derivative(it):
-        for k in range(1, TM):
-            forward_arrival(it, k).wait_recv()
-
-        def derive(v, c):
-            x = [gat[it, t // 2, t % 2, v] for t in range(SAMPLE_COUNT)]
-            diff = {}
-            for t in range(SAMPLE_COUNT // 2):
-                for m in range(1, SAMPLE_COUNT // 2):
-                    diff[t, m] = x[(t + m) % SAMPLE_COUNT] - x[(t - m) % SAMPLE_COUNT]
-            for t in range(SAMPLE_COUNT // 2):
-                near = jnp.float32(weights[0]) * diff[t, 1]
-                opposite = jnp.float32(-weights[SAMPLE_COUNT // 2 - 2]) * diff[t, 1]
-                for m in range(2, SAMPLE_COUNT // 2):
-                    near = near + jnp.float32(weights[m - 1]) * diff[t, m]
-                    opposite = opposite - jnp.float32(weights[SAMPLE_COUNT // 2 - m - 1]) * diff[t, m]
-                der[it, t, v] = near
-                der[it, t + SAMPLE_COUNT // 2, v] = opposite
-            return c
-
-        lax.fori_loop(0, VARS, derive, 0)
-        for k in range(1, TM):
-            back_copy(it, k).start()
-        tem[it, :, :, rows_of(tm), :] = der[it, pl.ds(2 * tm, 2)]
+    def spectral(load_at, store_at):
+        x = [load_at(t) for t in range(SAMPLE_COUNT)]
+        half = SAMPLE_COUNT // 2
+        for t in range(half):
+            near = opposite = None
+            for m in range(1, half):
+                diff = x[(t + m) % SAMPLE_COUNT] - x[(t - m) % SAMPLE_COUNT]
+                one, two = jnp.float32(weights[m - 1]) * diff, jnp.float32(-weights[half - m - 1]) * diff
+                near = one if near is None else near + one
+                opposite = two if opposite is None else opposite + two
+            store_at(t, near)
+            store_at(t + half, opposite)
+
+    def first_derivative(v, c):
+        spectral(lambda t: gat[t // 2, t % 2, v], lambda t, value: der.__setitem__((t, v), value))
+        return c
+
+    def second_derivative(v, c):
+        spectral(lambda t: der[t, v], lambda t, value: der2.__setitem__((t, v), value))
+        return c
+
+    def sliding_derivative(i, c):
+        spectral(lambda t: sig_gat[t // 2, t % 2, i], lambda t, value: sig_der.__setitem__((t, i), value))
+        return c
+
+    def exchange_all(make, kind, method):
+        for k in range(len(MOVES)):
+            getattr(make(kind, k), method)()
 
     def offset_of(kind, t):
         group, shift = group_ref[t], shift_ref[t]
@@ -350,10 +374,10 @@
         for t in range(2):
             ring[0][t][z] = ub[0, t, :, pl.ds(3, 16, stride=4), :]
             ring_start(0, t)
-        for k in range(1, TM):
-            forward_copy(0, k).start()
         pack_traces(0)
-        gat[0, tm] = ub[0, :, :, rows_of(tm), :]
+        exchange_all(forward_copy, 0, "start")
+        gat[tm] = ub[0, :, :, rows_of(tm), :]
+        sig[:, pl.ds(2 * VARS, 4)] = jnp.zeros((2, 4, 8, LANES), jnp.float32)
     with scope("matrix"):
         build_matrix()
     with scope("volume0"):
@@ -363,26 +387,33 @@
         ring_relay(0, 1, 1)
     with scope("ring0_2a"):
         ring_relay(0, 2, 0)
+    with scope("fwd0"):
+        exchange_all(forward_arrival, 0, "wait_recv")
     with scope("derive0"):
-        time_derivative(0)
+        lax.fori_loop(0, VARS, first_derivative, 0)
+        exchange_all(back_copy, 0, "start")
+        tem[:, :, rows_of(tm), :] = der[pl.ds(2 * tm, 2)]
     with scope("ring0_2b"):
         ring_relay(0, 2, 1)
     with scope("first0"):
         first_direction(0)
     with scope("ring0_3"):
         ring_relay(0, 3, 0)
+    with scope("derive2"):
+        lax.fori_loop(0, VARS, second_derivative, 0)
+        tem2[:, :, rows_of(tm), :] = der2[pl.ds(2 * tm, 2)]
+    with scope("ring0_3b"):
         ring_relay(0, 3, 1)
     with scope("ring0_4"):
         for t in range(2):
             ring_relay(0, 4, t)
             column_start(0, t)
     with scope("back0"):
-        for k in range(1, TM):
-            back_arrival(0, k).wait_recv()
+        exchange_all(back_arrival, 0, "wait_recv")
 
     def partial_state(v, c):
         for t in range(2):
-            ub[1, t, v] = ub[0, t, v] - step_size * (res_ref[t, v] + tem[0, t, v])
+            ub[1, t, v] = ub[0, t, v] - step_size * (res_ref[t, v] + tem[t, v])
         return c
 
     with scope("w"):
@@ -393,6 +424,7 @@
     with scope("cols1_start"):
         for t in range(2):
             column_start(1, t)
+        exchange_all(back_copy, 2, "start")
     with scope("ring1_1a"):
         ring_relay(1, 1, 0)
     with scope("cols0_relay"):
@@ -407,17 +439,20 @@
 
     def next_state(v, c):
         for t in range(2):
-            ub[1, t, v, pl.ds(3, 16, stride=4), :] += -step_size * slide_term(t, v)
+            term = slide_term(t, v)
+            sig[t, 2 * v] = term[0:8]
+            sig[t, 2 * v + 1] = term[8:16]
+            ub[1, t, v, pl.ds(3, 16, stride=4), :] += -step_size * term
+            ub[2, t, v] = ub[1, t, v] - step_size * tem[t, v]
         return c
 
     with scope("u1"):
         lax.fori_loop(0, VARS, next_state, 0)
-        for k in range(1, TM):
-            forward_copy(1, k).start()
-        pack_traces(1)
-        gat[1, tm] = ub[1, :, :, rows_of(tm), :]
+        exchange_all(forward_copy, 1, "start")
+        pack_traces(2)
+        sig_gat[tm] = sig[:, three(tm)]
     with scope("volume1"):
-        volume_part(1)
+        volume_part(2)
     with scope("ring1_2"):
         ring_relay(1, 2, 0)
     with scope("cols1_relay"):
@@ -425,6 +460,8 @@
             column_relay(1, t)
     with scope("ring1_2b"):
         ring_relay(1, 2, 1)
+    with scope("first1"):
+        first_direction(2)
     with scope("cols1_finish"):
         for t in range(2):
             sl_b[t] = column_finish(1, t)
@@ -436,53 +473,63 @@
             return c
 
         lax.fori_loop(0, VARS, twice, 0)
-    with scope("first1"):
-        first_direction(1)
     with scope("ring1_3"):
         ring_relay(1, 3, 0)
         ring_relay(1, 3, 1)
+    with scope("fwd1"):
+        exchange_all(forward_arrival, 1, "wait_recv")
     with scope("derive1"):
-        time_derivative(1)
+        lax.fori_loop(0, 3, sliding_derivative, 0)
+        exchange_all(back_copy, 1, "start")
+        sig_tem[:, three(tm)] = sig_der[pl.ds(2 * tm, 2)]
     with scope("ring1_4"):
         for t in range(2):
             ring_relay(1, 4, t)
             column_start(2, t)
+    with scope("back2"):
+        exchange_all(back_arrival, 2, "wait_recv")
+
+    def without_slide(v, c):
+        for t in range(2):
+            res_ref[t, v] += tem[t, v] - step_size * tem2[t, v]
+        return c
+
+    with scope("without_slide"):
+        lax.fori_loop(0, VARS, without_slide, 0)
     with scope("cols2_relay"):
         for t in range(2):
             column_relay(2, t)
+    with scope("back1"):
+        exchange_all(back_arrival, 1, "wait_recv")
     with scope("cols2_finish"):
         for t in range(2):
             sl_b[t] = column_finish(2, t) - tw_b[t]
             turn(t)
-    with scope("back1"):
-        for k in range(1, TM):
-            back_arrival(1, k).wait_recv()
 
     def finish(v, c):
         for t in range(2):
-            res_ref[t, v, pl.ds(3, 16, stride=4), :] += slide_term(t, v)
-            total = res_ref[t, v] + tem[1, t, v]
-            res_ref[t, v] = total
-            new_ref[t, v] = ub[1, t, v] - step_size * total
+            late = jnp.concatenate([sig_tem[t, 2 * v], sig_tem[t, 2 * v + 1]], axis=0)
+            res_ref[t, v, pl.ds(3, 16, stride=4), :] += slide_term(t, v) - step_size * late
+            new_ref[t, v] = ub[1, t, v] - step_size * res_ref[t, v]
         return c
 
     with scope("finish"):
         lax.fori_loop(0, VARS, finish, 0)
     with scope("sends"):
+        for kind in range(3):
+            if kind < 2:
+                exchange_all(forward_copy, kind, "wait_send")
+            exchange_all(back_copy, kind, "wait_send")
+            for hop in range(3):
+                for t in range(2):
+                    column_copy(kind, hop, t).wait_send()
         for it in range(ITERS):
-            for k in range(1, TM):
-                forward_copy(it, k).wait_send()
-                back_copy(it, k).wait_send()
             for step in range(1, 5):
                 for t in range(2):
                     for way, part in ring_chunks(step, t):
                         ring_copy(it, step, way, t, part).wait_send()
             for way in range(2):
                 pack_copy(it, way).wait_send()
-        for kind in range(3):
-            for hop in range(3):
-                for t in range(2):
-                    column_copy(kind, hop, t).wait_send()
 
 
 def per_device(conserved_field, face_neighbours, counterpart_group, counterpart_shift, volume_operator, flux_matrix):
@@ -497,12 +544,18 @@
         in_specs=[pl.BlockSpec(memory_space=pl.ANY), vmem, smem, smem, vmem, smem],
         out_specs=(vmem, vmem),
         scratch_shapes=[
-            pltpu.VMEM((ITERS, 2, VARS, NODES, LANES), f32),
+            pltpu.VMEM((3, 2, VARS, NODES, LANES), f32),
             pltpu.VMEM((VARS * NODES, VARS * NODES), bf16),
             pltpu.VMEM((VARS * NODES, VARS * NODES), bf16),
-            pltpu.VMEM((ITERS, TM, 2, VARS, 8, LANES), f32),
-            pltpu.VMEM((ITERS, SAMPLE_COUNT, VARS, 8, LANES), f32),
-            pltpu.VMEM((ITERS, 2, VARS, NODES, LANES), f32),
+            pltpu.VMEM((TM, 2, VARS, 8, LANES), f32),
+            pltpu.VMEM((SAMPLE_COUNT, VARS, 8, LANES), f32),
+            pltpu.VMEM((SAMPLE_COUNT, VARS, 8, LANES), f32),
+            pltpu.VMEM((2, VARS, NODES, LANES), f32),
+            pltpu.VMEM((2, VARS, NODES, LANES), f32),
+            pltpu.VMEM((2, 3 * TM, 8, LANES), f32),
+            pltpu.VMEM((TM, 2, 3, 8, LANES), f32),
+            pltpu.VMEM((SAMPLE_COUNT, 3, 8, LANES), f32),
+            pltpu.VMEM((2, 3 * TM, 8, LANES), f32),
             *[pltpu.VMEM((Z, VARS, 16, LANES), f32)] * 4,
             *[pltpu.VMEM((Q, VARS, 16, LANES), f32)] * 6,
             pltpu.VMEM((ITERS, 2, 16, LANES), f32),
@@ -513,8 +566,8 @@
             pltpu.VMEM((2, VARS, 16, LANES), f32),
             pltpu.VMEM((2, VARS, 16, LANES), f32),
             dma,
-            dma((ITERS, TM)), dma((ITERS, TM)),
-            dma((ITERS, TM)), dma((ITERS, TM)),
+            dma((2, 7)), dma((2, 7)),
+            dma((3, 7)), dma((3, 7)),
             dma((ITERS, 16 * PARTS)), dma((ITERS, 16 * PARTS)),
             dma((3, 6)), dma((3, 6)),
             dma((ITERS, 2)), dma((ITERS, 2)),

time: 71.1 us -> 69.6 us (0.979)
  Pallas kernels: 64.5 us -> 63 us
    pallas_call x1, Pallas kernels: 64.5 us -> 63 us  [per_device(): pl.pallas_call(kernel, out_shape=(state, state), in_specs=[pl.BlockSpec(m...]
where the time goes in v3:
time: 69.6 us; the launch traced here: 69.3 us
  Pallas kernels  63 us (91%)
  local copies, waits for them, and re-layouts  5.64 us (8%)
    pallas_call x1, Pallas kernels, per_device(): pl.pallas_call(kernel, out_shape=(state, state), in_specs=[pl.BlockSpec(m...  63 us
    unnamed x14, local copies, waits for them, and re-layouts  5.64 us

profile of v3, /device:TPU:1, one launch (start us, length us, event | category | flops | bytes accessed | tf_op | source)
XLA Modules:
  0.0 69.3 jit_solution(15004569659306545347)
XLA Ops:
  0.6 0.0 copy-start.4
  0.6 0.0 copy-start.3
  0.7 0.6 copy-done.4
  1.3 0.0 copy-done.3
  1.3 0.0 copy-start
  1.3 1.1 %copy-done = f32[2,10,64,128]{3,2,1,0:T(8,128)S(1)} copy-done((f32[2,10,64,128]{3,2,1,0:T(8,128)S(1)}, f32[2,10,64,128]{3,2,1,0:T(8,128)}, u32[]{:S(2)}) %copy-start) | copy-done | bytes 655384
  2.4 0.0 copy-start.1
  2.4 0.8 %copy-done.1 = f32[2,64,64]{2,1,0:T(8,128)S(1)} copy-done((f32[2,64,64]{2,1,0:T(8,128)S(1)}, f32[2,64,64]{2,1,0:T(8,128)}, u32[]{:S(2)}) %copy-start.1) | copy-done | bytes 32792
  3.3 0.0 copy-start.2
  3.3 0.7 %copy-done.2 = f32[2,10,10]{2,0,1:T(2,128)S(1)} copy-done((f32[2,10,10]{2,0,1:T(2,128)S(1)}, f32[2,10,10]{2,0,1:T(2,128)}, u32[]{:S(2)}) %copy-start.2) | copy-done | bytes 824
  4.0 0.0 copy-start.5
  4.0 0.7 copy-done.5
  4.6 63.0 %iterations.1 = (f32[2,10,64,128]{3,2,1,0:T(8,128)S(1)}, f32[2,10,64,128]{3,2,1,0:T(8,128)S(1)}) custom-call(f32[2,10,64,128]{3,2,1,0:T(8,128)S(1)} %copy-done, s32[2,128]{1,0:T(2,128)S(1)} %copy-done.3, s32[2]{0:T(128)S(1)} %copy-done.4, s32[2]{0:T(128)S(1)} %copy-done.5, f32[2,64,64]{2,1,0:T(8,128)S(1)} %copy-done.1, f32[10,2,10]{2,1,0:T(2,128)S(1)} %bitcast.1), custom_call_target="tpu_custom_call" | custom-call | tf_op jit(solution)/shard_map/iterations/pallas_call | solution.py:541
  67.7 0.8 %copy.10 = f32[2,10,64,128]{3,2,1,0:T(8,128)} copy(f32[2,10,64,128]{3,2,1,0:T(8,128)S(1)} %get-tuple-element.4) | data formatting | bytes 1310720
  68.5 0.8 %copy.11 = f32[2,10,64,128]{3,2,1,0:T(8,128)} copy(f32[2,10,64,128]{3,2,1,0:T(8,128)S(1)} %get-tuple-element.5) | data formatting | bytes 1310720
Async XLA Ops:
  0.6 0.7 copy-start.4
  0.6 0.7 copy-start.3
  1.3 1.1 %copy-start = (f32[2,10,64,128]{3,2,1,0:T(8,128)S(1)}, f32[2,10,64,128]{3,2,1,0:T(8,128)}, u32[]{:S(2)}) copy-start(f32[2,10,64,128]{3,2,1,0:T(8,128)} %u_ref.1) | copy-start | bytes 1966084
  2.4 0.8 %copy-start.1 = (f32[2,64,64]{2,1,0:T(8,128)S(1)}, f32[2,64,64]{2,1,0:T(8,128)}, u32[]{:S(2)}) copy-start(f32[2,64,64]{2,1,0:T(8,128)} %vol_ref.1) | copy-start | bytes 98308
  3.3 0.7 %copy-start.2 = (f32[2,10,10]{2,0,1:T(2,128)S(1)}, f32[2,10,10]{2,0,1:T(2,128)}, u32[]{:S(2)}) copy-start(f32[2,10,10]{2,0,1:T(2,128)} %param.11) | copy-start | bytes 2404
  4.0 0.7 copy-start.5

commit v4 on v3

--- a/solution.py
+++ b/solution.py
@@ -42,6 +42,25 @@
     return weights
 
 
+def spectral_squares():
+    first = [0.0] + spectral_weights() + [0.0]
+    full = first + [-first[SAMPLE_COUNT - m] for m in range(SAMPLE_COUNT // 2 + 1, SAMPLE_COUNT)]
+    return [
+        sum(full[j] * full[(m - j) % SAMPLE_COUNT] for j in range(SAMPLE_COUNT))
+        for m in range(SAMPLE_COUNT // 2 + 1)
+    ]
+
+
+def slide_place(v, h):
+    index = 2 * v + h
+    return index // 5, index % 5
+
+
+def other_place(v, c, h):
+    index = 6 * v + 2 * c + h
+    return index // 15, 5 + index % 15
+
+
 def pick(index, values):
     out = jnp.float32(values[0])
     for k in range(1, len(values)):
@@ -50,9 +69,9 @@
 
 
 def kernel(
-    u_ref, fn_ref, group_ref, shift_ref, vol_ref, flux_ref,
-    new_ref, res_ref,
-    ub, a_hi, a_lo, gat, der, der2, tem, tem2, sig, sig_gat, sig_der, sig_tem, ring_00, ring_01, ring_10, ring_11, cols_00, cols_01, cols_10, cols_11, cols_20, cols_21,
+    u_hbm, fn_hbm, group_hbm, shift_hbm, vol_hbm, flux_hbm,
+    new_ref, res_ref, fn_ref, group_ref, shift_ref, vol_ref, flux_ref,
+    ub, a_hi, a_lo, up, gat, dt, dt2, tem, tem2, sig, sig_gat, sig_dt, sig_tem, ring_00, ring_01, ring_10, ring_11, cols_00, cols_01, cols_10, cols_11, cols_20, cols_21,
     packs, packed, side, lo_b, up_b, sl_b, tw_b, in_sem, fs, fr, bs, br, zs, zr, cs, cr, ps, pr,
 ):
     ring = ((ring_00, ring_01), (ring_10, ring_11))
@@ -61,6 +80,8 @@
     sp = lax.axis_index("space")
     z = sp // Q
     q = sp % Q
+    y = tm // 2
+    side_x = tm % 2
 
     def space_of(zz, qq):
         return zz * Q + qq
@@ -72,8 +93,14 @@
     after = (sp + 1) % SP
     before = (sp + SP - 1) % SP
 
-    load = pltpu.make_async_copy(u_ref, ub.at[0], in_sem)
-    load.start()
+    loads = [
+        pltpu.make_async_copy(source, target, in_sem.at[k])
+        for k, (source, target) in enumerate((
+            (u_hbm, ub.at[0]), (flux_hbm, flux_ref), (vol_hbm, vol_ref),
+            (fn_hbm, fn_ref), (group_hbm, group_ref), (shift_hbm, shift_ref)))
+    ]
+    for load in loads:
+        load.start()
 
     barrier = pltpu.get_barrier_semaphore()
     for k in range(1, TM):
@@ -81,7 +108,8 @@
     for other in (z_up, z_dn, mate, cross, after, before):
         pl.semaphore_signal(barrier, inc=1, device_id={"space": other}, device_id_type=MESH)
     with jax.named_scope("entry"):
-        load.wait()
+        for load in loads:
+            load.wait()
         pl.semaphore_wait(barrier, TM - 1 + 6)
 
     lane16 = lax.broadcasted_iota(jnp.int32, (16, LANES), 1)
@@ -90,54 +118,66 @@
     ahead_gap = jnp.bitwise_and(fn_ref[1:2, :] - gidx, SP * LANES - 1)
 
     weights = spectral_weights()
+    squares = spectral_squares()
     cosines = [math.cos(2.0 * math.pi * k / SAMPLE_COUNT) for k in range(SAMPLE_COUNT)]
     sines = [math.sin(2.0 * math.pi * k / SAMPLE_COUNT) for k in range(SAMPLE_COUNT)]
 
-    def rows_of(index):
-        return pl.ds(pl.multiple_of(index * 8, 8), 8)
+    OUT = ((0, 5), (5, 5), (10, 10))
+    BACK = ((0, 5), (5, 15), (0, 20))
 
     def peer_at(k, sign):
         dy, dx = MOVES[k]
-        return ((tm // 2 + sign * dy + 4) % 4) * 2 + (tm % 2 + dx) % 2
-
-    def three(index):
-        return pl.ds(3 * index, 3)
-
-    def forward_copy(kind, k):
-        peer = peer_at(k, 1)
-        source = ub.at[0, :, :, rows_of(peer), :] if kind == 0 else sig.at[:, three(peer)]
-        target = gat.at[tm] if kind == 0 else sig_gat.at[tm]
+        row = (y + sign * dy + 4) % 4
+        return row, row * 2 + (side_x + dx) % 2
+
+    def out_refs(kind, row, place):
+        if kind == 3:
+            return sig.at[:, pl.ds(5 * row, 5)], sig_gat.at[place]
+        tiles = pl.ds(*OUT[kind])
+        return up.at[:, row, tiles], gat.at[place, :, tiles]
+
+    def back_refs(kind, row, place):
+        if kind == 3:
+            return sig_dt.at[row], sig_tem.at[:, pl.ds(5 * place, 5)]
+        tiles = pl.ds(*BACK[kind])
+        source, target = ((dt, tem), (dt, tem), (dt2, tem2))[kind]
+        return source.at[row, :, tiles], target.at[:, place, tiles]
+
+    def out_copy(kind, k):
+        row, peer = peer_at(k, 1)
+        source, target = out_refs(kind, row, tm)
         return pltpu.make_async_remote_copy(
             src_ref=source, dst_ref=target, send_sem=fs.at[kind, k], recv_sem=fr.at[kind, k],
             device_id={"tm": peer}, device_id_type=MESH)
 
-    def forward_arrival(kind, k):
-        peer = peer_at(k, -1)
-        source = ub.at[0, :, :, rows_of(peer), :] if kind == 0 else sig.at[:, three(peer)]
-        target = gat.at[peer] if kind == 0 else sig_gat.at[peer]
+    def out_arrival(kind, k):
+        row, peer = peer_at(k, -1)
+        source, target = out_refs(kind, row, peer)
         return pltpu.make_async_remote_copy(
             src_ref=source, dst_ref=target, send_sem=fs.at[kind, k], recv_sem=fr.at[kind, k],
             device_id={"tm": peer}, device_id_type=MESH)
 
-    def back_refs(kind, peer, place):
-        source = (der, sig_der, der2)[kind].at[pl.ds(2 * peer, 2)]
-        if kind == 1:
-            return source, sig_tem.at[:, three(place)]
-        return source, (tem, None, tem2)[kind].at[:, :, rows_of(place), :]
-
     def back_copy(kind, k):
-        peer = peer_at(k, 1)
-        source, target = back_refs(kind, peer, tm)
-        return pltpu.make_async_remote_copy(
-            src_ref=source, dst_ref=target, send_sem=bs.at[kind, k], recv_sem=br.at[kind, k],
+        row, peer = peer_at(k, 1)
+        source, target = back_refs(kind, row, y)
+        return pltpu.make_async_remote_copy(
+            src_ref=source, dst_ref=target, send_sem=bs.at[kind, k - 4], recv_sem=br.at[kind, k - 4],
             device_id={"tm": peer}, device_id_type=MESH)
 
     def back_arrival(kind, k):
-        peer = peer_at(k, -1)
-        source, target = back_refs(kind, peer, peer)
-        return pltpu.make_async_remote_copy(
-            src_ref=source, dst_ref=target, send_sem=bs.at[kind, k], recv_sem=br.at[kind, k],
+        row, peer = peer_at(k, -1)
+        source, target = back_refs(kind, row, row)
+        return pltpu.make_async_remote_copy(
+            src_ref=source, dst_ref=target, send_sem=bs.at[kind, k - 4], recv_sem=br.at[kind, k - 4],
             device_id={"tm": peer}, device_id_type=MESH)
+
+    def out_all(make, kind, method):
+        for k in range(7):
+            getattr(make(kind, k), method)()
+
+    def back_all(make, kind, method):
+        for k in range(4, 7):
+            getattr(make(kind, k), method)()
 
     def ring_slot(step, way, t, part):
         return (((step - 1) * 2 + way) * 2 + t) * PARTS + part
@@ -292,34 +332,48 @@
 
         lax.fori_loop(0, VARS, first_faces, 0)
 
-    def spectral(load_at, store_at):
-        x = [load_at(t) for t in range(SAMPLE_COUNT)]
-        half = SAMPLE_COUNT // 2
-        for t in range(half):
+    half = SAMPLE_COUNT // 2
+
+    def spectral(source, first, second, i):
+        x = [source[(side_x + r // 2) % TM, r % 2, i] for r in range(SAMPLE_COUNT)]
+        for r in (0, 1, 4, 5):
             near = opposite = None
             for m in range(1, half):
-                diff = x[(t + m) % SAMPLE_COUNT] - x[(t - m) % SAMPLE_COUNT]
+                diff = x[(r + m) % SAMPLE_COUNT] - x[(r - m) % SAMPLE_COUNT]
                 one, two = jnp.float32(weights[m - 1]) * diff, jnp.float32(-weights[half - m - 1]) * diff
                 near = one if near is None else near + one
                 opposite = two if opposite is None else opposite + two
-            store_at(t, near)
-            store_at(t + half, opposite)
-
-    def first_derivative(v, c):
-        spectral(lambda t: gat[t // 2, t % 2, v], lambda t, value: der.__setitem__((t, v), value))
+            first[r // 4, r % 2, i] = near
+            first[r // 4 + 2, r % 2, i] = opposite
+            if second is None:
+                continue
+            zero, eight = jnp.float32(squares[0]), jnp.float32(squares[half])
+            near = zero * x[r] + eight * x[r + half]
+            opposite = eight * x[r] + zero * x[r + half]
+            for m in range(1, half):
+                both = x[(r + m) % SAMPLE_COUNT] + x[(r - m) % SAMPLE_COUNT]
+                near = near + jnp.float32(squares[m]) * both
+                opposite = opposite + jnp.float32(squares[half - m]) * both
+            second[r // 4, r % 2, i] = near
+            second[r // 4 + 2, r % 2, i] = opposite
+
+    def derive_state(i, c):
+        spectral(gat, dt, dt2, i)
         return c
 
-    def second_derivative(v, c):
-        spectral(lambda t: der[t, v], lambda t, value: der2.__setitem__((t, v), value))
+    def derive_term(i, c):
+        spectral(sig_gat, sig_dt, None, i)
         return c
 
-    def sliding_derivative(i, c):
-        spectral(lambda t: sig_gat[t // 2, t % 2, i], lambda t, value: sig_der.__setitem__((t, i), value))
-        return c
-
-    def exchange_all(make, kind, method):
-        for k in range(len(MOVES)):
-            getattr(make(kind, k), method)()
+    def rows(c):
+        return pl.ds(c, 16, stride=4)
+
+    def tiles_of(buffer, t, v, c):
+        places = [slide_place(v, h) if c == 3 else other_place(v, c, h) for h in range(2)]
+        return jnp.concatenate([buffer[t, j, i] for j, i in places], axis=0)
+
+    def term_tiles(t, v):
+        return jnp.concatenate([sig_tem[t, 2 * v], sig_tem[t, 2 * v + 1]], axis=0)
 
     def offset_of(kind, t):
         group, shift = group_ref[t], shift_ref[t]
@@ -372,12 +426,24 @@
 
     with scope("start0"):
         for t in range(2):
-            ring[0][t][z] = ub[0, t, :, pl.ds(3, 16, stride=4), :]
+            for v in range(VARS):
+                points = ub[0, t, v, rows(3), :]
+                ring[0][t][z, v] = points
+                for h in range(2):
+                    j, i = slide_place(v, h)
+                    up[t, j, i] = points[8 * h:8 * h + 8]
             ring_start(0, t)
+        out_all(out_copy, 0, "start")
         pack_traces(0)
-        exchange_all(forward_copy, 0, "start")
-        gat[tm] = ub[0, :, :, rows_of(tm), :]
-        sig[:, pl.ds(2 * VARS, 4)] = jnp.zeros((2, 4, 8, LANES), jnp.float32)
+        for t in range(2):
+            for v in range(VARS):
+                for c in range(3):
+                    points = ub[0, t, v, rows(c), :]
+                    for h in range(2):
+                        j, i = other_place(v, c, h)
+                        up[t, j, i] = points[8 * h:8 * h + 8]
+        out_all(out_copy, 1, "start")
+        gat[tm] = up[:, y]
     with scope("matrix"):
         build_matrix()
     with scope("volume0"):
@@ -385,83 +451,107 @@
     with scope("ring0_1"):
         ring_relay(0, 1, 0)
         ring_relay(0, 1, 1)
-    with scope("ring0_2a"):
+    with scope("out_slide"):
+        out_all(out_arrival, 0, "wait_recv")
+    with scope("derive_slide"):
+        lax.fori_loop(0, 5, derive_state, 0)
+        back_all(back_copy, 0, "start")
+        out_all(out_copy, 2, "start")
+        tem[:, y, pl.ds(0, 5)] = dt[y, :, pl.ds(0, 5)]
+    with scope("ring0_2"):
         ring_relay(0, 2, 0)
-    with scope("fwd0"):
-        exchange_all(forward_arrival, 0, "wait_recv")
-    with scope("derive0"):
-        lax.fori_loop(0, VARS, first_derivative, 0)
-        exchange_all(back_copy, 0, "start")
-        tem[:, :, rows_of(tm), :] = der[pl.ds(2 * tm, 2)]
-    with scope("ring0_2b"):
         ring_relay(0, 2, 1)
     with scope("first0"):
         first_direction(0)
     with scope("ring0_3"):
         ring_relay(0, 3, 0)
-    with scope("derive2"):
-        lax.fori_loop(0, VARS, second_derivative, 0)
-        tem2[:, :, rows_of(tm), :] = der2[pl.ds(2 * tm, 2)]
+    with scope("back_slide"):
+        back_all(back_arrival, 0, "wait_recv")
+    with scope("w"):
+        for t in range(2):
+            for v in range(VARS):
+                rest = res_ref[t, v, rows(3), :] + tiles_of(tem, t, v, 3)
+                ring[1][t][z, v] = ub[0, t, v, rows(3), :] - step_size * rest
     with scope("ring0_3b"):
         ring_relay(0, 3, 1)
+        for t in range(2):
+            ring_start(1, t)
     with scope("ring0_4"):
         for t in range(2):
             ring_relay(0, 4, t)
             column_start(0, t)
-    with scope("back0"):
-        exchange_all(back_arrival, 0, "wait_recv")
-
-    def partial_state(v, c):
-        for t in range(2):
-            ub[1, t, v] = ub[0, t, v] - step_size * (res_ref[t, v] + tem[t, v])
-        return c
-
-    with scope("w"):
-        lax.fori_loop(0, VARS, partial_state, 0)
-        for t in range(2):
-            ring[1][t][z] = ub[1, t, :, pl.ds(3, 16, stride=4), :]
-            ring_start(1, t)
     with scope("cols1_start"):
         for t in range(2):
             column_start(1, t)
-        exchange_all(back_copy, 2, "start")
     with scope("ring1_1a"):
         ring_relay(1, 1, 0)
-    with scope("cols0_relay"):
-        for t in range(2):
-            column_relay(0, t)
+    with scope("out_rest"):
+        out_all(out_arrival, 1, "wait_recv")
+        out_all(out_arrival, 2, "wait_recv")
+    with scope("derive_rest"):
+        lax.fori_loop(5, 20, derive_state, 0)
+        back_all(back_copy, 1, "start")
+        back_all(back_copy, 2, "start")
+        tem[:, y, pl.ds(5, 15)] = dt[y, :, pl.ds(5, 15)]
+        tem2[:, y] = dt2[y]
     with scope("ring1_1b"):
         ring_relay(1, 1, 1)
+    with scope("cols0_relay"):
+        for t in range(2):
+            column_relay(0, t)
+    with scope("ring1_2a"):
+        ring_relay(1, 2, 0)
     with scope("cols0_finish"):
         for t in range(2):
             sl_b[t] = column_finish(0, t)
             turn(t)
 
-    def next_state(v, c):
+    def sliding_term(v, c):
         for t in range(2):
             term = slide_term(t, v)
             sig[t, 2 * v] = term[0:8]
             sig[t, 2 * v + 1] = term[8:16]
-            ub[1, t, v, pl.ds(3, 16, stride=4), :] += -step_size * term
-            ub[2, t, v] = ub[1, t, v] - step_size * tem[t, v]
         return c
 
+    with scope("sigma"):
+        lax.fori_loop(0, VARS, sliding_term, 0)
+        out_all(out_copy, 3, "start")
+        sig_gat[tm] = sig[:, pl.ds(5 * y, 5)]
+    with scope("ring1_2b"):
+        ring_relay(1, 2, 1)
+    with scope("cols1_relay"):
+        for t in range(2):
+            column_relay(1, t)
+    with scope("back_rest"):
+        back_all(back_arrival, 1, "wait_recv")
     with scope("u1"):
-        lax.fori_loop(0, VARS, next_state, 0)
-        exchange_all(forward_copy, 1, "start")
+        for t in range(2):
+            for v in range(VARS):
+                for c in range(4):
+                    late = tiles_of(tem, t, v, c)
+                    rest = res_ref[t, v, rows(c), :] + late
+                    if c == 3:
+                        rest = rest + jnp.concatenate([sig[t, 2 * v], sig[t, 2 * v + 1]], axis=0)
+                    state = ub[0, t, v, rows(c), :] - step_size * rest
+                    ub[1, t, v, rows(c), :] = state
+                    ub[2, t, v, rows(c), :] = state - step_size * late
         pack_traces(2)
-        sig_gat[tm] = sig[:, three(tm)]
+    with scope("ring1_3a"):
+        ring_relay(1, 3, 0)
     with scope("volume1"):
         volume_part(2)
-    with scope("ring1_2"):
-        ring_relay(1, 2, 0)
-    with scope("cols1_relay"):
-        for t in range(2):
-            column_relay(1, t)
-    with scope("ring1_2b"):
-        ring_relay(1, 2, 1)
-    with scope("first1"):
-        first_direction(2)
+    with scope("ring1_3b"):
+        ring_relay(1, 3, 1)
+    with scope("out_term"):
+        out_all(out_arrival, 3, "wait_recv")
+    with scope("derive_term"):
+        lax.fori_loop(0, 5, derive_term, 0)
+        back_all(back_copy, 3, "start")
+        sig_tem[:, pl.ds(5 * y, 5)] = sig_dt[y]
+    with scope("ring1_4"):
+        for t in range(2):
+            ring_relay(1, 4, t)
+            column_start(2, t)
     with scope("cols1_finish"):
         for t in range(2):
             sl_b[t] = column_finish(1, t)
@@ -473,34 +563,25 @@
             return c
 
         lax.fori_loop(0, VARS, twice, 0)
-    with scope("ring1_3"):
-        ring_relay(1, 3, 0)
-        ring_relay(1, 3, 1)
-    with scope("fwd1"):
-        exchange_all(forward_arrival, 1, "wait_recv")
-    with scope("derive1"):
-        lax.fori_loop(0, 3, sliding_derivative, 0)
-        exchange_all(back_copy, 1, "start")
-        sig_tem[:, three(tm)] = sig_der[pl.ds(2 * tm, 2)]
-    with scope("ring1_4"):
-        for t in range(2):
-            ring_relay(1, 4, t)
-            column_start(2, t)
-    with scope("back2"):
-        exchange_all(back_arrival, 2, "wait_recv")
-
-    def without_slide(v, c):
-        for t in range(2):
-            res_ref[t, v] += tem[t, v] - step_size * tem2[t, v]
-        return c
-
+    with scope("first1"):
+        first_direction(2)
+    with scope("back_late"):
+        back_all(back_arrival, 2, "wait_recv")
+        back_all(back_arrival, 3, "wait_recv")
     with scope("without_slide"):
-        lax.fori_loop(0, VARS, without_slide, 0)
+        for t in range(2):
+            for v in range(VARS):
+                for c in range(4):
+                    late = tiles_of(tem2, t, v, c)
+                    if c == 3:
+                        late = late + term_tiles(t, v)
+                    total = res_ref[t, v, rows(c), :] + (tiles_of(tem, t, v, c) - step_size * late)
+                    res_ref[t, v, rows(c), :] = total
+                    if c < 3:
+                        new_ref[t, v, rows(c), :] = ub[1, t, v, rows(c), :] - step_size * total
     with scope("cols2_relay"):
         for t in range(2):
             column_relay(2, t)
-    with scope("back1"):
-        exchange_all(back_arrival, 1, "wait_recv")
     with scope("cols2_finish"):
         for t in range(2):
             sl_b[t] = column_finish(2, t) - tw_b[t]
@@ -508,18 +589,18 @@
 
     def finish(v, c):
         for t in range(2):
-            late = jnp.concatenate([sig_tem[t, 2 * v], sig_tem[t, 2 * v + 1]], axis=0)
-            res_ref[t, v, pl.ds(3, 16, stride=4), :] += slide_term(t, v) - step_size * late
-            new_ref[t, v] = ub[1, t, v] - step_size * res_ref[t, v]
+            total = res_ref[t, v, rows(3), :] + slide_term(t, v)
+            res_ref[t, v, rows(3), :] = total
+            new_ref[t, v, rows(3), :] = ub[1, t, v, rows(3), :] - step_size * total
         return c
 
     with scope("finish"):
         lax.fori_loop(0, VARS, finish, 0)
     with scope("sends"):
+        for kind in range(4):
+            out_all(out_copy, kind, "wait_send")
+            back_all(back_copy, kind, "wait_send")
         for kind in range(3):
-            if kind < 2:
-                exchange_all(forward_copy, kind, "wait_send")
-            exchange_all(back_copy, kind, "wait_send")
             for hop in range(3):
                 for t in range(2):
                     column_copy(kind, hop, t).wait_send()
@@ -535,27 +616,32 @@
 def per_device(conserved_field, face_neighbours, counterpart_group, counterpart_shift, volume_operator, flux_matrix):
     state = jax.ShapeDtypeStruct(conserved_field.shape, jnp.float32)
     vmem = pl.BlockSpec(memory_space=pltpu.VMEM)
-    smem = pl.BlockSpec(memory_space=pltpu.SMEM)
     f32, bf16 = jnp.float32, jnp.bfloat16
     dma = pltpu.SemaphoreType.DMA
     return pl.pallas_call(
         kernel,
         out_shape=(state, state),
-        in_specs=[pl.BlockSpec(memory_space=pl.ANY), vmem, smem, smem, vmem, smem],
+        in_specs=[pl.BlockSpec(memory_space=pltpu.HBM)] * 6,
         out_specs=(vmem, vmem),
         scratch_shapes=[
+            pltpu.VMEM((2, LANES), jnp.int32),
+            pltpu.SMEM((2,), jnp.int32),
+            pltpu.SMEM((2,), jnp.int32),
+            pltpu.VMEM((2, NODES, NODES), f32),
+            pltpu.SMEM((VARS, 2, VARS), f32),
             pltpu.VMEM((3, 2, VARS, NODES, LANES), f32),
             pltpu.VMEM((VARS * NODES, VARS * NODES), bf16),
             pltpu.VMEM((VARS * NODES, VARS * NODES), bf16),
-            pltpu.VMEM((TM, 2, VARS, 8, LANES), f32),
-            pltpu.VMEM((SAMPLE_COUNT, VARS, 8, LANES), f32),
-            pltpu.VMEM((SAMPLE_COUNT, VARS, 8, LANES), f32),
-            pltpu.VMEM((2, VARS, NODES, LANES), f32),
-            pltpu.VMEM((2, VARS, NODES, LANES), f32),
-            pltpu.VMEM((2, 3 * TM, 8, LANES), f32),
-            pltpu.VMEM((TM, 2, 3, 8, LANES), f32),
-            pltpu.VMEM((SAMPLE_COUNT, 3, 8, LANES), f32),
-            pltpu.VMEM((2, 3 * TM, 8, LANES), f32),
+            pltpu.VMEM((2, 4, 20, 8, LANES), f32),
+            pltpu.VMEM((TM, 2, 20, 8, LANES), f32),
+            pltpu.VMEM((4, 2, 20, 8, LANES), f32),
+            pltpu.VMEM((4, 2, 20, 8, LANES), f32),
+            pltpu.VMEM((2, 4, 20, 8, LANES), f32),
+            pltpu.VMEM((2, 4, 20, 8, LANES), f32),
+            pltpu.VMEM((2, 20, 8, LANES), f32),
+            pltpu.VMEM((TM, 2, 5, 8, LANES), f32),
+            pltpu.VMEM((4, 2, 5, 8, LANES), f32),
+            pltpu.VMEM((2, 20, 8, LANES), f32),
             *[pltpu.VMEM((Z, VARS, 16, LANES), f32)] * 4,
             *[pltpu.VMEM((Q, VARS, 16, LANES), f32)] * 6,
             pltpu.VMEM((ITERS, 2, 16, LANES), f32),
@@ -565,9 +651,9 @@
             pltpu.VMEM((2, VARS, 16, LANES), f32),
             pltpu.VMEM((2, VARS, 16, LANES), f32),
             pltpu.VMEM((2, VARS, 16, LANES), f32),
-            dma,
-            dma((2, 7)), dma((2, 7)),
-            dma((3, 7)), dma((3, 7)),
+            dma((6,)),
+            dma((4, 7)), dma((4, 7)),
+            dma((4, 3)), dma((4, 3)),
             dma((ITERS, 16 * PARTS)), dma((ITERS, 16 * PARTS)),
             dma((3, 6)), dma((3, 6)),
             dma((ITERS, 2)), dma((ITERS, 2)),

time: 69.6 us -> 64.5 us (0.927)
  Pallas kernels: 63 us -> 57.9 us
    pallas_call x1, Pallas kernels: 63 us -> 57.9 us  [per_device(): pl.pallas_call(kernel, out_shape=(state, state), in_specs=[pl.BlockSpec(m...]
where the time goes in v4:
time: 64.5 us; the launch traced here: 64.2 us
  Pallas kernels  57.9 us (90%)
  local copies, waits for them, and re-layouts  5.64 us (9%)
  between operations  0.66 us (1%)
    pallas_call x1, Pallas kernels, per_device(): pl.pallas_call(kernel, out_shape=(state, state), in_specs=[pl.BlockSpec(m...  57.9 us
    unnamed x14, local copies, waits for them, and re-layouts  5.64 us

profile of v4, /device:TPU:1, one launch (start us, length us, event | category | flops | bytes accessed | tf_op | source)
XLA Modules:
  0.0 64.2 jit_solution(6640946319994682547)
XLA Ops:
  0.6 0.0 copy-start.4
  0.6 0.0 copy-start.3
  0.7 0.6 copy-done.4
  1.3 0.0 copy-done.3
  1.3 0.0 copy-start
  1.3 1.1 %copy-done = f32[2,10,64,128]{3,2,1,0:T(8,128)S(1)} copy-done((f32[2,10,64,128]{3,2,1,0:T(8,128)S(1)}, f32[2,10,64,128]{3,2,1,0:T(8,128)}, u32[]{:S(2)}) %copy-start) | copy-done | bytes 655384
  2.4 0.0 copy-start.1
  2.4 0.8 %copy-done.1 = f32[2,64,64]{2,1,0:T(8,128)S(1)} copy-done((f32[2,64,64]{2,1,0:T(8,128)S(1)}, f32[2,64,64]{2,1,0:T(8,128)}, u32[]{:S(2)}) %copy-start.1) | copy-done | bytes 32792
  3.3 0.0 copy-start.2
  3.3 0.7 %copy-done.2 = f32[2,10,10]{2,0,1:T(2,128)S(1)} copy-done((f32[2,10,10]{2,0,1:T(2,128)S(1)}, f32[2,10,10]{2,0,1:T(2,128)}, u32[]{:S(2)}) %copy-start.2) | copy-done | bytes 824
  4.0 0.0 copy-start.5
  4.0 0.7 %copy-done.5 = s32[2]{0:T(128)S(1)} copy-done((s32[2]{0:T(128)S(1)}, s32[2]{0:T(128)}, u32[]{:S(2)}) %copy-start.5) | copy-done | bytes 32
  4.6 57.9 %iterations.1 = (f32[2,10,64,128]{3,2,1,0:T(8,128)S(1)}, f32[2,10,64,128]{3,2,1,0:T(8,128)S(1)}) custom-call(f32[2,10,64,128]{3,2,1,0:T(8,128)S(1)} %copy-done, s32[2,128]{1,0:T(2,128)S(1)} %copy-done.3, s32[2]{0:T(128)S(1)} %copy-done.4, s32[2]{0:T(128)S(1)} %copy-done.5, f32[2,64,64]{2,1,0:T(8,128)S(1)} %copy-done.1, f32[10,2,10]{2,1,0:T(2,128)S(1)} %bitcast.1), custom_call_target="tpu_custom_call" | custom-call | tf_op jit(solution)/shard_map/iterations/pallas_call | solution.py:621
  62.5 0.8 %copy.10 = f32[2,10,64,128]{3,2,1,0:T(8,128)} copy(f32[2,10,64,128]{3,2,1,0:T(8,128)S(1)} %get-tuple-element.4) | data formatting | bytes 1310720
  63.4 0.8 %copy.11 = f32[2,10,64,128]{3,2,1,0:T(8,128)} copy(f32[2,10,64,128]{3,2,1,0:T(8,128)S(1)} %get-tuple-element.5) | data formatting | bytes 1310720
Async XLA Ops:
  0.6 0.7 %copy-start.4 = (s32[2]{0:T(128)S(1)}, s32[2]{0:T(128)}, u32[]{:S(2)}) copy-start(s32[2]{0:T(128)} %group_hbm.1) | copy-start | bytes 28
  0.6 0.7 %copy-start.3 = (s32[2,128]{1,0:T(2,128)S(1)}, s32[2,128]{1,0:T(2,128)}, u32[]{:S(2)}) copy-start(s32[2,128]{1,0:T(2,128)} %fn_hbm.1) | copy-start | bytes 3076
  1.3 1.1 %copy-start = (f32[2,10,64,128]{3,2,1,0:T(8,128)S(1)}, f32[2,10,64,128]{3,2,1,0:T(8,128)}, u32[]{:S(2)}) copy-start(f32[2,10,64,128]{3,2,1,0:T(8,128)} %u_hbm.1) | copy-start | bytes 1966084
  2.4 0.8 %copy-start.1 = (f32[2,64,64]{2,1,0:T(8,128)S(1)}, f32[2,64,64]{2,1,0:T(8,128)}, u32[]{:S(2)}) copy-start(f32[2,64,64]{2,1,0:T(8,128)} %vol_hbm.1) | copy-start | bytes 98308
  3.3 0.7 %copy-start.2 = (f32[2,10,10]{2,0,1:T(2,128)S(1)}, f32[2,10,10]{2,0,1:T(2,128)}, u32[]{:S(2)}) copy-start(f32[2,10,10]{2,0,1:T(2,128)} %param.11) | copy-start | bytes 2404
  4.0 0.7 %copy-start.5 = (s32[2]{0:T(128)S(1)}, s32[2]{0:T(128)}, u32[]{:S(2)}) copy-start(s32[2]{0:T(128)} %shift_hbm.1) | copy-start | bytes 28

commit v5 on v4

--- a/solution.py
+++ b/solution.py
@@ -72,7 +72,7 @@
     u_hbm, fn_hbm, group_hbm, shift_hbm, vol_hbm, flux_hbm,
     new_ref, res_ref, fn_ref, group_ref, shift_ref, vol_ref, flux_ref,
     ub, a_hi, a_lo, up, gat, dt, dt2, tem, tem2, sig, sig_gat, sig_dt, sig_tem, ring_00, ring_01, ring_10, ring_11, cols_00, cols_01, cols_10, cols_11, cols_20, cols_21,
-    packs, packed, side, lo_b, up_b, sl_b, tw_b, in_sem, fs, fr, bs, br, zs, zr, cs, cr, ps, pr,
+    packs, packed, side, lo_b, up_b, sl_b, tw_b, in_sem, fs, fr, bs, br, zs, zr, cs, cr, ps, pr, xs, xr,
 ):
     ring = ((ring_00, ring_01), (ring_10, ring_11))
     cols = ((cols_00, cols_01), (cols_10, cols_11), (cols_20, cols_21))
@@ -123,7 +123,7 @@
     sines = [math.sin(2.0 * math.pi * k / SAMPLE_COUNT) for k in range(SAMPLE_COUNT)]
 
     OUT = ((0, 5), (5, 5), (10, 10))
-    BACK = ((0, 5), (5, 15), (0, 20))
+    BACK = ((0, 5), (5, 5), (10, 10), None, (0, 5), (5, 5), (10, 10))
 
     def peer_at(k, sign):
         dy, dx = MOVES[k]
@@ -140,7 +140,7 @@
         if kind == 3:
             return sig_dt.at[row], sig_tem.at[:, pl.ds(5 * place, 5)]
         tiles = pl.ds(*BACK[kind])
-        source, target = ((dt, tem), (dt, tem), (dt2, tem2))[kind]
+        source, target = (dt2, tem2) if kind > 3 else (dt, tem)
         return source.at[row, :, tiles], target.at[:, place, tiles]
 
     def out_copy(kind, k):
@@ -172,8 +172,26 @@
             device_id={"tm": peer}, device_id_type=MESH)
 
     def out_all(make, kind, method):
-        for k in range(7):
+        for k in range(7) if kind in (0, 3) else range(4, 7):
             getattr(make(kind, k), method)()
+
+    def pass_on(kind, k, side):
+        row = (y if k == 7 else peer_at(k, -1)[0])
+        place = row * 2 + (side_x if side == 0 else 1 - side_x)
+        block = gat.at[place, :, pl.ds(*OUT[kind])]
+        slot = (kind - 1) * 4 + k - 4
+        return pltpu.make_async_remote_copy(
+            src_ref=block, dst_ref=block, send_sem=xs.at[slot], recv_sem=xr.at[slot],
+            device_id={"tm": y * 2 + 1 - side_x}, device_id_type=MESH)
+
+    def relay_points(kind):
+        for k in (5, 6, 4):
+            out_arrival(kind, k).wait_recv()
+            pass_on(kind, k, 0).start()
+
+    def wait_points(kind):
+        for k in (7, 5, 6, 4):
+            pass_on(kind, k, 1).wait_recv()
 
     def back_all(make, kind, method):
         for k in range(4, 7):
@@ -442,8 +460,10 @@
                     for h in range(2):
                         j, i = other_place(v, c, h)
                         up[t, j, i] = points[8 * h:8 * h + 8]
-        out_all(out_copy, 1, "start")
         gat[tm] = up[:, y]
+        for kind in (1, 2):
+            out_all(out_copy, kind, "start")
+            pass_on(kind, 7, 0).start()
     with scope("matrix"):
         build_matrix()
     with scope("volume0"):
@@ -451,20 +471,31 @@
     with scope("ring0_1"):
         ring_relay(0, 1, 0)
         ring_relay(0, 1, 1)
+    with scope("ring0_2a"):
+        ring_relay(0, 2, 0)
     with scope("out_slide"):
         out_all(out_arrival, 0, "wait_recv")
     with scope("derive_slide"):
         lax.fori_loop(0, 5, derive_state, 0)
         back_all(back_copy, 0, "start")
-        out_all(out_copy, 2, "start")
+        back_all(back_copy, 4, "start")
         tem[:, y, pl.ds(0, 5)] = dt[y, :, pl.ds(0, 5)]
-    with scope("ring0_2"):
-        ring_relay(0, 2, 0)
+    with scope("ring0_2b"):
         ring_relay(0, 2, 1)
+    with scope("points1"):
+        relay_points(1)
     with scope("first0"):
         first_direction(0)
     with scope("ring0_3"):
         ring_relay(0, 3, 0)
+    with scope("points2"):
+        relay_points(2)
+    with scope("ring0_3b"):
+        ring_relay(0, 3, 1)
+    with scope("ring0_4"):
+        for t in range(2):
+            ring_relay(0, 4, t)
+            column_start(0, t)
     with scope("back_slide"):
         back_all(back_arrival, 0, "wait_recv")
     with scope("w"):
@@ -472,35 +503,34 @@
             for v in range(VARS):
                 rest = res_ref[t, v, rows(3), :] + tiles_of(tem, t, v, 3)
                 ring[1][t][z, v] = ub[0, t, v, rows(3), :] - step_size * rest
-    with scope("ring0_3b"):
-        ring_relay(0, 3, 1)
-        for t in range(2):
             ring_start(1, t)
-    with scope("ring0_4"):
-        for t in range(2):
-            ring_relay(0, 4, t)
-            column_start(0, t)
     with scope("cols1_start"):
         for t in range(2):
             column_start(1, t)
+    with scope("rest1"):
+        wait_points(1)
+        lax.fori_loop(5, 10, derive_state, 0)
+        back_all(back_copy, 1, "start")
+        back_all(back_copy, 5, "start")
+        tem[:, y, pl.ds(5, 5)] = dt[y, :, pl.ds(5, 5)]
     with scope("ring1_1a"):
         ring_relay(1, 1, 0)
-    with scope("out_rest"):
-        out_all(out_arrival, 1, "wait_recv")
-        out_all(out_arrival, 2, "wait_recv")
-    with scope("derive_rest"):
-        lax.fori_loop(5, 20, derive_state, 0)
-        back_all(back_copy, 1, "start")
+    with scope("rest2"):
+        wait_points(2)
+        lax.fori_loop(10, 20, derive_state, 0)
         back_all(back_copy, 2, "start")
-        tem[:, y, pl.ds(5, 15)] = dt[y, :, pl.ds(5, 15)]
+        back_all(back_copy, 6, "start")
+        tem[:, y, pl.ds(10, 10)] = dt[y, :, pl.ds(10, 10)]
         tem2[:, y] = dt2[y]
     with scope("ring1_1b"):
         ring_relay(1, 1, 1)
-    with scope("cols0_relay"):
-        for t in range(2):
-            column_relay(0, t)
     with scope("ring1_2a"):
         ring_relay(1, 2, 0)
+    with scope("cols0_relay"):
+        for t in range(2):
+            column_relay(0, t)
+    with scope("ring1_2b"):
+        ring_relay(1, 2, 1)
     with scope("cols0_finish"):
         for t in range(2):
             sl_b[t] = column_finish(0, t)
@@ -517,13 +547,14 @@
         lax.fori_loop(0, VARS, sliding_term, 0)
         out_all(out_copy, 3, "start")
         sig_gat[tm] = sig[:, pl.ds(5 * y, 5)]
-    with scope("ring1_2b"):
-        ring_relay(1, 2, 1)
+    with scope("ring1_3a"):
+        ring_relay(1, 3, 0)
     with scope("cols1_relay"):
         for t in range(2):
             column_relay(1, t)
     with scope("back_rest"):
         back_all(back_arrival, 1, "wait_recv")
+        back_all(back_arrival, 2, "wait_recv")
     with scope("u1"):
         for t in range(2):
             for v in range(VARS):
@@ -536,22 +567,20 @@
                     ub[1, t, v, rows(c), :] = state
                     ub[2, t, v, rows(c), :] = state - step_size * late
         pack_traces(2)
-    with scope("ring1_3a"):
-        ring_relay(1, 3, 0)
+    with scope("ring1_3b"):
+        ring_relay(1, 3, 1)
     with scope("volume1"):
         volume_part(2)
-    with scope("ring1_3b"):
-        ring_relay(1, 3, 1)
+    with scope("ring1_4"):
+        for t in range(2):
+            ring_relay(1, 4, t)
+            column_start(2, t)
     with scope("out_term"):
         out_all(out_arrival, 3, "wait_recv")
     with scope("derive_term"):
         lax.fori_loop(0, 5, derive_term, 0)
         back_all(back_copy, 3, "start")
         sig_tem[:, pl.ds(5 * y, 5)] = sig_dt[y]
-    with scope("ring1_4"):
-        for t in range(2):
-            ring_relay(1, 4, t)
-            column_start(2, t)
     with scope("cols1_finish"):
         for t in range(2):
             sl_b[t] = column_finish(1, t)
@@ -565,9 +594,12 @@
         lax.fori_loop(0, VARS, twice, 0)
     with scope("first1"):
         first_direction(2)
+    with scope("cols2_relay"):
+        for t in range(2):
+            column_relay(2, t)
     with scope("back_late"):
-        back_all(back_arrival, 2, "wait_recv")
-        back_all(back_arrival, 3, "wait_recv")
+        for kind in (4, 5, 6, 3):
+            back_all(back_arrival, kind, "wait_recv")
     with scope("without_slide"):
         for t in range(2):
             for v in range(VARS):
@@ -579,9 +611,6 @@
                     res_ref[t, v, rows(c), :] = total
                     if c < 3:
                         new_ref[t, v, rows(c), :] = ub[1, t, v, rows(c), :] - step_size * total
-    with scope("cols2_relay"):
-        for t in range(2):
-            column_relay(2, t)
     with scope("cols2_finish"):
         for t in range(2):
             sl_b[t] = column_finish(2, t) - tw_b[t]
@@ -599,7 +628,11 @@
     with scope("sends"):
         for kind in range(4):
             out_all(out_copy, kind, "wait_send")
+        for kind in range(7):
             back_all(back_copy, kind, "wait_send")
+        for kind in (1, 2):
+            for k in range(4, 8):
+                pass_on(kind, k, 0).wait_send()
         for kind in range(3):
             for hop in range(3):
                 for t in range(2):
@@ -653,13 +686,14 @@
             pltpu.VMEM((2, VARS, 16, LANES), f32),
             dma((6,)),
             dma((4, 7)), dma((4, 7)),
-            dma((4, 3)), dma((4, 3)),
+            dma((7, 3)), dma((7, 3)),
             dma((ITERS, 16 * PARTS)), dma((ITERS, 16 * PARTS)),
             dma((3, 6)), dma((3, 6)),
             dma((ITERS, 2)), dma((ITERS, 2)),
+            dma((8,)), dma((8,)),
         ],
         compiler_params=pltpu.CompilerParams(
-            collective_id=0, has_side_effects=True, vmem_limit_bytes=48 * 1024 * 1024),
+            collective_id=0, has_side_effects=True, vmem_limit_bytes=63 * 1024 * 1024),
         name="iterations",
     )(conserved_field, face_neighbours, counterpart_group, counterpart_shift, volume_operator,
       jnp.transpose(flux_matrix, (1, 0, 2)))

time: 64.5 us -> 58.8 us (0.912)
  Pallas kernels: 57.9 us -> 55.1 us
  local copies, waits for them, and re-layouts: 5.64 us -> 2.89 us
    pallas_call x1, Pallas kernels: 57.9 us -> 55.1 us  [per_device(): pl.pallas_call(kernel, out_shape=(state, state), in_specs=[pl.BlockSpec(m...]
    unnamed x14 -> x4, local copies, waits for them, and re-layouts: 5.64 us -> 2.89 us
where the time goes in v5:
time: 58.8 us; the launch traced here: 58.7 us
  Pallas kernels  55.1 us (94%)
  local copies, waits for them, and re-layouts  2.89 us (5%)
  between operations  0.65 us (1%)
    pallas_call x1, Pallas kernels, per_device(): pl.pallas_call(kernel, out_shape=(state, state), in_specs=[pl.BlockSpec(m...  55.1 us
    unnamed x4, local copies, waits for them, and re-layouts  2.89 us

profile of v5, /device:TPU:1, one launch (start us, length us, event | category | flops | bytes accessed | tf_op | source)
XLA Modules:
  0.0 58.7 jit_solution(12426378642645936459)
XLA Ops:
  0.6 55.1 %iterations.1 = (f32[2,10,64,128]{3,2,1,0:T(8,128)}, f32[2,10,64,128]{3,2,1,0:T(8,128)}) custom-call(f32[2,10,64,128]{3,2,1,0:T(8,128)} %u_hbm.1, s32[2,128]{1,0:T(2,128)} %fn_hbm.1, s32[2]{0:T(128)} %group_hbm.1, s32[2]{0:T(128)} %shift_hbm.1, f32[2,64,64]{2,1,0:T(8,128)} %vol_hbm.1, f32[10,2,10]{2,1,0:T(2,128)} %bitcast.1), custom_call_target="tpu_custom_call" | custom-call | tf_op jit(solution)/shard_map/iterations/pallas_call | solution.py:654
  55.8 0.0 copy-start
  55.8 2.0 %copy.10 = f32[2,10,64,128]{3,2,1,0:T(8,128)} copy(f32[2,10,64,128]{3,2,1,0:T(8,128)} %get-tuple-element.4) | data formatting | bytes 1310720
  57.8 0.0 copy-done
  57.8 0.8 %copy.11 = f32[2,10,64,128]{3,2,1,0:T(8,128)} copy(f32[2,10,64,128]{3,2,1,0:T(8,128)S(1)} %copy-done) | data formatting | bytes 1310720
Async XLA Ops:
  55.8 2.1 %copy-start = (f32[2,10,64,128]{3,2,1,0:T(8,128)S(1)}, f32[2,10,64,128]{3,2,1,0:T(8,128)}, u32[]{:S(2)}) copy-start(f32[2,10,64,128]{3,2,1,0:T(8,128)} %get-tuple-element.5) | copy-start | bytes 1966084

commit v6 on v5

--- a/solution.py
+++ b/solution.py
@@ -480,10 +480,10 @@
         back_all(back_copy, 0, "start")
         back_all(back_copy, 4, "start")
         tem[:, y, pl.ds(0, 5)] = dt[y, :, pl.ds(0, 5)]
+    with scope("points1"):
+        relay_points(1)
     with scope("ring0_2b"):
         ring_relay(0, 2, 1)
-    with scope("points1"):
-        relay_points(1)
     with scope("first0"):
         first_direction(0)
     with scope("ring0_3"):
@@ -492,10 +492,6 @@
         relay_points(2)
     with scope("ring0_3b"):
         ring_relay(0, 3, 1)
-    with scope("ring0_4"):
-        for t in range(2):
-            ring_relay(0, 4, t)
-            column_start(0, t)
     with scope("back_slide"):
         back_all(back_arrival, 0, "wait_recv")
     with scope("w"):
@@ -504,6 +500,10 @@
                 rest = res_ref[t, v, rows(3), :] + tiles_of(tem, t, v, 3)
                 ring[1][t][z, v] = ub[0, t, v, rows(3), :] - step_size * rest
             ring_start(1, t)
+    with scope("ring0_4"):
+        for t in range(2):
+            ring_relay(0, 4, t)
+            column_start(0, t)
     with scope("cols1_start"):
         for t in range(2):
             column_start(1, t)
@@ -594,6 +594,25 @@
         lax.fori_loop(0, VARS, twice, 0)
     with scope("first1"):
         first_direction(2)
+    with scope("sends_early"):
+        for kind in range(3):
+            out_all(out_copy, kind, "wait_send")
+        for kind in (0, 1, 2, 4, 5):
+            back_all(back_copy, kind, "wait_send")
+        for kind in (1, 2):
+            for k in range(4, 8):
+                pass_on(kind, k, 0).wait_send()
+        for kind in range(2):
+            for hop in range(3):
+                for t in range(2):
+                    column_copy(kind, hop, t).wait_send()
+        for it in range(ITERS):
+            for step in range(1, 5 - it):
+                for t in range(2):
+                    for way, part in ring_chunks(step, t):
+                        ring_copy(it, step, way, t, part).wait_send()
+            for way in range(2):
+                pack_copy(it, way).wait_send()
     with scope("cols2_relay"):
         for t in range(2):
             column_relay(2, t)
@@ -626,24 +645,14 @@
     with scope("finish"):
         lax.fori_loop(0, VARS, finish, 0)
     with scope("sends"):
-        for kind in range(4):
-            out_all(out_copy, kind, "wait_send")
-        for kind in range(7):
+        out_all(out_copy, 3, "wait_send")
+        for kind in (3, 6):
             back_all(back_copy, kind, "wait_send")
-        for kind in (1, 2):
-            for k in range(4, 8):
-                pass_on(kind, k, 0).wait_send()
-        for kind in range(3):
+        for t in range(2):
             for hop in range(3):
-                for t in range(2):
-                    column_copy(kind, hop, t).wait_send()
-        for it in range(ITERS):
-            for step in range(1, 5):
-                for t in range(2):
-                    for way, part in ring_chunks(step, t):
-                        ring_copy(it, step, way, t, part).wait_send()
-            for way in range(2):
-                pack_copy(it, way).wait_send()
+                column_copy(2, hop, t).wait_send()
+            for way, part in ring_chunks(4, t):
+                ring_copy(1, 4, way, t, part).wait_send()
 
 
 def per_device(conserved_field, face_neighbours, counterpart_group, counterpart_shift, volume_operator, flux_matrix):

time: 58.8 us -> 56.8 us (0.966)
  Pallas kernels: 55.1 us -> 53.1 us
    pallas_call x1, Pallas kernels: 55.1 us -> 53.1 us  [per_device(): pl.pallas_call(kernel, out_shape=(state, state), in_specs=[pl.BlockSpec(m...]
where the time goes in v6:
time: 56.8 us; the launch traced here: 56.7 us
  Pallas kernels  53.1 us (93%)
  local copies, waits for them, and re-layouts  2.89 us (5%)
  between operations  0.65 us (1%)
    pallas_call x1, Pallas kernels, per_device(): pl.pallas_call(kernel, out_shape=(state, state), in_specs=[pl.BlockSpec(m...  53.1 us
    unnamed x4, local copies, waits for them, and re-layouts  2.89 us

profile of v6, /device:TPU:1, one launch (start us, length us, event | category | flops | bytes accessed | tf_op | source)
XLA Modules:
  0.0 56.7 jit_solution(2045875163796807600)
XLA Ops:
  0.6 53.1 %iterations.1 = (f32[2,10,64,128]{3,2,1,0:T(8,128)}, f32[2,10,64,128]{3,2,1,0:T(8,128)}) custom-call(f32[2,10,64,128]{3,2,1,0:T(8,128)} %u_hbm.1, s32[2,128]{1,0:T(2,128)} %fn_hbm.1, s32[2]{0:T(128)} %group_hbm.1, s32[2]{0:T(128)} %shift_hbm.1, f32[2,64,64]{2,1,0:T(8,128)} %vol_hbm.1, f32[10,2,10]{2,1,0:T(2,128)} %bitcast.1), custom_call_target="tpu_custom_call" | custom-call | tf_op jit(solution)/shard_map/iterations/pallas_call | solution.py:663
  53.8 0.0 copy-start
  53.8 2.0 %copy.10 = f32[2,10,64,128]{3,2,1,0:T(8,128)} copy(f32[2,10,64,128]{3,2,1,0:T(8,128)} %get-tuple-element.4) | data formatting | bytes 1310720
  55.8 0.0 copy-done
  55.8 0.8 %copy.11 = f32[2,10,64,128]{3,2,1,0:T(8,128)} copy(f32[2,10,64,128]{3,2,1,0:T(8,128)S(1)} %copy-done) | data formatting | bytes 1310720
Async XLA Ops:
  53.8 2.1 %copy-start = (f32[2,10,64,128]{3,2,1,0:T(8,128)S(1)}, f32[2,10,64,128]{3,2,1,0:T(8,128)}, u32[]{:S(2)}) copy-start(f32[2,10,64,128]{3,2,1,0:T(8,128)} %get-tuple-element.5) | copy-start | bytes 1966084

commit v7 on v6

--- a/solution.py
+++ b/solution.py
@@ -125,6 +125,27 @@
     OUT = ((0, 5), (5, 5), (10, 10))
     BACK = ((0, 5), (5, 5), (10, 10), None, (0, 5), (5, 5), (10, 10))
 
+    OUT_SEM = (0, 1, 4, 7)
+
+    def settle(view, send=None, receive=None):
+        copy = pltpu.make_async_remote_copy(
+            src_ref=view, dst_ref=view, send_sem=bs.at[0] if send is None else send,
+            recv_sem=br.at[0] if receive is None else receive, device_id={"tm": (tm + 1) % TM}, device_id_type=MESH)
+        if send is None:
+            copy.wait_recv()
+        else:
+            copy.wait_send()
+
+    def out_view(kind, count):
+        if kind == 3:
+            return sig_gat.at[pl.ds(0, count)]
+        return gat.at[pl.ds(0, count), :, pl.ds(*OUT[kind])]
+
+    def back_view(kind):
+        if kind == 3:
+            return sig_tem.at[:, pl.ds(0, 15)]
+        return (tem2 if kind > 3 else tem).at[:, pl.ds(0, 3), pl.ds(*BACK[kind])]
+
     def peer_at(k, sign):
         dy, dx = MOVES[k]
         row = (y + sign * dy + 4) % 4
@@ -147,41 +168,33 @@
         row, peer = peer_at(k, 1)
         source, target = out_refs(kind, row, tm)
         return pltpu.make_async_remote_copy(
-            src_ref=source, dst_ref=target, send_sem=fs.at[kind, k], recv_sem=fr.at[kind, k],
+            src_ref=source, dst_ref=target, send_sem=fs.at[kind], recv_sem=fr.at[OUT_SEM[kind] + (k - 4 if kind in (1, 2) else 0)],
             device_id={"tm": peer}, device_id_type=MESH)
 
     def out_arrival(kind, k):
         row, peer = peer_at(k, -1)
         source, target = out_refs(kind, row, peer)
         return pltpu.make_async_remote_copy(
-            src_ref=source, dst_ref=target, send_sem=fs.at[kind, k], recv_sem=fr.at[kind, k],
+            src_ref=source, dst_ref=target, send_sem=fs.at[kind], recv_sem=fr.at[OUT_SEM[kind] + (k - 4 if kind in (1, 2) else 0)],
             device_id={"tm": peer}, device_id_type=MESH)
 
     def back_copy(kind, k):
         row, peer = peer_at(k, 1)
         source, target = back_refs(kind, row, y)
         return pltpu.make_async_remote_copy(
-            src_ref=source, dst_ref=target, send_sem=bs.at[kind, k - 4], recv_sem=br.at[kind, k - 4],
+            src_ref=source, dst_ref=target, send_sem=bs.at[kind], recv_sem=br.at[kind],
             device_id={"tm": peer}, device_id_type=MESH)
 
-    def back_arrival(kind, k):
-        row, peer = peer_at(k, -1)
-        source, target = back_refs(kind, row, row)
-        return pltpu.make_async_remote_copy(
-            src_ref=source, dst_ref=target, send_sem=bs.at[kind, k - 4], recv_sem=br.at[kind, k - 4],
-            device_id={"tm": peer}, device_id_type=MESH)
-
-    def out_all(make, kind, method):
+    def out_start(kind):
         for k in range(7) if kind in (0, 3) else range(4, 7):
-            getattr(make(kind, k), method)()
+            out_copy(kind, k).start()
 
     def pass_on(kind, k, side):
         row = (y if k == 7 else peer_at(k, -1)[0])
         place = row * 2 + (side_x if side == 0 else 1 - side_x)
         block = gat.at[place, :, pl.ds(*OUT[kind])]
-        slot = (kind - 1) * 4 + k - 4
-        return pltpu.make_async_remote_copy(
-            src_ref=block, dst_ref=block, send_sem=xs.at[slot], recv_sem=xr.at[slot],
+        return pltpu.make_async_remote_copy(
+            src_ref=block, dst_ref=block, send_sem=xs.at[kind - 1], recv_sem=xr.at[kind - 1],
             device_id={"tm": y * 2 + 1 - side_x}, device_id_type=MESH)
 
     def relay_points(kind):
@@ -190,12 +203,11 @@
             pass_on(kind, k, 0).start()
 
     def wait_points(kind):
-        for k in (7, 5, 6, 4):
-            pass_on(kind, k, 1).wait_recv()
-
-    def back_all(make, kind, method):
+        settle(out_view(kind, 4), receive=xr.at[kind - 1])
+
+    def back_start(kind):
         for k in range(4, 7):
-            getattr(make(kind, k), method)()
+            back_copy(kind, k).start()
 
     def ring_slot(step, way, t, part):
         return (((step - 1) * 2 + way) * 2 + t) * PARTS + part
@@ -208,7 +220,7 @@
         block = ring[it][t].at[origin, pl.ds(part * PIECE, PIECE)]
         slot = ring_slot(step, way, t, part)
         return pltpu.make_async_remote_copy(
-            src_ref=block, dst_ref=block, send_sem=zs.at[it, slot], recv_sem=zr.at[it, slot],
+            src_ref=block, dst_ref=block, send_sem=zs.at[it * 2 + t], recv_sem=zr.at[slot],
             device_id={"space": target}, device_id_type=MESH)
 
     def ring_arrival(it, step, way, t, part):
@@ -219,30 +231,28 @@
         block = ring[it][t].at[origin, pl.ds(part * PIECE, PIECE)]
         slot = ring_slot(step, way, t, part)
         return pltpu.make_async_remote_copy(
-            src_ref=block, dst_ref=block, send_sem=zs.at[it, slot], recv_sem=zr.at[it, slot],
+            src_ref=block, dst_ref=block, send_sem=zs.at[it * 2 + t], recv_sem=zr.at[slot],
             device_id={"space": target}, device_id_type=MESH)
 
     def column_copy(kind, hop, t):
         origin, target = ((q, mate), (q, cross), ((q + 2) % Q, mate))[hop]
         block = cols[kind][t].at[origin]
-        slot = hop * 2 + t
-        return pltpu.make_async_remote_copy(
-            src_ref=block, dst_ref=block, send_sem=cs.at[kind, slot], recv_sem=cr.at[kind, slot],
+        return pltpu.make_async_remote_copy(
+            src_ref=block, dst_ref=block, send_sem=cs.at[kind], recv_sem=cr.at[kind * 4 + (2 if hop == 1 else 0) + t],
             device_id={"space": target}, device_id_type=MESH)
 
     def column_arrival(kind, hop, t):
         mate_q = q + 1 - 2 * (q % 2)
         origin, target = ((mate_q, mate), ((q + 2) % Q, cross), ((mate_q + 2) % Q, mate))[hop]
         block = cols[kind][t].at[origin]
-        slot = hop * 2 + t
-        return pltpu.make_async_remote_copy(
-            src_ref=block, dst_ref=block, send_sem=cs.at[kind, slot], recv_sem=cr.at[kind, slot],
+        return pltpu.make_async_remote_copy(
+            src_ref=block, dst_ref=block, send_sem=cs.at[kind], recv_sem=cr.at[kind * 4 + (2 if hop == 1 else 0) + t],
             device_id={"space": target}, device_id_type=MESH)
 
     def pack_copy(it, way):
         target = (after, before)[way]
         return pltpu.make_async_remote_copy(
-            src_ref=packs.at[it, way], dst_ref=packed.at[it, way], send_sem=ps.at[it, way], recv_sem=pr.at[it, way],
+            src_ref=packs.at[it, way], dst_ref=packed.at[it, way], send_sem=ps.at[it], recv_sem=pr.at[it],
             device_id={"space": target}, device_id_type=MESH)
 
     def build_matrix():
@@ -321,8 +331,7 @@
     loss = jnp.float32(0.5 * lift_scale * dissipation)
 
     def first_direction(it):
-        for way in range(2):
-            pack_copy(it // 2, way).wait_recv()
+        settle(packed.at[it // 2], receive=pr.at[it // 2])
         from_before = packed[it // 2, 0]
         from_after = packed[it // 2, 1]
         behind = lane16 - back_gap
@@ -418,8 +427,7 @@
         column_copy(kind, 2, t).start()
 
     def column_finish(kind, t):
-        column_arrival(kind, 0, t).wait_recv()
-        column_arrival(kind, 2, t).wait_recv()
+        settle(cols[kind][t].at[pl.ds(0, 2)], receive=cr.at[kind * 4 + t])
         group, shift = offset_of(kind, t)
         first = cols[kind][t][jnp.bitwise_and(q + group, Q - 1)]
         second = cols[kind][t][jnp.bitwise_and(q + group + 1, Q - 1)]
@@ -451,7 +459,7 @@
                     j, i = slide_place(v, h)
                     up[t, j, i] = points[8 * h:8 * h + 8]
             ring_start(0, t)
-        out_all(out_copy, 0, "start")
+        out_start(0)
         pack_traces(0)
         for t in range(2):
             for v in range(VARS):
@@ -462,7 +470,7 @@
                         up[t, j, i] = points[8 * h:8 * h + 8]
         gat[tm] = up[:, y]
         for kind in (1, 2):
-            out_all(out_copy, kind, "start")
+            out_start(kind)
             pass_on(kind, 7, 0).start()
     with scope("matrix"):
         build_matrix()
@@ -474,11 +482,11 @@
     with scope("ring0_2a"):
         ring_relay(0, 2, 0)
     with scope("out_slide"):
-        out_all(out_arrival, 0, "wait_recv")
+        settle(out_view(0, 7), receive=fr.at[OUT_SEM[0]])
     with scope("derive_slide"):
         lax.fori_loop(0, 5, derive_state, 0)
-        back_all(back_copy, 0, "start")
-        back_all(back_copy, 4, "start")
+        back_start(0)
+        back_start(4)
         tem[:, y, pl.ds(0, 5)] = dt[y, :, pl.ds(0, 5)]
     with scope("points1"):
         relay_points(1)
@@ -493,7 +501,7 @@
     with scope("ring0_3b"):
         ring_relay(0, 3, 1)
     with scope("back_slide"):
-        back_all(back_arrival, 0, "wait_recv")
+        settle(back_view(0), receive=br.at[0])
     with scope("w"):
         for t in range(2):
             for v in range(VARS):
@@ -510,16 +518,16 @@
     with scope("rest1"):
         wait_points(1)
         lax.fori_loop(5, 10, derive_state, 0)
-        back_all(back_copy, 1, "start")
-        back_all(back_copy, 5, "start")
+        back_start(1)
+        back_start(5)
         tem[:, y, pl.ds(5, 5)] = dt[y, :, pl.ds(5, 5)]
     with scope("ring1_1a"):
         ring_relay(1, 1, 0)
     with scope("rest2"):
         wait_points(2)
         lax.fori_loop(10, 20, derive_state, 0)
-        back_all(back_copy, 2, "start")
-        back_all(back_copy, 6, "start")
+        back_start(2)
+        back_start(6)
         tem[:, y, pl.ds(10, 10)] = dt[y, :, pl.ds(10, 10)]
         tem2[:, y] = dt2[y]
     with scope("ring1_1b"):
@@ -545,7 +553,7 @@
 
     with scope("sigma"):
         lax.fori_loop(0, VARS, sliding_term, 0)
-        out_all(out_copy, 3, "start")
+        out_start(3)
         sig_gat[tm] = sig[:, pl.ds(5 * y, 5)]
     with scope("ring1_3a"):
         ring_relay(1, 3, 0)
@@ -553,8 +561,8 @@
         for t in range(2):
             column_relay(1, t)
     with scope("back_rest"):
-        back_all(back_arrival, 1, "wait_recv")
-        back_all(back_arrival, 2, "wait_recv")
+        settle(back_view(1), receive=br.at[1])
+        settle(back_view(2), receive=br.at[2])
     with scope("u1"):
         for t in range(2):
             for v in range(VARS):
@@ -576,10 +584,10 @@
             ring_relay(1, 4, t)
             column_start(2, t)
     with scope("out_term"):
-        out_all(out_arrival, 3, "wait_recv")
+        settle(out_view(3, 7), receive=fr.at[OUT_SEM[3]])
     with scope("derive_term"):
         lax.fori_loop(0, 5, derive_term, 0)
-        back_all(back_copy, 3, "start")
+        back_start(3)
         sig_tem[:, pl.ds(5 * y, 5)] = sig_dt[y]
     with scope("cols1_finish"):
         for t in range(2):
@@ -595,30 +603,24 @@
     with scope("first1"):
         first_direction(2)
     with scope("sends_early"):
-        for kind in range(3):
-            out_all(out_copy, kind, "wait_send")
+        settle(out_view(0, 7), send=fs.at[0])
+        for kind in (1, 2):
+            settle(out_view(kind, 3), send=fs.at[kind])
+            settle(out_view(kind, 4), send=xs.at[kind - 1])
         for kind in (0, 1, 2, 4, 5):
-            back_all(back_copy, kind, "wait_send")
-        for kind in (1, 2):
-            for k in range(4, 8):
-                pass_on(kind, k, 0).wait_send()
+            settle(back_view(kind), send=bs.at[kind])
         for kind in range(2):
-            for hop in range(3):
-                for t in range(2):
-                    column_copy(kind, hop, t).wait_send()
+            settle(ring[0][0].at[pl.ds(0, 6)], send=cs.at[kind])
+        for t in range(2):
+            settle(ring[0][t].at[pl.ds(0, 7)], send=zs.at[t])
         for it in range(ITERS):
-            for step in range(1, 5 - it):
-                for t in range(2):
-                    for way, part in ring_chunks(step, t):
-                        ring_copy(it, step, way, t, part).wait_send()
-            for way in range(2):
-                pack_copy(it, way).wait_send()
+            settle(packs.at[it], send=ps.at[it])
     with scope("cols2_relay"):
         for t in range(2):
             column_relay(2, t)
     with scope("back_late"):
         for kind in (4, 5, 6, 3):
-            back_all(back_arrival, kind, "wait_recv")
+            settle(back_view(kind), receive=br.at[kind])
     with scope("without_slide"):
         for t in range(2):
             for v in range(VARS):
@@ -645,18 +647,16 @@
     with scope("finish"):
         lax.fori_loop(0, VARS, finish, 0)
     with scope("sends"):
-        out_all(out_copy, 3, "wait_send")
+        settle(out_view(3, 7), send=fs.at[3])
         for kind in (3, 6):
-            back_all(back_copy, kind, "wait_send")
-        for t in range(2):
-            for hop in range(3):
-                column_copy(2, hop, t).wait_send()
-            for way, part in ring_chunks(4, t):
-                ring_copy(1, 4, way, t, part).wait_send()
+            settle(back_view(kind), send=bs.at[kind])
+        settle(ring[0][0].at[pl.ds(0, 6)], send=cs.at[2])
+        for t in range(2):
+            settle(ring[1][t].at[pl.ds(0, 7)], send=zs.at[2 + t])
 
 
 def per_device(conserved_field, face_neighbours, counterpart_group, counterpart_shift, volume_operator, flux_matrix):
-    state = jax.ShapeDtypeStruct(conserved_field.shape, jnp.float32)
+    state = pltpu.VMEM(conserved_field.shape, jnp.float32)
     vmem = pl.BlockSpec(memory_space=pltpu.VMEM)
     f32, bf16 = jnp.float32, jnp.bfloat16
     dma = pltpu.SemaphoreType.DMA
@@ -694,15 +694,15 @@
             pltpu.VMEM((2, VARS, 16, LANES), f32),
             pltpu.VMEM((2, VARS, 16, LANES), f32),
             dma((6,)),
-            dma((4, 7)), dma((4, 7)),
-            dma((7, 3)), dma((7, 3)),
-            dma((ITERS, 16 * PARTS)), dma((ITERS, 16 * PARTS)),
-            dma((3, 6)), dma((3, 6)),
-            dma((ITERS, 2)), dma((ITERS, 2)),
-            dma((8,)), dma((8,)),
+            dma((4,)), dma((8,)),
+            dma((7,)), dma((7,)),
+            dma((4,)), dma((16 * PARTS,)),
+            dma((3,)), dma((12,)),
+            dma((2,)), dma((2,)),
+            dma((2,)), dma((2,)),
         ],
         compiler_params=pltpu.CompilerParams(
-            collective_id=0, has_side_effects=True, vmem_limit_bytes=63 * 1024 * 1024),
+            collective_id=0, has_side_effects=True, vmem_limit_bytes=60 * 1024 * 1024),
         name="iterations",
     )(conserved_field, face_neighbours, counterpart_group, counterpart_shift, volume_operator,
       jnp.transpose(flux_matrix, (1, 0, 2)))

time: 56.8 us -> 51.3 us (0.903)
  Pallas kernels: 53.1 us -> 48.9 us
  local copies, waits for them, and re-layouts: 2.89 us -> 1.67 us
    pallas_call x1, Pallas kernels: 53.1 us -> 48.9 us  [per_device(): pl.pallas_call(kernel, out_shape=(state, state), in_specs=[pl.BlockSpec(m...]
    unnamed x4 -> x2, local copies, waits for them, and re-layouts: 2.89 us -> 1.67 us
where the time goes in v7:
time: 51.3 us; the launch traced here: 51.2 us
  Pallas kernels  48.9 us (95%)
  local copies, waits for them, and re-layouts  1.67 us (3%)
  between operations  0.64 us (1%)
    pallas_call x1, Pallas kernels, per_device(): pl.pallas_call(kernel, out_shape=(state, state), in_specs=[pl.BlockSpec(m...  48.9 us
    unnamed x2, local copies, waits for them, and re-layouts  1.67 us

profile of v7, /device:TPU:1, one launch (start us, length us, event | category | flops | bytes accessed | tf_op | source)
XLA Modules:
  0.0 51.2 jit_solution(2981493505388448283)
XLA Ops:
  0.6 48.9 %iterations.1 = (f32[2,10,64,128]{3,2,1,0:T(8,128)S(1)}, f32[2,10,64,128]{3,2,1,0:T(8,128)S(1)}) custom-call(f32[2,10,64,128]{3,2,1,0:T(8,128)} %u_hbm.1, s32[2,128]{1,0:T(2,128)} %fn_hbm.1, s32[2]{0:T(128)} %group_hbm.1, s32[2]{0:T(128)} %shift_hbm.1, f32[2,64,64]{2,1,0:T(8,128)} %vol_hbm.1, f32[10,2,10]{2,1,0:T(2,128)} %bitcast.1), custom_call_target="tpu_custom_call" | custom-call | tf_op jit(solution)/shard_map/iterations/pallas_call | solution.py:663
  49.6 0.8 %copy.10 = f32[2,10,64,128]{3,2,1,0:T(8,128)} copy(f32[2,10,64,128]{3,2,1,0:T(8,128)S(1)} %get-tuple-element.2) | data formatting | bytes 1310720
  50.4 0.8 %copy.11 = f32[2,10,64,128]{3,2,1,0:T(8,128)} copy(f32[2,10,64,128]{3,2,1,0:T(8,128)S(1)} %get-tuple-element.3) | data formatting | bytes 1310720

commit v8 on v7

--- a/solution.py
+++ b/solution.py
@@ -96,7 +96,8 @@
     loads = [
         pltpu.make_async_copy(source, target, in_sem.at[k])
         for k, (source, target) in enumerate((
-            (u_hbm, ub.at[0]), (flux_hbm, flux_ref), (vol_hbm, vol_ref),
+            *((u_hbm.at[t, pl.ds(5 * h, 5)], ub.at[0, t, pl.ds(5 * h, 5)]) for t in range(2) for h in range(2)),
+            (flux_hbm, flux_ref), (vol_hbm, vol_ref),
             (fn_hbm, fn_ref), (group_hbm, group_ref), (shift_hbm, shift_ref)))
     ]
     for load in loads:
@@ -108,14 +109,11 @@
     for other in (z_up, z_dn, mate, cross, after, before):
         pl.semaphore_signal(barrier, inc=1, device_id={"space": other}, device_id_type=MESH)
     with jax.named_scope("entry"):
-        for load in loads:
+        for load in loads[:4]:
             load.wait()
         pl.semaphore_wait(barrier, TM - 1 + 6)
 
     lane16 = lax.broadcasted_iota(jnp.int32, (16, LANES), 1)
-    gidx = sp * LANES + lane16
-    back_gap = jnp.bitwise_and(gidx - fn_ref[0:1, :], SP * LANES - 1)
-    ahead_gap = jnp.bitwise_and(fn_ref[1:2, :] - gidx, SP * LANES - 1)
 
     weights = spectral_weights()
     squares = spectral_squares()
@@ -197,8 +195,8 @@
             src_ref=block, dst_ref=block, send_sem=xs.at[kind - 1], recv_sem=xr.at[kind - 1],
             device_id={"tm": y * 2 + 1 - side_x}, device_id_type=MESH)
 
-    def relay_points(kind):
-        for k in (5, 6, 4):
+    def relay_points(kind, moves):
+        for k in moves:
             out_arrival(kind, k).wait_recv()
             pass_on(kind, k, 0).start()
 
@@ -210,7 +208,7 @@
             back_copy(kind, k).start()
 
     def ring_slot(step, way, t, part):
-        return (((step - 1) * 2 + way) * 2 + t) * PARTS + part
+        return 12 * PARTS + t if step == 4 else (((step - 1) * 2 + way) * 2 + t) * PARTS + part
 
     def ring_copy(it, step, way, t, part):
         if way == 0:
@@ -237,16 +235,9 @@
     def column_copy(kind, hop, t):
         origin, target = ((q, mate), (q, cross), ((q + 2) % Q, mate))[hop]
         block = cols[kind][t].at[origin]
+        place = kind * 4 + t + (2 if hop == 1 else 0)
         return pltpu.make_async_remote_copy(
-            src_ref=block, dst_ref=block, send_sem=cs.at[kind], recv_sem=cr.at[kind * 4 + (2 if hop == 1 else 0) + t],
-            device_id={"space": target}, device_id_type=MESH)
-
-    def column_arrival(kind, hop, t):
-        mate_q = q + 1 - 2 * (q % 2)
-        origin, target = ((mate_q, mate), ((q + 2) % Q, cross), ((mate_q + 2) % Q, mate))[hop]
-        block = cols[kind][t].at[origin]
-        return pltpu.make_async_remote_copy(
-            src_ref=block, dst_ref=block, send_sem=cs.at[kind], recv_sem=cr.at[kind * 4 + (2 if hop == 1 else 0) + t],
+            src_ref=block, dst_ref=block, send_sem=cs.at[kind], recv_sem=cr.at[place],
             device_id={"space": target}, device_id_type=MESH)
 
     def pack_copy(it, way):
@@ -307,7 +298,10 @@
             ring_copy(it, 1, way, t, part).start()
 
     def ring_relay(it, step, t):
-        onward = ring_chunks(step + 1, t) if step < 4 else []
+        if step == 4:
+            settle(ring[it][t].at[0], receive=zr.at[ring_slot(4, t, t, 0)])
+            return
+        onward = ring_chunks(step + 1, t)
         for way, part in ring_chunks(step, t):
             ring_arrival(it, step, way, t, part).wait_recv()
             if (way, part) in onward:
@@ -332,6 +326,9 @@
 
     def first_direction(it):
         settle(packed.at[it // 2], receive=pr.at[it // 2])
+        gidx = sp * LANES + lane16
+        back_gap = jnp.bitwise_and(gidx - fn_ref[0:1, :], SP * LANES - 1)
+        ahead_gap = jnp.bitwise_and(fn_ref[1:2, :] - gidx, SP * LANES - 1)
         from_before = packed[it // 2, 0]
         from_after = packed[it // 2, 1]
         behind = lane16 - back_gap
@@ -423,7 +420,7 @@
         column_copy(kind, 0, t).start()
 
     def column_relay(kind, t):
-        column_arrival(kind, 1, t).wait_recv()
+        settle(cols[kind][t].at[0], receive=cr.at[kind * 4 + 2 + t])
         column_copy(kind, 2, t).start()
 
     def column_finish(kind, t):
@@ -473,6 +470,8 @@
             out_start(kind)
             pass_on(kind, 7, 0).start()
     with scope("matrix"):
+        for load in loads[4:]:
+            load.wait()
         build_matrix()
     with scope("volume0"):
         volume_part(0)
@@ -489,7 +488,7 @@
         back_start(4)
         tem[:, y, pl.ds(0, 5)] = dt[y, :, pl.ds(0, 5)]
     with scope("points1"):
-        relay_points(1)
+        relay_points(1, (5, 6, 4))
     with scope("ring0_2b"):
         ring_relay(0, 2, 1)
     with scope("first0"):
@@ -497,7 +496,7 @@
     with scope("ring0_3"):
         ring_relay(0, 3, 0)
     with scope("points2"):
-        relay_points(2)
+        relay_points(2, (5, 6, 4))
     with scope("ring0_3b"):
         ring_relay(0, 3, 1)
     with scope("back_slide"):
@@ -603,6 +602,7 @@
     with scope("first1"):
         first_direction(2)
     with scope("sends_early"):
+        new_ref[...] = ub[1]
         settle(out_view(0, 7), send=fs.at[0])
         for kind in (1, 2):
             settle(out_view(kind, 3), send=fs.at[kind])
@@ -618,10 +618,21 @@
     with scope("cols2_relay"):
         for t in range(2):
             column_relay(2, t)
+    for t in range(2):
+        with scope("cols2_finish%d" % t):
+            sl_b[t] = column_finish(2, t) - tw_b[t]
+            turn(t)
+
+        def slide_part(v, c, t=t):
+            res_ref[t, v, rows(3), :] += slide_term(t, v)
+            return c
+
+        with scope("slide_part%d" % t):
+            lax.fori_loop(0, VARS, slide_part, 0)
     with scope("back_late"):
         for kind in (4, 5, 6, 3):
             settle(back_view(kind), receive=br.at[kind])
-    with scope("without_slide"):
+    with scope("finish"):
         for t in range(2):
             for v in range(VARS):
                 for c in range(4):
@@ -629,23 +640,7 @@
                     if c == 3:
                         late = late + term_tiles(t, v)
                     total = res_ref[t, v, rows(c), :] + (tiles_of(tem, t, v, c) - step_size * late)
-                    res_ref[t, v, rows(c), :] = total
-                    if c < 3:
-                        new_ref[t, v, rows(c), :] = ub[1, t, v, rows(c), :] - step_size * total
-    with scope("cols2_finish"):
-        for t in range(2):
-            sl_b[t] = column_finish(2, t) - tw_b[t]
-            turn(t)
-
-    def finish(v, c):
-        for t in range(2):
-            total = res_ref[t, v, rows(3), :] + slide_term(t, v)
-            res_ref[t, v, rows(3), :] = total
-            new_ref[t, v, rows(3), :] = ub[1, t, v, rows(3), :] - step_size * total
-        return c
-
-    with scope("finish"):
-        lax.fori_loop(0, VARS, finish, 0)
+                    res_ref[t, v, rows(c), :] = jnp.float32(0.5) * total
     with scope("sends"):
         settle(out_view(3, 7), send=fs.at[3])
         for kind in (3, 6):
@@ -660,7 +655,7 @@
     vmem = pl.BlockSpec(memory_space=pltpu.VMEM)
     f32, bf16 = jnp.float32, jnp.bfloat16
     dma = pltpu.SemaphoreType.DMA
-    return pl.pallas_call(
+    before, half = pl.pallas_call(
         kernel,
         out_shape=(state, state),
         in_specs=[pl.BlockSpec(memory_space=pltpu.HBM)] * 6,
@@ -693,10 +688,10 @@
             pltpu.VMEM((2, VARS, 16, LANES), f32),
             pltpu.VMEM((2, VARS, 16, LANES), f32),
             pltpu.VMEM((2, VARS, 16, LANES), f32),
-            dma((6,)),
+            dma((9,)),
             dma((4,)), dma((8,)),
             dma((7,)), dma((7,)),
-            dma((4,)), dma((16 * PARTS,)),
+            dma((4,)), dma((12 * PARTS + 2,)),
             dma((3,)), dma((12,)),
             dma((2,)), dma((2,)),
             dma((2,)), dma((2,)),
@@ -706,6 +701,7 @@
         name="iterations",
     )(conserved_field, face_neighbours, counterpart_group, counterpart_shift, volume_operator,
       jnp.transpose(flux_matrix, (1, 0, 2)))
+    return before - jnp.float32(2.0 * pseudo_step) * half, half + half
 
 
 def solution(mesh):

time: 51.3 us -> 50.8 us (level)
  local copies, waits for them, and re-layouts: 1.67 us -> 0 us
  other arithmetic: 0 us -> 1.23 us
    unnamed x2 -> x0, local copies, waits for them, and re-layouts: 1.67 us -> none
    sub x0 -> x1, other arithmetic: none -> 1.23 us  [per_device(): return (before - jnp.float32(2.0 * pseudo_step) * half, half + half)]
where the time goes in v8:
time: 50.8 us; the launch traced here: 50.7 us
  Pallas kernels  48.9 us (96%)
  other arithmetic  1.23 us (2%)
  between operations  0.64 us (1%)
    pallas_call x1, Pallas kernels, per_device(): pl.pallas_call(kernel, out_shape=(state, state), in_specs=[pl.BlockSpec(m...  48.9 us
    sub x1, other arithmetic, per_device(): return (before - jnp.float32(2.0 * pseudo_step) * half, half + half)  1.23 us

profile of v8, /device:TPU:1, one launch (start us, length us, event | category | flops | bytes accessed | tf_op | source)
XLA Modules:
  0.0 50.7 jit_solution(192611845744890818)
XLA Ops:
  0.6 48.9 %iterations.1 = (f32[2,10,64,128]{3,2,1,0:T(8,128)S(1)}, f32[2,10,64,128]{3,2,1,0:T(8,128)S(1)}) custom-call(f32[2,10,64,128]{3,2,1,0:T(8,128)} %u_hbm.1, s32[2,128]{1,0:T(2,128)} %fn_hbm.1, s32[2]{0:T(128)} %group_hbm.1, s32[2]{0:T(128)} %shift_hbm.1, f32[2,64,64]{2,1,0:T(8,128)} %vol_hbm.1, f32[10,2,10]{2,1,0:T(2,128)} %bitcast.1), custom_call_target="tpu_custom_call" | custom-call | tf_op jit(solution)/shard_map/iterations/pallas_call | solution.py:658
  49.5 1.2 %multiply_subtract_fusion = (f32[2,10,64,128]{3,2,1,0:T(8,128)}, f32[2,10,64,128]{3,2,1,0:T(8,128)}) fusion(f32[2,10,64,128]{3,2,1,0:T(8,128)S(1)} %get-tuple-element.4, f32[2,10,64,128]{3,2,1,0:T(8,128)S(1)} %get-tuple-element.5), kind=kLoop, calls=%fused_computation | loop fusion | flops 491520 | bytes 2621440 | tf_op jit(solution)/shard_map/sub | solution.py:704

commit v9 on v8

--- a/solution.py
+++ b/solution.py
@@ -15,6 +15,7 @@
 LANES = 128
 PARTS = 5
 PIECE = VARS // PARTS
+GROUPS = (6, 4)
 
 lift_scale = 2.0
 dissipation = 1.5
@@ -71,10 +72,10 @@
 def kernel(
     u_hbm, fn_hbm, group_hbm, shift_hbm, vol_hbm, flux_hbm,
     new_ref, res_ref, fn_ref, group_ref, shift_ref, vol_ref, flux_ref,
-    ub, a_hi, a_lo, up, gat, dt, dt2, tem, tem2, sig, sig_gat, sig_dt, sig_tem, ring_00, ring_01, ring_10, ring_11, cols_00, cols_01, cols_10, cols_11, cols_20, cols_21,
+    ub, a_hi, a_lo, up, gat, dt, dt2, tem, tem2, sig, sig_gat, sig_dt, sig_tem, ring_000, ring_001, ring_010, ring_011, ring_100, ring_101, ring_110, ring_111, cols_00, cols_01, cols_10, cols_11, cols_20, cols_21,
     packs, packed, side, lo_b, up_b, sl_b, tw_b, in_sem, fs, fr, bs, br, zs, zr, cs, cr, ps, pr, xs, xr,
 ):
-    ring = ((ring_00, ring_01), (ring_10, ring_11))
+    ring = (((ring_000, ring_001), (ring_010, ring_011)), ((ring_100, ring_101), (ring_110, ring_111)))
     cols = ((cols_00, cols_01), (cols_10, cols_11), (cols_20, cols_21))
     tm = lax.axis_index("tm")
     sp = lax.axis_index("space")
@@ -208,14 +209,27 @@
             back_copy(kind, k).start()
 
     def ring_slot(step, way, t, part):
-        return 12 * PARTS + t if step == 4 else (((step - 1) * 2 + way) * 2 + t) * PARTS + part
+        if step == 4:
+            return 12 * PARTS + 2 * t + group_of(part)
+        return (((step - 1) * 2 + way) * 2 + t) * PARTS + part
+
+    def group_of(part):
+        return int(part * PIECE >= GROUPS[0])
+
+    def ring_block(it, t, origin, part):
+        group = group_of(part)
+        return ring[it][t][group].at[origin, pl.ds(part * PIECE - group * GROUPS[0], PIECE)]
+
+    def ring_own(it, t, v, points):
+        group = int(v >= GROUPS[0])
+        ring[it][t][group][z, v - group * GROUPS[0]] = points
 
     def ring_copy(it, step, way, t, part):
         if way == 0:
             origin, target = (z + Z - (step - 1)) % Z, z_up
         else:
             origin, target = (z + step - 1) % Z, z_dn
-        block = ring[it][t].at[origin, pl.ds(part * PIECE, PIECE)]
+        block = ring_block(it, t, origin, part)
         slot = ring_slot(step, way, t, part)
         return pltpu.make_async_remote_copy(
             src_ref=block, dst_ref=block, send_sem=zs.at[it * 2 + t], recv_sem=zr.at[slot],
@@ -226,16 +240,19 @@
             origin, target = (z + Z - step) % Z, z_up
         else:
             origin, target = (z + step) % Z, z_dn
-        block = ring[it][t].at[origin, pl.ds(part * PIECE, PIECE)]
+        block = ring_block(it, t, origin, part)
         slot = ring_slot(step, way, t, part)
         return pltpu.make_async_remote_copy(
             src_ref=block, dst_ref=block, send_sem=zs.at[it * 2 + t], recv_sem=zr.at[slot],
             device_id={"space": target}, device_id_type=MESH)
 
-    def column_copy(kind, hop, t):
+    def members(group):
+        return pl.ds(group * GROUPS[0], GROUPS[group])
+
+    def column_copy(kind, hop, t, group):
         origin, target = ((q, mate), (q, cross), ((q + 2) % Q, mate))[hop]
-        block = cols[kind][t].at[origin]
-        place = kind * 4 + t + (2 if hop == 1 else 0)
+        block = cols[kind][t].at[origin, members(group)]
+        place = kind * 6 + (2 + 2 * t + group if hop == 1 else t)
         return pltpu.make_async_remote_copy(
             src_ref=block, dst_ref=block, send_sem=cs.at[kind], recv_sem=cr.at[place],
             device_id={"space": target}, device_id_type=MESH)
@@ -298,14 +315,14 @@
             ring_copy(it, 1, way, t, part).start()
 
     def ring_relay(it, step, t):
-        if step == 4:
-            settle(ring[it][t].at[0], receive=zr.at[ring_slot(4, t, t, 0)])
-            return
         onward = ring_chunks(step + 1, t)
         for way, part in ring_chunks(step, t):
             ring_arrival(it, step, way, t, part).wait_recv()
             if (way, part) in onward:
                 ring_copy(it, step + 1, way, t, part).start()
+
+    def ring_last(it, t, group):
+        settle(ring[it][t][group].at[0], receive=zr.at[12 * PARTS + 2 * t + group])
 
     def pack_traces(it):
         up_pack = jnp.zeros((16, LANES), jnp.float32)
@@ -408,23 +425,26 @@
 
     lane_b = lax.broadcasted_iota(jnp.int32, (VARS, 16, LANES), 2)
 
-    def column_start(kind, t):
+    def column_start(kind, t, group):
         it = kind // 2
-        group, shift = offset_of(kind, t)
-        first_dst = jnp.bitwise_and(q - group, Q - 1)
-        second_dst = jnp.bitwise_and(q - group - 1, Q - 1)
-        first = jnp.bitwise_and(z + lax.shift_right_arithmetic(first_dst + group - q, 2), Z - 1)
-        second = jnp.bitwise_and(z + lax.shift_right_arithmetic(second_dst + group + 1 - q, 2), Z - 1)
-        cols[kind][t][q] = jnp.where(lane_b >= shift, ring[it][t][first], ring[it][t][second])
-        column_copy(kind, 1, t).start()
-        column_copy(kind, 0, t).start()
+        block, shift = offset_of(kind, t)
+        first_dst = jnp.bitwise_and(q - block, Q - 1)
+        second_dst = jnp.bitwise_and(q - block - 1, Q - 1)
+        first = jnp.bitwise_and(z + lax.shift_right_arithmetic(first_dst + block - q, 2), Z - 1)
+        second = jnp.bitwise_and(z + lax.shift_right_arithmetic(second_dst + block + 1 - q, 2), Z - 1)
+        source = ring[it][t][group]
+        lanes = lax.broadcasted_iota(jnp.int32, (GROUPS[group], 16, LANES), 2)
+        cols[kind][t][q, members(group)] = jnp.where(lanes >= shift, source[first], source[second])
+        column_copy(kind, 1, t, group).start()
+        column_copy(kind, 0, t, group).start()
 
     def column_relay(kind, t):
-        settle(cols[kind][t].at[0], receive=cr.at[kind * 4 + 2 + t])
-        column_copy(kind, 2, t).start()
+        for group in range(2):
+            settle(cols[kind][t].at[0, members(group)], receive=cr.at[kind * 6 + 2 + 2 * t + group])
+            column_copy(kind, 2, t, group).start()
 
     def column_finish(kind, t):
-        settle(cols[kind][t].at[pl.ds(0, 2)], receive=cr.at[kind * 4 + t])
+        settle(cols[kind][t].at[pl.ds(0, 2)], receive=cr.at[kind * 6 + t])
         group, shift = offset_of(kind, t)
         first = cols[kind][t][jnp.bitwise_and(q + group, Q - 1)]
         second = cols[kind][t][jnp.bitwise_and(q + group + 1, Q - 1)]
@@ -451,7 +471,7 @@
         for t in range(2):
             for v in range(VARS):
                 points = ub[0, t, v, rows(3), :]
-                ring[0][t][z, v] = points
+                ring_own(0, t, v, points)
                 for h in range(2):
                     j, i = slide_place(v, h)
                     up[t, j, i] = points[8 * h:8 * h + 8]
@@ -505,15 +525,17 @@
         for t in range(2):
             for v in range(VARS):
                 rest = res_ref[t, v, rows(3), :] + tiles_of(tem, t, v, 3)
-                ring[1][t][z, v] = ub[0, t, v, rows(3), :] - step_size * rest
+                ring_own(1, t, v, ub[0, t, v, rows(3), :] - step_size * rest)
             ring_start(1, t)
     with scope("ring0_4"):
         for t in range(2):
-            ring_relay(0, 4, t)
-            column_start(0, t)
+            for group in range(2):
+                ring_last(0, t, group)
+                column_start(0, t, group)
     with scope("cols1_start"):
         for t in range(2):
-            column_start(1, t)
+            for group in range(2):
+                column_start(1, t, group)
     with scope("rest1"):
         wait_points(1)
         lax.fori_loop(5, 10, derive_state, 0)
@@ -580,8 +602,9 @@
         volume_part(2)
     with scope("ring1_4"):
         for t in range(2):
-            ring_relay(1, 4, t)
-            column_start(2, t)
+            for group in range(2):
+                ring_last(1, t, group)
+                column_start(2, t, group)
     with scope("out_term"):
         settle(out_view(3, 7), receive=fr.at[OUT_SEM[3]])
     with scope("derive_term"):
@@ -610,9 +633,9 @@
         for kind in (0, 1, 2, 4, 5):
             settle(back_view(kind), send=bs.at[kind])
         for kind in range(2):
-            settle(ring[0][0].at[pl.ds(0, 6)], send=cs.at[kind])
-        for t in range(2):
-            settle(ring[0][t].at[pl.ds(0, 7)], send=zs.at[t])
+            settle(gat.at[pl.ds(0, 6), 0], send=cs.at[kind])
+        for t in range(2):
+            settle(gat.at[pl.ds(0, 7), 0], send=zs.at[t])
         for it in range(ITERS):
             settle(packs.at[it], send=ps.at[it])
     with scope("cols2_relay"):
@@ -645,9 +668,9 @@
         settle(out_view(3, 7), send=fs.at[3])
         for kind in (3, 6):
             settle(back_view(kind), send=bs.at[kind])
-        settle(ring[0][0].at[pl.ds(0, 6)], send=cs.at[2])
-        for t in range(2):
-            settle(ring[1][t].at[pl.ds(0, 7)], send=zs.at[2 + t])
+        settle(gat.at[pl.ds(0, 6), 0], send=cs.at[2])
+        for t in range(2):
+            settle(gat.at[pl.ds(0, 7), 0], send=zs.at[2 + t])
 
 
 def per_device(conserved_field, face_neighbours, counterpart_group, counterpart_shift, volume_operator, flux_matrix):
@@ -679,7 +702,7 @@
             pltpu.VMEM((TM, 2, 5, 8, LANES), f32),
             pltpu.VMEM((4, 2, 5, 8, LANES), f32),
             pltpu.VMEM((2, 20, 8, LANES), f32),
-            *[pltpu.VMEM((Z, VARS, 16, LANES), f32)] * 4,
+            *[pltpu.VMEM((Z, count, 16, LANES), f32) for count in GROUPS] * 4,
             *[pltpu.VMEM((Q, VARS, 16, LANES), f32)] * 6,
             pltpu.VMEM((ITERS, 2, 16, LANES), f32),
             pltpu.VMEM((ITERS, 2, 16, LANES), f32),
@@ -691,8 +714,8 @@
             dma((9,)),
             dma((4,)), dma((8,)),
             dma((7,)), dma((7,)),
-            dma((4,)), dma((12 * PARTS + 2,)),
-            dma((3,)), dma((12,)),
+            dma((4,)), dma((12 * PARTS + 4,)),
+            dma((3,)), dma((18,)),
             dma((2,)), dma((2,)),
             dma((2,)), dma((2,)),
         ],

time: 50.8 us -> 50.2 us (0.988)
  Pallas kernels: 48.9 us -> 48.2 us
    pallas_call x1, Pallas kernels: 48.9 us -> 48.2 us  [per_device(): pl.pallas_call(kernel, out_shape=(state, state), in_specs=[pl.BlockSpec(m...]
where the time goes in v9:
time: 50.2 us; the launch traced here: 50.1 us
  Pallas kernels  48.2 us (96%)
  other arithmetic  1.23 us (2%)
  between operations  0.64 us (1%)
    pallas_call x1, Pallas kernels, per_device(): pl.pallas_call(kernel, out_shape=(state, state), in_specs=[pl.BlockSpec(m...  48.2 us
    sub x1, other arithmetic, per_device(): return (before - jnp.float32(2.0 * pseudo_step) * half, half + half)  1.23 us

profile of v9, /device:TPU:1, one launch (start us, length us, event | category | flops | bytes accessed | tf_op | source)
XLA Modules:
  0.0 50.1 jit_solution(10514285737765285596)
XLA Ops:
  0.6 48.2 %iterations.1 = (f32[2,10,64,128]{3,2,1,0:T(8,128)S(1)}, f32[2,10,64,128]{3,2,1,0:T(8,128)S(1)}) custom-call(f32[2,10,64,128]{3,2,1,0:T(8,128)} %u_hbm.1, s32[2,128]{1,0:T(2,128)} %fn_hbm.1, s32[2]{0:T(128)} %group_hbm.1, s32[2]{0:T(128)} %shift_hbm.1, f32[2,64,64]{2,1,0:T(8,128)} %vol_hbm.1, f32[10,2,10]{2,1,0:T(2,128)} %bitcast.1), custom_call_target="tpu_custom_call" | custom-call | tf_op jit(solution)/shard_map/iterations/pallas_call | solution.py:681
  48.8 1.2 %multiply_subtract_fusion = (f32[2,10,64,128]{3,2,1,0:T(8,128)}, f32[2,10,64,128]{3,2,1,0:T(8,128)}) fusion(f32[2,10,64,128]{3,2,1,0:T(8,128)S(1)} %get-tuple-element.4, f32[2,10,64,128]{3,2,1,0:T(8,128)S(1)} %get-tuple-element.5), kind=kLoop, calls=%fused_computation | loop fusion | flops 491520 | bytes 2621440 | tf_op jit(solution)/shard_map/sub | solution.py:727

commit v10 on v9

--- a/solution.py
+++ b/solution.py
@@ -625,7 +625,6 @@
     with scope("first1"):
         first_direction(2)
     with scope("sends_early"):
-        new_ref[...] = ub[1]
         settle(out_view(0, 7), send=fs.at[0])
         for kind in (1, 2):
             settle(out_view(kind, 3), send=fs.at[kind])
@@ -663,7 +662,8 @@
                     if c == 3:
                         late = late + term_tiles(t, v)
                     total = res_ref[t, v, rows(c), :] + (tiles_of(tem, t, v, c) - step_size * late)
-                    res_ref[t, v, rows(c), :] = jnp.float32(0.5) * total
+                    res_ref[t, v, rows(c), :] = total
+                    new_ref[t, v, rows(c), :] = ub[1, t, v, rows(c), :] - step_size * total
     with scope("sends"):
         settle(out_view(3, 7), send=fs.at[3])
         for kind in (3, 6):
@@ -673,12 +673,23 @@
             settle(gat.at[pl.ds(0, 7), 0], send=zs.at[2 + t])
 
 
+def write_out(new_ref, res_ref, new_hbm, res_hbm, sem):
+    copies = [
+        pltpu.make_async_copy(source, target, sem.at[k])
+        for k, (source, target) in enumerate(((new_ref, new_hbm), (res_ref, res_hbm)))
+    ]
+    for copy in copies:
+        copy.start()
+    for copy in copies:
+        copy.wait()
+
+
 def per_device(conserved_field, face_neighbours, counterpart_group, counterpart_shift, volume_operator, flux_matrix):
     state = pltpu.VMEM(conserved_field.shape, jnp.float32)
     vmem = pl.BlockSpec(memory_space=pltpu.VMEM)
     f32, bf16 = jnp.float32, jnp.bfloat16
     dma = pltpu.SemaphoreType.DMA
-    before, half = pl.pallas_call(
+    after, residual = pl.pallas_call(
         kernel,
         out_shape=(state, state),
         in_specs=[pl.BlockSpec(memory_space=pltpu.HBM)] * 6,
@@ -724,7 +735,15 @@
         name="iterations",
     )(conserved_field, face_neighbours, counterpart_group, counterpart_shift, volume_operator,
       jnp.transpose(flux_matrix, (1, 0, 2)))
-    return before - jnp.float32(2.0 * pseudo_step) * half, half + half
+    shape = jax.ShapeDtypeStruct(conserved_field.shape, f32)
+    return pl.pallas_call(
+        write_out,
+        out_shape=(shape, shape),
+        in_specs=(vmem, vmem),
+        out_specs=(pl.BlockSpec(memory_space=pltpu.HBM),) * 2,
+        scratch_shapes=[dma((2,))],
+        name="write_out",
+    )(pltpu.with_memory_space_constraint(after, pltpu.VMEM), pltpu.with_memory_space_constraint(residual, pltpu.VMEM))
 
 
 def solution(mesh):

time: 50.2 us -> 50.1 us (level)
  other arithmetic: 1.23 us -> 0 us
  Pallas kernels: 48.2 us -> 49.3 us
    sub x1 -> x0, other arithmetic: 1.23 us -> none  [per_device(): return (before - jnp.float32(2.0 * pseudo_step) * half, half + half)]
    pallas_call x0 -> x1, Pallas kernels: none -> 1.07 us  [per_device(): pl.pallas_call(write_out, out_shape=(shape, shape), in_specs=(vmem, vmem)...]
where the time goes in v10:
time: 50.1 us; the launch traced here: 50 us
  Pallas kernels  49.3 us (98%)
  between operations  0.64 us (1%)
    pallas_call x1, Pallas kernels, per_device(): pl.pallas_call(kernel, out_shape=(state, state), in_specs=[pl.BlockSpec(m...  48.3 us
    pallas_call x1, Pallas kernels, per_device(): pl.pallas_call(write_out, out_shape=(shape, shape), in_specs=(vmem, vmem)...  1.07 us

profile of v10, /device:TPU:1, one launch (start us, length us, event | category | flops | bytes accessed | tf_op | source)
XLA Modules:
  0.0 50.0 jit_solution(10168592150266184438)
XLA Ops:
  0.6 48.3 %iterations.1 = (f32[2,10,64,128]{3,2,1,0:T(8,128)S(1)}, f32[2,10,64,128]{3,2,1,0:T(8,128)S(1)}) custom-call(f32[2,10,64,128]{3,2,1,0:T(8,128)} %u_hbm.1, s32[2,128]{1,0:T(2,128)} %fn_hbm.1, s32[2]{0:T(128)} %group_hbm.1, s32[2]{0:T(128)} %shift_hbm.1, f32[2,64,64]{2,1,0:T(8,128)} %vol_hbm.1, f32[10,2,10]{2,1,0:T(2,128)} %bitcast.1), custom_call_target="tpu_custom_call" | custom-call | tf_op jit(solution)/shard_map/iterations/pallas_call | solution.py:692
  48.9 1.1 %write_out.1 = (f32[2,10,64,128]{3,2,1,0:T(8,128)}, f32[2,10,64,128]{3,2,1,0:T(8,128)}) custom-call(f32[2,10,64,128]{3,2,1,0:T(8,128)S(1)} %get-tuple-element.4.new_ref, f32[2,10,64,128]{3,2,1,0:T(8,128)S(1)} %get-tuple-element.5.res_ref), custom_call_target="tpu_custom_call" | custom-call | tf_op jit(solution)/shard_map/write_out/pallas_call | solution.py:739
